TPU v7x, 32 devices: a whole 2x2x4 slice. The times are simulated.
32 devices in a mesh: shard: 4 (over z), width: 2 (over core), shift: 4 (over y, x).
Axes of the slice: x: 2, y: 2, z: 4, core: 2. Of those that a mesh axis runs over, the one named last changes fastest.
Arguments:
- w_query: bfloat16 [8192, 2048], P(('shift', 'shard'), 'width'), parts along dimension 0, may hold values from -0.125 to 0.125
- low_query: bfloat16 [8192, 16], P(('shift', 'shard')), parts along dimension 0, may hold values from -0.125 to 0.125
- high_query: bfloat16 [64, 2048], P('shift', 'width'), parts along dimension 0, may hold values from -1.5 to 1.5
- w_key: bfloat16 [8192, 512], P(('shift', 'shard'), 'width'), parts along dimension 0, may hold values from -0.125 to 0.125
- low_key: bfloat16 [8192, 16], P(('shift', 'shard')), parts along dimension 0, may hold values from -0.125 to 0.125
- high_key: bfloat16 [64, 512], P('shift', 'width'), parts along dimension 0, may hold values from -1.5 to 1.5
- w_value: bfloat16 [8192, 512], P(('shift', 'shard'), 'width'), parts along dimension 0, may hold values from -0.125 to 0.125
- low_value: bfloat16 [8192, 16], P(('shift', 'shard')), parts along dimension 0, may hold values from -0.125 to 0.125
- high_value: bfloat16 [64, 512], P('shift', 'width'), parts along dimension 0, may hold values from -1.5 to 1.5
- w_mixed: bfloat16 [8192, 2048], P(('shift', 'width'), 'shard'), parts along dimension 0, may hold values from -0.125 to 0.125
- low_mixed: bfloat16 [8192, 16], P(('shift', 'width')), parts along dimension 0, may hold values from -0.125 to 0.125
- high_mixed: bfloat16 [64, 2048], P('shift', 'shard'), parts along dimension 0, may hold values from -1.5 to 1.5
- norm_train: float32 [8192], P(('shift', 'shard', 'width')), parts along dimension 0, may hold values from 0.25 to 1.75
- norm_step: float32 [8192], P(('shift', 'shard', 'width')), parts along dimension 0, may hold values from -0.3 to 0.3
Outputs:
- final_query: bfloat16 [8192, 2048], P(('shift', 'width')), parts along dimension 0
- final_key: bfloat16 [2048, 2048], P(('shift', 'width')), parts along dimension 0
- final_value: bfloat16 [2048, 2048], P(('shift', 'width')), parts along dimension 0
- final_mixed: bfloat16 [8192, 2048], P('shift', 'width'), parts along dimension 0
- serve_norm: bfloat16 [8192], P('shift'), parts along dimension 0
There are 4 independent parts, one for each index of `shift`. A program takes and returns all parts, laid end to end along the dimension named above; each array names one. Nothing has to cross between parts.
All inputs are finite; a program needn't handle non-finite values.
Results may differ from a plain program's by a relative error of at most 0.001.
Values may be sent and summed in bfloat16 or wider, within the bound.
No kernel may reach another device: no remote copies, remote signals or barrier semaphores. Data moves between devices by JAX's collectives and lax.ppermute only.
A program may use at most 64 MiB of HBM per device.

v0:
```python
import functools

import jax
import jax.numpy as jnp
from jax import lax
from jax.experimental import pallas as pl
from jax.experimental.pallas import tpu as pltpu
from jax.sharding import PartitionSpec as P


mix_rate = 0.5
lanes = 128
sublanes = 8


in_vmem = pl.BlockSpec(memory_space=pltpu.VMEM)
in_hbm = pl.BlockSpec(memory_space=pltpu.HBM)


def merge_body(count, block, extra, *refs):
    sources = refs[: 3 * count]
    row_ref = refs[3 * count] if extra else None
    out_ref = refs[3 * count + extra]
    held = refs[3 * count + extra + 1 : -1]
    sems = refs[-1]
    copies = []
    for j in range(count):
        w, low, high = sources[3 * j : 3 * j + 3]
        w_held, low_held, high_held = held[3 * j : 3 * j + 3]
        columns = w.shape[1]
        pairs = [(low, low_held), (high, high_held)]
        for first in range(0, columns, block):
            part = (slice(None), pl.ds(first, block))
            pairs.append((w.at[part], w_held.at[part]))
        for source, target in pairs:
            copies.append(pltpu.make_async_copy(source, target, sems.at[len(copies)]))
    for copy in copies:
        copy.start()
    waits = iter(copies)
    base = 0
    for j in range(count):
        w_held, low_held, high_held = held[3 * j : 3 * j + 3]
        columns = w_held.shape[1]
        next(waits).wait()
        next(waits).wait()
        for first in range(0, columns, block):
            next(waits).wait()
            part = pl.ds(first, block)
            delta = lax.dot_general(
                high_held[:, part],
                low_held[...],
                (((0,), (0,)), ((), ())),
                preferred_element_type=jnp.float32,
            )
            kept = w_held[:, part].T.astype(jnp.float32)
            out_ref[pl.ds(base + first, block), :] = (kept + mix_rate * delta).astype(jnp.bfloat16)
        base += columns
    if extra:
        out_ref[pl.ds(base, sublanes), :] = jnp.broadcast_to(
            row_ref[...], (sublanes, row_ref.shape[1])
        )


def merged(weights, block, row=None):
    rows = weights[0][0].shape[0]
    columns = sum(w.shape[1] for w, _, _ in weights)
    extra = int(row is not None)
    operands, held, parts = [], [], 0
    for w, low, high in weights:
        operands += [w, low.T, high]
        held += [pltpu.VMEM(array.shape, array.dtype) for array in operands[-3:]]
        parts += 2 + w.shape[1] // block
    operands = [pltpu.with_memory_space_constraint(array, pltpu.HBM) for array in operands]
    return pl.pallas_call(
        functools.partial(merge_body, len(weights), block, extra),
        in_specs=[in_hbm] * len(operands) + [in_vmem] * extra,
        out_specs=in_vmem,
        out_shape=jax.ShapeDtypeStruct((columns + sublanes * extra, rows), jnp.bfloat16),
        scratch_shapes=[*held, pltpu.SemaphoreType.DMA((parts,))],
        compiler_params=pltpu.CompilerParams(vmem_limit_bytes=12 << 20),
    )(*operands, *([row] if extra else []))


def place_body(count, targets, offsets, *refs):
    pieces, outs, sems = refs[: len(offsets)], refs[-1 - len(targets) : -1], refs[-1]
    me = lax.axis_index("shard")
    sign = 1 - 2 * lax.rem(me, 2)
    for act in ("start", "wait"):
        for j, (piece, offset) in enumerate(zip(pieces, offsets)):
            owner = me + sign * offset

            @pl.when(jnp.logical_and(owner >= 0, owner < count))
            def _():
                base = 0
                for t, (rows, axis) in enumerate(targets):
                    extent = rows if axis == 0 else piece.shape[1]
                    start = pl.multiple_of(owner * extent, sublanes if axis == 0 else lanes)
                    where = [slice(None), slice(None)]
                    where[axis] = pl.ds(start, extent)
                    copy = pltpu.make_async_copy(
                        piece.at[pl.ds(base, rows)], outs[t].at[tuple(where)], sems.at[j, t]
                    )
                    getattr(copy, act)()
                    base += rows


def place(outs, pieces, count, targets):
    arrays = [array for array, _ in pieces]
    offsets = [offset for _, offset in pieces]
    width = arrays[0].shape[1]
    shapes = [
        jax.ShapeDtypeStruct((rows * count, width) if axis == 0 else (rows, width * count), jnp.bfloat16)
        for rows, axis in targets
    ]
    return pl.pallas_call(
        functools.partial(place_body, count, targets, offsets),
        in_specs=[in_vmem] * len(arrays) + [in_hbm] * len(outs),
        out_specs=[in_hbm] * len(targets),
        out_shape=shapes,
        scratch_shapes=[pltpu.SemaphoreType.DMA((len(arrays), len(targets)))],
        input_output_aliases={len(arrays) + t: t for t in range(len(outs))},
        compiler_params=pltpu.CompilerParams(vmem_limit_bytes=1 << 20),
    )(*arrays, *outs)


def hops(count):
    plan = []
    for k in range(1, count):
        for name, source, parity in (("a", "b", 0), ("b", "a", 1)):
            pairs = []
            for i in range(parity, count - 1, 2):
                if i + k < count:
                    pairs.append((i + 1, i))
                if i + 1 - k >= 0:
                    pairs.append((i, i + 1))
            if pairs:
                offset = k if parity == 0 else -k
                plan.append((f"{name}{k}", f"{source}{k - 1}", pairs, offset))
    return plan


def by_line(count, query, key, value, mixed, norms):
    first = merged([mixed], 256)
    pair = lax.all_gather((norms[0] + norms[1]).astype(jnp.bfloat16), "width", axis=0, tiled=True)
    second = merged([query], 256, pair[None])
    third = merged([key, value], 256)
    own = [first, second, third]
    targets = [
        ((mixed[0].shape[1], 0),),
        ((query[0].shape[1], 1), (sublanes, 0)),
        ((key[0].shape[1], 1), (value[0].shape[1], 1)),
    ]
    plan = hops(count)
    outs = []
    for c, piece in enumerate(own):
        held = {"a0": piece, "b0": piece}
        arrived = [(piece, 0)]
        out = []
        for k in range(1, count):
            for name, source, pairs, offset in plan:
                if int(name[1:]) == k:
                    held[name] = lax.ppermute(held[source], "shard", pairs)
                    arrived.append((held[name], offset))
            out = place(out, arrived, count, targets[c])
            arrived = []
        outs.append(out)
    final_mixed, final_query, rows = outs[0][0], outs[1][0], outs[1][1]
    serve_norm = rows.reshape(count, sublanes, -1)[:, 0].reshape(-1)
    return final_query, *outs[2], final_mixed, serve_norm


def by_gather(count, query, key, value, mixed, norms):
    finals = []
    for axis, (w, low, high) in ((0, query), (0, key), (0, value), (1, mixed)):
        result = w.astype(jnp.float32) + mix_rate * jnp.dot(
            low, high, preferred_element_type=jnp.float32
        )
        narrow = result.astype(jnp.bfloat16)
        finals.append(lax.all_gather(narrow, "shard", axis=axis, tiled=True).T)
    norm = (norms[0] + norms[1]).astype(jnp.bfloat16)
    serve_norm = lax.all_gather(norm, ("shard", "width"), axis=0, tiled=True)
    return *finals, serve_norm


def on_device(form, count, *args):
    weights = [args[3 * j : 3 * j + 3] for j in range(4)]
    return form(count, *weights, args[12:])


def solution(mesh):
    column_cut = (P(("shift", "shard"), "width"), P(("shift", "shard"), None), P("shift", "width"))
    row_cut = (P(("shift", "width"), "shard"), P(("shift", "width"), None), P("shift", "shard"))
    norm = P(("shift", "shard", "width"))
    count = mesh.shape["shard"]

    def step(*args):
        rows = args[0].shape[0] // (mesh.shape["shift"] * count)
        columns = args[9].shape[1] // count
        narrow = [args[j].shape[1] // mesh.shape["width"] for j in (0, 3, 6)]
        aligned = all(size % (2 * lanes) == 0 for size in (rows, columns, *narrow))
        line = count > 2 and aligned
        program = jax.shard_map(
            functools.partial(on_device, by_line if line else by_gather, count),
            mesh=mesh,
            in_specs=(*column_cut, *column_cut, *column_cut, *row_cut, norm, norm),
            out_specs=(
                P(("shift", "width"), None),
                P(("shift", "width"), None),
                P(("shift", "width"), None),
                P("shift", "width"),
                P("shift"),
            ),
            check_vma=False,
        )
        return program(*args)

    return step
```

profile of v0, /device:TPU:0, one launch (start us, length us, event | category | flops | bytes accessed | tf_op | source)
XLA Modules:
  0.0 205.7 jit_solution(4939015451088785057)
XLA Ops:
  0.6 0.7 add_convert_fusion
  1.3 1.9 all-gather
  3.3 2.1 %shard_map.173.refs_0_ = bf16[1032,512]{1,0:T(8,128)(2,1)S(1)} custom-call(bf16[512,1024]{1,0:T(8,128)(2,1)} %refs_0_.3, bf16[16,512]{1,0:T(8,128)(2,1)} %bitcast.11, bf16[16,1024]{1,0:T(8,128)(2,1)} %refs_2_.3, bf16[1,512]{1,0:T(2,128)(2,1)S(1)} %bitcast.9), custom_call_target="tpu_custom_call" | custom-call | tf_op jit(solution)/shard_map/pallas_call | solution.py:74
  5.4 3.0 %collective-permute-start = (bf16[1032,512]{1,0:T(8,128)(2,1)S(1)}, bf16[1032,512]{1,0:T(8,128)(2,1)S(1)}, u32[]{:S(2)}, u32[]{:S(2)}) collective-permute-start(bf16[1032,512]{1,0:T(8,128)(2,1)S(1)} %shard_map.173.refs_0_), channel_id=1, source_target_pairs={{8,0},{0,8},{24,16},{16,24},{9,1},{1,9},{25,17},{17,25},{10,2},{2,... | collective-permute-start | bytes 3170312 | tf_op jit(solution)/shard_map/ppermute | solution.py:162
  8.4 1.8 shard_map.181.refs_0_
  10.2 1.6 shard_map.177.refs_0_
  11.8 2.1 %collective-permute-start.5 = (bf16[512,512]{1,0:T(8,128)(2,1)S(1)}, bf16[512,512]{1,0:T(8,128)(2,1)S(1)}, u32[]{:S(2)}, u32[]{:S(2)}) collective-permute-start(bf16[512,512]{1,0:T(8,128)(2,1)S(1)} %shard_map.177.refs_0_), channel_id=1, source_target_pairs={{8,0},{0,8},{24,16},{16,24},{9,1},{1,9},{25,17},{17,25},{10,2},{2,... | collective-permute-start | bytes 1572872 | tf_op jit(solution)/shard_map/ppermute | solution.py:162
  13.9 0.7 collective-permute-start.3
  14.6 17.9 %collective-permute-done.refs_1_ = bf16[1032,512]{1,0:T(8,128)(2,1)S(1)} collective-permute-done((bf16[1032,512]{1,0:T(8,128)(2,1)S(1)}, bf16[1032,512]{1,0:T(8,128)(2,1)S(1)}, u32[]{:S(2)}, u32[]{:S(2)}) %collective-permute-start) | collective-permute-done | bytes 1056800 | tf_op jit(solution)/shard_map/ppermute | solution.py:162
  32.6 0.7 collective-permute-start.1
  33.3 0.7 collective-permute-start.8
  34.0 31.8 %collective-permute-done.5.refs_1_ = bf16[512,512]{1,0:T(8,128)(2,1)S(1)} collective-permute-done((bf16[512,512]{1,0:T(8,128)(2,1)S(1)}, bf16[512,512]{1,0:T(8,128)(2,1)S(1)}, u32[]{:S(2)}, u32[]{:S(2)}) %collective-permute-start.5) | collective-permute-done | bytes 524320 | tf_op jit(solution)/shard_map/ppermute | solution.py:162
  65.7 0.7 collective-permute-start.13
  66.5 0.7 collective-permute-start.11
  67.2 0.7 collective-permute-start.6
  67.9 1.3 collective-permute-start.4
  69.2 1.3 collective-permute-start.2
  70.6 1.3 collective-permute-start.9
  71.9 1.3 collective-permute-start.14
  73.2 1.3 collective-permute-start.12
  74.5 71.4 %collective-permute-done.9.refs_0_ = bf16[512,512]{1,0:T(8,128)(2,1)S(1)} collective-permute-done((bf16[512,512]{1,0:T(8,128)(2,1)S(1)}, bf16[512,512]{1,0:T(8,128)(2,1)S(1)}, u32[]{:S(2)}, u32[]{:S(2)}) %collective-permute-start.9) | collective-permute-done | bytes 524320 | tf_op jit(solution)/shard_map/ppermute | solution.py:162
  145.9 1.3 collective-permute-start.7
  147.2 1.0 shard_map.178
  148.2 1.4 shard_map.182.refs_2_
  149.6 0.8 shard_map.179
  150.4 1.4 shard_map.174
  151.8 48.3 %collective-permute-done.7.refs_0_ = bf16[512,512]{1,0:T(8,128)(2,1)S(1)} collective-permute-done((bf16[512,512]{1,0:T(8,128)(2,1)S(1)}, bf16[512,512]{1,0:T(8,128)(2,1)S(1)}, u32[]{:S(2)}, u32[]{:S(2)}) %collective-permute-start.7) | collective-permute-done | bytes 524320 | tf_op jit(solution)/shard_map/ppermute | solution.py:162
  200.1 0.8 shard_map.180
  200.9 1.0 shard_map.183.refs_1_
  202.0 1.0 shard_map.175
  203.0 1.0 shard_map.184
  204.0 1.0 shard_map.176
  (15 shorter events, 0.7 us)
Async XLA Ops:
  5.4 27.2 %collective-permute-start = (bf16[1032,512]{1,0:T(8,128)(2,1)S(1)}, bf16[1032,512]{1,0:T(8,128)(2,1)S(1)}, u32[]{:S(2)}, u32[]{:S(2)}) collective-permute-start(bf16[1032,512]{1,0:T(8,128)(2,1)S(1)} %shard_map.173.refs_0_), channel_id=1, source_target_pairs={{8,0},{0,8},{24,16},{16,24},{9,1},{1,9},{25,17},{17,25},{10,2},{2,... | collective-permute-start | bytes 3170312 | tf_op jit(solution)/shard_map/ppermute | solution.py:162
  10.2 56.3 %collective-permute-start.10 = (bf16[512,1024]{1,0:T(8,128)(2,1)S(1)}, bf16[512,1024]{1,0:T(8,128)(2,1)S(1)}, u32[]{:S(2)}, u32[]{:S(2)}) collective-permute-start(bf16[512,1024]{1,0:T(8,128)(2,1)S(1)} %shard_map.181.refs_0_), channel_id=1, source_target_pairs={{8,0},{0,8},{24,16},{16,24},{9,1},{1,9},{25,17},{17,25},{10,2},{2,... | collective-permute-start | bytes 3145736 | tf_op jit(solution)/shard_map/ppermute | solution.py:162
  11.8 53.9 %collective-permute-start.5 = (bf16[512,512]{1,0:T(8,128)(2,1)S(1)}, bf16[512,512]{1,0:T(8,128)(2,1)S(1)}, u32[]{:S(2)}, u32[]{:S(2)}) collective-permute-start(bf16[512,512]{1,0:T(8,128)(2,1)S(1)} %shard_map.177.refs_0_), channel_id=1, source_target_pairs={{8,0},{0,8},{24,16},{16,24},{9,1},{1,9},{25,17},{17,25},{10,2},{2,... | collective-permute-start | bytes 1572872 | tf_op jit(solution)/shard_map/ppermute | solution.py:162
  13.9 54.0 %collective-permute-start.3 = (bf16[1032,512]{1,0:T(8,128)(2,1)S(1)}, bf16[1032,512]{1,0:T(8,128)(2,1)S(1)}, u32[]{:S(2)}, u32[]{:S(2)}) collective-permute-start(bf16[1032,512]{1,0:T(8,128)(2,1)S(1)} %shard_map.173.refs_0_), channel_id=1, source_target_pairs={{16,8},{8,16},{17,9},{9,17},{18,10},{10,18},{19,11},{11,19},{20,12... | collective-permute-start | bytes 3170312 | tf_op jit(solution)/shard_map/ppermute | solution.py:162
  32.6 36.7 %collective-permute-start.1 = (bf16[1032,512]{1,0:T(8,128)(2,1)S(1)}, bf16[1032,512]{1,0:T(8,128)(2,1)S(1)}, u32[]{:S(2)}, u32[]{:S(2)}) collective-permute-start(bf16[1032,512]{1,0:T(8,128)(2,1)S(1)} %collective-permute-done.refs_1_), channel_id=1, source_target_pairs={{16,8},{8,16},{17,9},{9,17},{18,10},{10,18},{19,11},{11,19},{20,12... | collective-permute-start | bytes 3170312 | tf_op jit(solution)/shard_map/ppermute | solution.py:162
  33.3 33.9 %collective-permute-start.8 = (bf16[512,512]{1,0:T(8,128)(2,1)S(1)}, bf16[512,512]{1,0:T(8,128)(2,1)S(1)}, u32[]{:S(2)}, u32[]{:S(2)}) collective-permute-start(bf16[512,512]{1,0:T(8,128)(2,1)S(1)} %shard_map.177.refs_0_), channel_id=1, source_target_pairs={{16,8},{8,16},{17,9},{9,17},{18,10},{10,18},{19,11},{11,19},{20,12... | collective-permute-start | bytes 1572872 | tf_op jit(solution)/shard_map/ppermute | solution.py:162
  65.7 6.1 %collective-permute-start.13 = (bf16[512,1024]{1,0:T(8,128)(2,1)S(1)}, bf16[512,1024]{1,0:T(8,128)(2,1)S(1)}, u32[]{:S(2)}, u32[]{:S(2)}) collective-permute-start(bf16[512,1024]{1,0:T(8,128)(2,1)S(1)} %shard_map.181.refs_0_), channel_id=1, source_target_pairs={{16,8},{8,16},{17,9},{9,17},{18,10},{10,18},{19,11},{11,19},{20,12... | collective-permute-start | bytes 3145736 | tf_op jit(solution)/shard_map/ppermute | solution.py:162
  66.5 6.7 %collective-permute-start.11 = (bf16[512,1024]{1,0:T(8,128)(2,1)S(1)}, bf16[512,1024]{1,0:T(8,128)(2,1)S(1)}, u32[]{:S(2)}, u32[]{:S(2)}) collective-permute-start(bf16[512,1024]{1,0:T(8,128)(2,1)S(1)} %collective-permute-done.10.refs_1_), channel_id=1, source_target_pairs={{16,8},{8,16},{17,9},{9,17},{18,10},{10,18},{19,11},{11,19},{20,12... | collective-permute-start | bytes 3145736 | tf_op jit(solution)/shard_map/ppermute | solution.py:162
  67.2 3.3 %collective-permute-start.6 = (bf16[512,512]{1,0:T(8,128)(2,1)S(1)}, bf16[512,512]{1,0:T(8,128)(2,1)S(1)}, u32[]{:S(2)}, u32[]{:S(2)}) collective-permute-start(bf16[512,512]{1,0:T(8,128)(2,1)S(1)} %collective-permute-done.5.refs_1_), channel_id=1, source_target_pairs={{16,8},{8,16},{17,9},{9,17},{18,10},{10,18},{19,11},{11,19},{20,12... | collective-permute-start | bytes 1572872 | tf_op jit(solution)/shard_map/ppermute | solution.py:162
  67.9 134.0 %collective-permute-start.4 = (bf16[1032,512]{1,0:T(8,128)(2,1)S(1)}, bf16[1032,512]{1,0:T(8,128)(2,1)S(1)}, u32[]{:S(2)}, u32[]{:S(2)}) collective-permute-start(bf16[1032,512]{1,0:T(8,128)(2,1)S(1)} %collective-permute-done.3.refs_2_), channel_id=1, source_target_pairs={{8,0},{16,24},{9,1},{17,25},{10,2},{18,26},{11,3},{19,27},{12,4},{... | collective-permute-start | bytes 3170312 | tf_op jit(solution)/shard_map/ppermute | solution.py:162
  69.2 134.8 %collective-permute-start.2 = (bf16[1032,512]{1,0:T(8,128)(2,1)S(1)}, bf16[1032,512]{1,0:T(8,128)(2,1)S(1)}, u32[]{:S(2)}, u32[]{:S(2)}) collective-permute-start(bf16[1032,512]{1,0:T(8,128)(2,1)S(1)} %collective-permute-done.1.refs_1_), channel_id=1, source_target_pairs={{8,0},{16,24},{9,1},{17,25},{10,2},{18,26},{11,3},{19,27},{12,4},{... | collective-permute-start | bytes 3170312 | tf_op jit(solution)/shard_map/ppermute | solution.py:162
  70.6 75.3 %collective-permute-start.9 = (bf16[512,512]{1,0:T(8,128)(2,1)S(1)}, bf16[512,512]{1,0:T(8,128)(2,1)S(1)}, u32[]{:S(2)}, u32[]{:S(2)}) collective-permute-start(bf16[512,512]{1,0:T(8,128)(2,1)S(1)} %collective-permute-done.8.refs_2_), channel_id=1, source_target_pairs={{8,0},{16,24},{9,1},{17,25},{10,2},{18,26},{11,3},{19,27},{12,4},{... | collective-permute-start | bytes 1572872 | tf_op jit(solution)/shard_map/ppermute | solution.py:162
  71.9 129.1 %collective-permute-start.14 = (bf16[512,1024]{1,0:T(8,128)(2,1)S(1)}, bf16[512,1024]{1,0:T(8,128)(2,1)S(1)}, u32[]{:S(2)}, u32[]{:S(2)}) collective-permute-start(bf16[512,1024]{1,0:T(8,128)(2,1)S(1)} %collective-permute-done.13.refs_2_), channel_id=1, source_target_pairs={{8,0},{16,24},{9,1},{17,25},{10,2},{18,26},{11,3},{19,27},{12,4},{... | collective-permute-start | bytes 3145736 | tf_op jit(solution)/shard_map/ppermute | solution.py:162
  73.2 129.8 %collective-permute-start.12 = (bf16[512,1024]{1,0:T(8,128)(2,1)S(1)}, bf16[512,1024]{1,0:T(8,128)(2,1)S(1)}, u32[]{:S(2)}, u32[]{:S(2)}) collective-permute-start(bf16[512,1024]{1,0:T(8,128)(2,1)S(1)} %collective-permute-done.11.refs_1_), channel_id=1, source_target_pairs={{8,0},{16,24},{9,1},{17,25},{10,2},{18,26},{11,3},{19,27},{12,4},{... | collective-permute-start | bytes 3145736 | tf_op jit(solution)/shard_map/ppermute | solution.py:162
  145.9 54.3 %collective-permute-start.7 = (bf16[512,512]{1,0:T(8,128)(2,1)S(1)}, bf16[512,512]{1,0:T(8,128)(2,1)S(1)}, u32[]{:S(2)}, u32[]{:S(2)}) collective-permute-start(bf16[512,512]{1,0:T(8,128)(2,1)S(1)} %collective-permute-done.6.refs_1_), channel_id=1, source_target_pairs={{8,0},{16,24},{9,1},{17,25},{10,2},{18,26},{11,3},{19,27},{12,4},{... | collective-permute-start | bytes 1572872 | tf_op jit(solution)/shard_map/ppermute | solution.py:162
where the time goes:
time: 206 us
  waiting for transfers between devices  169 us (82%)
  starting transfers between devices  17.1 us (8%)
  Pallas kernels  14.9 us (7%)
    ppermute x15, waiting for transfers between devices, by_line(): held[name] = lax.ppermute(held[source], 'shard', pairs)  169 us
    ppermute x15, starting transfers between devices, by_line(): held[name] = lax.ppermute(held[source], 'shard', pairs)  17.1 us
    pallas_call x9, Pallas kernels, place(): pl.pallas_call(functools.partial(place_body, count, targets, offsets), in...  9.46 us
    pallas_call x3, Pallas kernels, merged(): pl.pallas_call(functools.partial(merge_body, len(weights), block, extra),...  5.46 us
  transfers between devices with their start and end apart: 15, of which 4 were waited for; matrix products, arithmetic and copies ran while one was open for 0% of the time, Pallas kernels for 6%

commit v1 on v0

v1 whole, which is shorter than its diff:
```python
import functools

import jax
import jax.numpy as jnp
from jax import lax
from jax.experimental import pallas as pl
from jax.experimental.pallas import tpu as pltpu
from jax.sharding import PartitionSpec as P


mix_rate = 0.5
lanes = 128
sublanes = 8


in_vmem = pl.BlockSpec(memory_space=pltpu.VMEM)
in_hbm = pl.BlockSpec(memory_space=pltpu.HBM)


def merge_body(first, blocks, w_ref, low_ref, high_ref, out_ref, w_held, low_held, high_held, sems):
    total = sum(blocks)
    copies = [
        pltpu.make_async_copy(low_ref, low_held, sems.at[0]),
        pltpu.make_async_copy(high_ref.at[:, pl.ds(first, total)], high_held, sems.at[1]),
    ]
    base = 0
    for j, block in enumerate(blocks):
        copies.append(
            pltpu.make_async_copy(
                w_ref.at[:, pl.ds(first + base, block)], w_held.at[:, pl.ds(base, block)], sems.at[2 + j]
            )
        )
        base += block
    for copy in copies:
        copy.start()
    copies[0].wait()
    copies[1].wait()
    base = 0
    for j, block in enumerate(blocks):
        copies[2 + j].wait()
        part = pl.ds(base, block)
        delta = lax.dot_general(
            high_held[:, part],
            low_held[...],
            (((0,), (0,)), ((), ())),
            preferred_element_type=jnp.float32,
        )
        kept = w_held[:, part].T.astype(jnp.float32)
        out_ref[part, :] = (kept + mix_rate * delta).astype(jnp.bfloat16)
        base += block


def merged(w, low, high, first, last):
    rows, total, rank = w.shape[0], last - first, low.shape[1]
    block = 2 * lanes
    blocks = [min(block, total - base) for base in range(0, total, block)]
    operands = [pltpu.with_memory_space_constraint(a, pltpu.HBM) for a in (w, low.T, high)]
    return pl.pallas_call(
        functools.partial(merge_body, first, blocks),
        in_specs=[in_hbm] * 3,
        out_specs=in_vmem,
        out_shape=jax.ShapeDtypeStruct((total, rows), jnp.bfloat16),
        scratch_shapes=[
            pltpu.VMEM((rows, total), jnp.bfloat16),
            pltpu.VMEM((rank, rows), jnp.bfloat16),
            pltpu.VMEM((rank, total), jnp.bfloat16),
            pltpu.SemaphoreType.DMA((2 + len(blocks),)),
        ],
        compiler_params=pltpu.CompilerParams(vmem_limit_bytes=12 << 20),
    )(*operands)


def sum_body(train_ref, step_ref, out_ref):
    out_ref[...] = jnp.zeros_like(out_ref)
    out_ref[: train_ref.shape[0], :] = (train_ref[...] + step_ref[...]).astype(jnp.bfloat16)


def summed(train, step):
    used = train.size // lanes
    tall = -(-used // sublanes) * sublanes
    return pl.pallas_call(
        sum_body,
        in_specs=[in_vmem] * 2,
        out_specs=in_vmem,
        out_shape=jax.ShapeDtypeStruct((tall, lanes), jnp.bfloat16),
        compiler_params=pltpu.CompilerParams(vmem_limit_bytes=1 << 20),
    )(train.reshape(used, lanes), step.reshape(used, lanes))


def place_body(count, axis, extent, base, offsets, *refs):
    pieces, out_ref, sems = refs[: len(offsets)], refs[-2], refs[-1]
    me = lax.axis_index("shard")
    sign = 1 - 2 * lax.rem(me, 2)
    for act in ("start", "wait"):
        for j, (piece, offset) in enumerate(zip(pieces, offsets)):
            owner = me + sign * offset

            @pl.when(jnp.logical_and(owner >= 0, owner < count))
            def _():
                start = pl.multiple_of(owner * extent + base, (sublanes, lanes)[axis])
                where = [slice(None), slice(None)]
                where[axis] = pl.ds(start, piece.shape[axis])
                copy = pltpu.make_async_copy(piece, out_ref.at[tuple(where)], sems.at[j])
                getattr(copy, act)()


def place(out, pieces, count, axis, extent, base):
    arrays = [array for array, _ in pieces]
    offsets = [offset for _, offset in pieces]
    shape = list(arrays[0].shape)
    shape[axis] = count * extent
    operands = arrays + ([] if out is None else [out])
    return pl.pallas_call(
        functools.partial(place_body, count, axis, extent, base, offsets),
        in_specs=[in_vmem] * len(arrays) + [in_hbm] * (len(operands) - len(arrays)),
        out_specs=in_hbm,
        out_shape=jax.ShapeDtypeStruct(tuple(shape), jnp.bfloat16),
        scratch_shapes=[pltpu.SemaphoreType.DMA((len(arrays),))],
        input_output_aliases={} if out is None else {len(arrays): 0},
        compiler_params=pltpu.CompilerParams(vmem_limit_bytes=4 << 20),
    )(*operands)


def hops(count):
    plan = []
    for k in range(1, count):
        for name, source, parity in (("a", "b", 0), ("b", "a", 1)):
            pairs = []
            for i in range(parity, count - 1, 2):
                if i + k < count:
                    pairs.append((i + 1, i))
                if i + 1 - k >= 0:
                    pairs.append((i, i + 1))
            if pairs:
                offset = k if parity == 0 else -k
                plan.append((f"{name}{k}", f"{source}{k - 1}", pairs, offset))
    return plan


chunk_names = ("mixed_head", "mixed_rest", "query", "norm", "key", "value")


def by_line(count, query, key, value, mixed, norms):
    columns = mixed[0].shape[1]
    pieces, where = {}, {}

    def chunk(name, weight, axis, extent, first, last):
        pieces[name] = merged(*weight, first, last)
        where[name] = (axis, extent, first if axis == 0 else 0)

    chunk("mixed_head", mixed, 0, columns, 0, lanes)
    chunk("mixed_rest", mixed, 0, columns, lanes, columns)
    for name, weight in (("query", query), ("key", key), ("value", value)):
        chunk(name, weight, 1, weight[0].shape[0], 0, weight[0].shape[1])
    row = summed(*norms)
    pieces["norm"] = lax.all_gather(row, "width", axis=0, tiled=True)
    where["norm"] = (0, pieces["norm"].shape[0], 0)

    plan = hops(count)
    outs = {}
    held = {name: {"a0": piece, "b0": piece} for name, piece in pieces.items()}
    arrived = {name: [(piece, 0)] for name, piece in pieces.items()}
    for k in range(1, count):
        for name in chunk_names:
            for hop, source, pairs, offset in plan:
                if int(hop[1:]) == k:
                    held[name][hop] = lax.ppermute(held[name][source], "shard", pairs)
                    arrived[name].append((held[name][hop], offset))
            target = name.split("_")[0]
            outs[target] = place(outs.get(target), arrived[name], count, *where[name])
            arrived[name] = []
    used = norms[0].size // lanes
    serve_norm = outs["norm"].reshape(-1, row.shape[0], lanes)[:, :used].reshape(-1)
    return outs["query"], outs["key"], outs["value"], outs["mixed"], serve_norm


def by_gather(count, query, key, value, mixed, norms):
    finals = []
    for axis, (w, low, high) in ((0, query), (0, key), (0, value), (1, mixed)):
        result = w.astype(jnp.float32) + mix_rate * jnp.dot(
            low, high, preferred_element_type=jnp.float32
        )
        narrow = result.astype(jnp.bfloat16)
        finals.append(lax.all_gather(narrow, "shard", axis=axis, tiled=True).T)
    norm = (norms[0] + norms[1]).astype(jnp.bfloat16)
    serve_norm = lax.all_gather(norm, ("shard", "width"), axis=0, tiled=True)
    return *finals, serve_norm


def on_device(form, count, *args):
    weights = [args[3 * j : 3 * j + 3] for j in range(4)]
    return form(count, *weights, args[12:])


def solution(mesh):
    column_cut = (P(("shift", "shard"), "width"), P(("shift", "shard"), None), P("shift", "width"))
    row_cut = (P(("shift", "width"), "shard"), P(("shift", "width"), None), P("shift", "shard"))
    norm = P(("shift", "shard", "width"))
    count = mesh.shape["shard"]

    def step(*args):
        rows = args[0].shape[0] // (mesh.shape["shift"] * count)
        columns = args[9].shape[1] // count
        narrow = [args[j].shape[1] // mesh.shape["width"] for j in (0, 3, 6)]
        gains = args[12].shape[0] // (mesh.shape["shift"] * count * mesh.shape["width"])
        aligned = all(size % (2 * lanes) == 0 for size in (rows, columns, *narrow, gains))
        line = count > 2 and aligned
        program = jax.shard_map(
            functools.partial(on_device, by_line if line else by_gather, count),
            mesh=mesh,
            in_specs=(*column_cut, *column_cut, *column_cut, *row_cut, norm, norm),
            out_specs=(
                P(("shift", "width"), None),
                P(("shift", "width"), None),
                P(("shift", "width"), None),
                P("shift", "width"),
                P("shift"),
            ),
            check_vma=False,
        )
        return program(*args)

    return step
```

time: 206 us -> 266 us (1.29)
  waiting for transfers between devices: 169 us -> 203 us
  starting transfers between devices: 17.1 us -> 36.2 us
  Pallas kernels: 14.9 us -> 21 us
    ppermute x15 -> x30, waiting for transfers between devices: 169 us -> 203 us  [by_line(): held[name][hop] = lax.ppermute(held[name][source], 'shard', pairs)]
    ppermute x15 -> x30, starting transfers between devices: 17.1 us -> 36.2 us  [by_line(): held[name][hop] = lax.ppermute(held[name][source], 'shard', pairs)]
    pallas_call x12 -> x24, Pallas kernels: 14.9 us -> 21 us  [the longest x18 13.4 us: place(): pl.pallas_call(functools.partial(place_body, count, axis, extent, base, o...]
  transfers between devices with their start and end apart: 15 -> 30, of which waited for: 4 -> 9; matrix products, arithmetic and copies ran while one was open for 0% -> 0% of each run, Pallas kernels for 6% -> 7%
where the time goes in v1:
time: 266 us
  waiting for transfers between devices  203 us (76%)
  starting transfers between devices  36.2 us (14%)
  Pallas kernels  21 us (8%)
    ppermute x30, waiting for transfers between devices, by_line(): held[name][hop] = lax.ppermute(held[name][source], 'shard', pairs)  203 us
    ppermute x30, starting transfers between devices, by_line(): held[name][hop] = lax.ppermute(held[name][source], 'shard', pairs)  36.2 us
    pallas_call x18, Pallas kernels, place(): pl.pallas_call(functools.partial(place_body, count, axis, extent, base, o...  13.4 us
    pallas_call x5, Pallas kernels, merged(): pl.pallas_call(functools.partial(merge_body, first, blocks), in_specs=[in...  7.64 us
  transfers between devices with their start and end apart: 30, of which 9 were waited for; matrix products, arithmetic and copies ran while one was open for 0% of the time, Pallas kernels for 7%

profile of v1, /device:TPU:0, one launch (start us, length us, event | category | flops | bytes accessed | tf_op | source)
XLA Modules:
  0.0 265.6 jit_solution(3231090055787732819)
XLA Ops:
  0.6 2.1 shard_map.173.refs_0_
  2.7 3.1 %collective-permute-start = (bf16[1024,512]{1,0:T(8,128)(2,1)S(1)}, bf16[1024,512]{1,0:T(8,128)(2,1)S(1)}, u32[]{:S(2)}, u32[]{:S(2)}) collective-permute-start(bf16[1024,512]{1,0:T(8,128)(2,1)S(1)} %shard_map.173.refs_0_), channel_id=1, source_target_pairs={{8,0},{0,8},{24,16},{16,24},{9,1},{1,9},{25,17},{17,25},{10,2},{2,... | collective-permute-start | bytes 3145736 | tf_op jit(solution)/shard_map/ppermute | solution.py:167
  5.9 1.3 shard_map.186.refs_0_
  9.3 1.8 all_gather.3.refs_0_
  11.1 4.8 %collective-permute-start.25 = (bf16[16,128]{1,0:T(8,128)(2,1)S(1)}, bf16[16,128]{1,0:T(8,128)(2,1)S(1)}, u32[]{:S(2)}, u32[]{:S(2)}) collective-permute-start(bf16[16,128]{1,0:T(8,128)(2,1)S(1)} %all_gather.3.refs_0_), channel_id=1, source_target_pairs={{8,0},{0,8},{24,16},{16,24},{9,1},{1,9},{25,17},{17,25},{10,2},{2,... | collective-permute-start | bytes 12296 | tf_op jit(solution)/shard_map/ppermute | solution.py:167
  16.6 18.1 %collective-permute-done.25.refs_1_ = bf16[16,128]{1,0:T(8,128)(2,1)S(1)} collective-permute-done((bf16[16,128]{1,0:T(8,128)(2,1)S(1)}, bf16[16,128]{1,0:T(8,128)(2,1)S(1)}, u32[]{:S(2)}, u32[]{:S(2)}) %collective-permute-start.25) | collective-permute-done | bytes 4128 | tf_op jit(solution)/shard_map/ppermute | solution.py:167
  35.4 1.3 collective-permute-start.29
  36.7 1.3 collective-permute-start.27
  38.0 1.3 shard_map.177.refs_0_
  39.3 3.5 %collective-permute-done.29.refs_0_ = bf16[16,128]{1,0:T(8,128)(2,1)S(1)} collective-permute-done((bf16[16,128]{1,0:T(8,128)(2,1)S(1)}, bf16[16,128]{1,0:T(8,128)(2,1)S(1)}, u32[]{:S(2)}, u32[]{:S(2)}) %collective-permute-start.29) | collective-permute-done | bytes 4128 | tf_op jit(solution)/shard_map/ppermute | solution.py:167
  42.8 1.8 collective-permute-start.5
  45.5 1.7 shard_map.185.refs_0_
  47.2 1.3 shard_map.181.refs_0_
  48.5 2.7 %collective-permute-start.10 = (bf16[256,512]{1,0:T(8,128)(2,1)S(1)}, bf16[256,512]{1,0:T(8,128)(2,1)S(1)}, u32[]{:S(2)}, u32[]{:S(2)}) collective-permute-start(bf16[256,512]{1,0:T(8,128)(2,1)S(1)} %shard_map.181.refs_0_), channel_id=1, source_target_pairs={{8,0},{0,8},{24,16},{16,24},{9,1},{1,9},{25,17},{17,25},{10,2},{2,... | collective-permute-start | bytes 786440 | tf_op jit(solution)/shard_map/ppermute | solution.py:167
  52.7 5.7 %collective-permute-done.10.refs_1_ = bf16[256,512]{1,0:T(8,128)(2,1)S(1)} collective-permute-done((bf16[256,512]{1,0:T(8,128)(2,1)S(1)}, bf16[256,512]{1,0:T(8,128)(2,1)S(1)}, u32[]{:S(2)}, u32[]{:S(2)}) %collective-permute-start.10) | collective-permute-done | bytes 262176 | tf_op jit(solution)/shard_map/ppermute | solution.py:167
  59.8 1.3 collective-permute-start.24
  61.8 15.9 %collective-permute-done.24.refs_0_ = bf16[128,1024]{1,0:T(8,128)(2,1)S(1)} collective-permute-done((bf16[128,1024]{1,0:T(8,128)(2,1)S(1)}, bf16[128,1024]{1,0:T(8,128)(2,1)S(1)}, u32[]{:S(2)}, u32[]{:S(2)}) %collective-permute-start.24) | collective-permute-done | bytes 262176 | tf_op jit(solution)/shard_map/ppermute | solution.py:167
  77.7 1.3 collective-permute-start.9
  80.4 5.5 %collective-permute-done.9.refs_0_ = bf16[256,512]{1,0:T(8,128)(2,1)S(1)} collective-permute-done((bf16[256,512]{1,0:T(8,128)(2,1)S(1)}, bf16[256,512]{1,0:T(8,128)(2,1)S(1)}, u32[]{:S(2)}, u32[]{:S(2)}) %collective-permute-start.9) | collective-permute-done | bytes 262176 | tf_op jit(solution)/shard_map/ppermute | solution.py:167
  86.6 1.3 collective-permute-start.14
  87.9 1.3 collective-permute-start.4
  89.3 1.3 collective-permute-start.2
  90.6 1.3 collective-permute-start.22
  91.9 73.0 %collective-permute-done.14.refs_0_ = bf16[256,512]{1,0:T(8,128)(2,1)S(1)} collective-permute-done((bf16[256,512]{1,0:T(8,128)(2,1)S(1)}, bf16[256,512]{1,0:T(8,128)(2,1)S(1)}, u32[]{:S(2)}, u32[]{:S(2)}) %collective-permute-start.14) | collective-permute-done | bytes 262176 | tf_op jit(solution)/shard_map/ppermute | solution.py:167
  164.8 1.3 collective-permute-start.7
  166.1 1.3 collective-permute-start.17
  167.4 64.8 %collective-permute-done.7.refs_0_ = bf16[256,512]{1,0:T(8,128)(2,1)S(1)} collective-permute-done((bf16[256,512]{1,0:T(8,128)(2,1)S(1)}, bf16[256,512]{1,0:T(8,128)(2,1)S(1)}, u32[]{:S(2)}, u32[]{:S(2)}) %collective-permute-start.7) | collective-permute-done | bytes 262176 | tf_op jit(solution)/shard_map/ppermute | solution.py:167
  232.3 1.3 collective-permute-start.12
  233.5 16.6 %collective-permute-done.12.refs_0_ = bf16[256,512]{1,0:T(8,128)(2,1)S(1)} collective-permute-done((bf16[256,512]{1,0:T(8,128)(2,1)S(1)}, bf16[256,512]{1,0:T(8,128)(2,1)S(1)}, u32[]{:S(2)}, u32[]{:S(2)}) %collective-permute-start.12) | collective-permute-done | bytes 262176 | tf_op jit(solution)/shard_map/ppermute | solution.py:167
  250.1 1.3 collective-permute-start.20
  257.7 1.2 shard_map.188.refs_2_
  259.6 1.4 shard_map.174.refs_2_
  (58 shorter events, 21.5 us)
Async XLA Ops:
  2.7 56.3 %collective-permute-start = (bf16[1024,512]{1,0:T(8,128)(2,1)S(1)}, bf16[1024,512]{1,0:T(8,128)(2,1)S(1)}, u32[]{:S(2)}, u32[]{:S(2)}) collective-permute-start(bf16[1024,512]{1,0:T(8,128)(2,1)S(1)} %shard_map.173.refs_0_), channel_id=1, source_target_pairs={{8,0},{0,8},{24,16},{16,24},{9,1},{1,9},{25,17},{17,25},{10,2},{2,... | collective-permute-start | bytes 3145736 | tf_op jit(solution)/shard_map/ppermute | solution.py:167
  7.1 41.4 %collective-permute-start.18 = (bf16[128,1024]{1,0:T(8,128)(2,1)S(1)}, bf16[128,1024]{1,0:T(8,128)(2,1)S(1)}, u32[]{:S(2)}, u32[]{:S(2)}) collective-permute-start(bf16[128,1024]{1,0:T(8,128)(2,1)S(1)} %shard_map.186.refs_0_), channel_id=1, source_target_pairs={{8,0},{0,8},{24,16},{16,24},{9,1},{1,9},{25,17},{17,25},{10,2},{2,... | collective-permute-start | bytes 786440 | tf_op jit(solution)/shard_map/ppermute | solution.py:167
  7.2 44.0 %collective-permute-start.23 = (bf16[128,1024]{1,0:T(8,128)(2,1)S(1)}, bf16[128,1024]{1,0:T(8,128)(2,1)S(1)}, u32[]{:S(2)}, u32[]{:S(2)}) collective-permute-start(bf16[128,1024]{1,0:T(8,128)(2,1)S(1)} %shard_map.186.refs_0_), channel_id=1, source_target_pairs={{16,8},{8,16},{17,9},{9,17},{18,10},{10,18},{19,11},{11,19},{20,12... | collective-permute-start | bytes 786440 | tf_op jit(solution)/shard_map/ppermute | solution.py:167
  7.9 0.7 copy-start
  8.6 0.7 copy-start.1
  11.1 23.6 %collective-permute-start.25 = (bf16[16,128]{1,0:T(8,128)(2,1)S(1)}, bf16[16,128]{1,0:T(8,128)(2,1)S(1)}, u32[]{:S(2)}, u32[]{:S(2)}) collective-permute-start(bf16[16,128]{1,0:T(8,128)(2,1)S(1)} %all_gather.3.refs_0_), channel_id=1, source_target_pairs={{8,0},{0,8},{24,16},{16,24},{9,1},{1,9},{25,17},{17,25},{10,2},{2,... | collective-permute-start | bytes 12296 | tf_op jit(solution)/shard_map/ppermute | solution.py:167
  15.9 19.4 %collective-permute-start.28 = (bf16[16,128]{1,0:T(8,128)(2,1)S(1)}, bf16[16,128]{1,0:T(8,128)(2,1)S(1)}, u32[]{:S(2)}, u32[]{:S(2)}) collective-permute-start(bf16[16,128]{1,0:T(8,128)(2,1)S(1)} %all_gather.3.refs_0_), channel_id=1, source_target_pairs={{16,8},{8,16},{17,9},{9,17},{18,10},{10,18},{19,11},{11,19},{20,12... | collective-permute-start | bytes 12296 | tf_op jit(solution)/shard_map/ppermute | solution.py:167
  34.7 2.0 collective-permute-start.26
  35.4 7.4 %collective-permute-start.29 = (bf16[16,128]{1,0:T(8,128)(2,1)S(1)}, bf16[16,128]{1,0:T(8,128)(2,1)S(1)}, u32[]{:S(2)}, u32[]{:S(2)}) collective-permute-start(bf16[16,128]{1,0:T(8,128)(2,1)S(1)} %collective-permute-done.28.refs_2_), channel_id=1, source_target_pairs={{8,0},{16,24},{9,1},{17,25},{10,2},{18,26},{11,3},{19,27},{12,4},{... | collective-permute-start | bytes 12296 | tf_op jit(solution)/shard_map/ppermute | solution.py:167
  36.7 8.1 %collective-permute-start.27 = (bf16[16,128]{1,0:T(8,128)(2,1)S(1)}, bf16[16,128]{1,0:T(8,128)(2,1)S(1)}, u32[]{:S(2)}, u32[]{:S(2)}) collective-permute-start(bf16[16,128]{1,0:T(8,128)(2,1)S(1)} %collective-permute-done.26.refs_1_), channel_id=1, source_target_pairs={{8,0},{16,24},{9,1},{17,25},{10,2},{18,26},{11,3},{19,27},{12,4},{... | collective-permute-start | bytes 12296 | tf_op jit(solution)/shard_map/ppermute | solution.py:167
  42.8 8.5 %collective-permute-start.5 = (bf16[256,512]{1,0:T(8,128)(2,1)S(1)}, bf16[256,512]{1,0:T(8,128)(2,1)S(1)}, u32[]{:S(2)}, u32[]{:S(2)}) collective-permute-start(bf16[256,512]{1,0:T(8,128)(2,1)S(1)} %shard_map.177.refs_0_), channel_id=1, source_target_pairs={{8,0},{0,8},{24,16},{16,24},{9,1},{1,9},{25,17},{17,25},{10,2},{2,... | collective-permute-start | bytes 786440 | tf_op jit(solution)/shard_map/ppermute | solution.py:167
  44.8 7.1 %collective-permute-start.8 = (bf16[256,512]{1,0:T(8,128)(2,1)S(1)}, bf16[256,512]{1,0:T(8,128)(2,1)S(1)}, u32[]{:S(2)}, u32[]{:S(2)}) collective-permute-start(bf16[256,512]{1,0:T(8,128)(2,1)S(1)} %shard_map.177.refs_0_), channel_id=1, source_target_pairs={{16,8},{8,16},{17,9},{9,17},{18,10},{10,18},{19,11},{11,19},{20,12... | collective-permute-start | bytes 786440 | tf_op jit(solution)/shard_map/ppermute | solution.py:167
  48.5 9.8 %collective-permute-start.10 = (bf16[256,512]{1,0:T(8,128)(2,1)S(1)}, bf16[256,512]{1,0:T(8,128)(2,1)S(1)}, u32[]{:S(2)}, u32[]{:S(2)}) collective-permute-start(bf16[256,512]{1,0:T(8,128)(2,1)S(1)} %shard_map.181.refs_0_), channel_id=1, source_target_pairs={{8,0},{0,8},{24,16},{16,24},{9,1},{1,9},{25,17},{17,25},{10,2},{2,... | collective-permute-start | bytes 786440 | tf_op jit(solution)/shard_map/ppermute | solution.py:167
  51.2 28.5 %collective-permute-start.15 = (bf16[384,1024]{1,0:T(8,128)(2,1)S(1)}, bf16[384,1024]{1,0:T(8,128)(2,1)S(1)}, u32[]{:S(2)}, u32[]{:S(2)}) collective-permute-start(bf16[384,1024]{1,0:T(8,128)(2,1)S(1)} %shard_map.185.refs_0_), channel_id=1, source_target_pairs={{8,0},{0,8},{24,16},{16,24},{9,1},{1,9},{25,17},{17,25},{10,2},{2,... | collective-permute-start | bytes 2359304 | tf_op jit(solution)/shard_map/ppermute | solution.py:167
  51.3 8.5 %collective-permute-start.13 = (bf16[256,512]{1,0:T(8,128)(2,1)S(1)}, bf16[256,512]{1,0:T(8,128)(2,1)S(1)}, u32[]{:S(2)}, u32[]{:S(2)}) collective-permute-start(bf16[256,512]{1,0:T(8,128)(2,1)S(1)} %shard_map.181.refs_0_), channel_id=1, source_target_pairs={{16,8},{8,16},{17,9},{9,17},{18,10},{10,18},{19,11},{11,19},{20,12... | collective-permute-start | bytes 786440 | tf_op jit(solution)/shard_map/ppermute | solution.py:167
  52.0 9.2 %collective-permute-start.19 = (bf16[128,1024]{1,0:T(8,128)(2,1)S(1)}, bf16[128,1024]{1,0:T(8,128)(2,1)S(1)}, u32[]{:S(2)}, u32[]{:S(2)}) collective-permute-start(bf16[128,1024]{1,0:T(8,128)(2,1)S(1)} %collective-permute-done.18.refs_1_), channel_id=1, source_target_pairs={{16,8},{8,16},{17,9},{9,17},{18,10},{10,18},{19,11},{11,19},{20,12... | collective-permute-start | bytes 786440 | tf_op jit(solution)/shard_map/ppermute | solution.py:167
  58.4 29.6 %collective-permute-start.3 = (bf16[1024,512]{1,0:T(8,128)(2,1)S(1)}, bf16[1024,512]{1,0:T(8,128)(2,1)S(1)}, u32[]{:S(2)}, u32[]{:S(2)}) collective-permute-start(bf16[1024,512]{1,0:T(8,128)(2,1)S(1)} %shard_map.173.refs_0_), channel_id=1, source_target_pairs={{16,8},{8,16},{17,9},{9,17},{18,10},{10,18},{19,11},{11,19},{20,12... | collective-permute-start | bytes 3145736 | tf_op jit(solution)/shard_map/ppermute | solution.py:167
  59.1 30.2 %collective-permute-start.1 = (bf16[1024,512]{1,0:T(8,128)(2,1)S(1)}, bf16[1024,512]{1,0:T(8,128)(2,1)S(1)}, u32[]{:S(2)}, u32[]{:S(2)}) collective-permute-start(bf16[1024,512]{1,0:T(8,128)(2,1)S(1)} %collective-permute-done.refs_1_), channel_id=1, source_target_pairs={{16,8},{8,16},{17,9},{9,17},{18,10},{10,18},{19,11},{11,19},{20,12... | collective-permute-start | bytes 3145736 | tf_op jit(solution)/shard_map/ppermute | solution.py:167
  59.8 17.9 %collective-permute-start.24 = (bf16[128,1024]{1,0:T(8,128)(2,1)S(1)}, bf16[128,1024]{1,0:T(8,128)(2,1)S(1)}, u32[]{:S(2)}, u32[]{:S(2)}) collective-permute-start(bf16[128,1024]{1,0:T(8,128)(2,1)S(1)} %collective-permute-done.23.refs_2_), channel_id=1, source_target_pairs={{8,0},{16,24},{9,1},{17,25},{10,2},{18,26},{11,3},{19,27},{12,4},{... | collective-permute-start | bytes 786440 | tf_op jit(solution)/shard_map/ppermute | solution.py:167
  61.2 17.8 %collective-permute-start.6 = (bf16[256,512]{1,0:T(8,128)(2,1)S(1)}, bf16[256,512]{1,0:T(8,128)(2,1)S(1)}, u32[]{:S(2)}, u32[]{:S(2)}) collective-permute-start(bf16[256,512]{1,0:T(8,128)(2,1)S(1)} %collective-permute-done.5.refs_1_), channel_id=1, source_target_pairs={{16,8},{8,16},{17,9},{9,17},{18,10},{10,18},{19,11},{11,19},{20,12... | collective-permute-start | bytes 786440 | tf_op jit(solution)/shard_map/ppermute | solution.py:167
  77.7 8.3 %collective-permute-start.9 = (bf16[256,512]{1,0:T(8,128)(2,1)S(1)}, bf16[256,512]{1,0:T(8,128)(2,1)S(1)}, u32[]{:S(2)}, u32[]{:S(2)}) collective-permute-start(bf16[256,512]{1,0:T(8,128)(2,1)S(1)} %collective-permute-done.8.refs_2_), channel_id=1, source_target_pairs={{8,0},{16,24},{9,1},{17,25},{10,2},{18,26},{11,3},{19,27},{12,4},{... | collective-permute-start | bytes 786440 | tf_op jit(solution)/shard_map/ppermute | solution.py:167
  79.0 11.6 %collective-permute-start.21 = (bf16[384,1024]{1,0:T(8,128)(2,1)S(1)}, bf16[384,1024]{1,0:T(8,128)(2,1)S(1)}, u32[]{:S(2)}, u32[]{:S(2)}) collective-permute-start(bf16[384,1024]{1,0:T(8,128)(2,1)S(1)} %shard_map.185.refs_0_), channel_id=1, source_target_pairs={{16,8},{8,16},{17,9},{9,17},{18,10},{10,18},{19,11},{11,19},{20,12... | collective-permute-start | bytes 2359304 | tf_op jit(solution)/shard_map/ppermute | solution.py:167
  79.7 86.4 %collective-permute-start.16 = (bf16[384,1024]{1,0:T(8,128)(2,1)S(1)}, bf16[384,1024]{1,0:T(8,128)(2,1)S(1)}, u32[]{:S(2)}, u32[]{:S(2)}) collective-permute-start(bf16[384,1024]{1,0:T(8,128)(2,1)S(1)} %collective-permute-done.15.refs_1_), channel_id=1, source_target_pairs={{16,8},{8,16},{17,9},{9,17},{18,10},{10,18},{19,11},{11,19},{20,12... | collective-permute-start | bytes 2359304 | tf_op jit(solution)/shard_map/ppermute | solution.py:167
  85.9 0.7 collective-permute-start.11
  86.6 78.2 %collective-permute-start.14 = (bf16[256,512]{1,0:T(8,128)(2,1)S(1)}, bf16[256,512]{1,0:T(8,128)(2,1)S(1)}, u32[]{:S(2)}, u32[]{:S(2)}) collective-permute-start(bf16[256,512]{1,0:T(8,128)(2,1)S(1)} %collective-permute-done.13.refs_2_), channel_id=1, source_target_pairs={{8,0},{16,24},{9,1},{17,25},{10,2},{18,26},{11,3},{19,27},{12,4},{... | collective-permute-start | bytes 786440 | tf_op jit(solution)/shard_map/ppermute | solution.py:167
  87.9 174.7 %collective-permute-start.4 = (bf16[1024,512]{1,0:T(8,128)(2,1)S(1)}, bf16[1024,512]{1,0:T(8,128)(2,1)S(1)}, u32[]{:S(2)}, u32[]{:S(2)}) collective-permute-start(bf16[1024,512]{1,0:T(8,128)(2,1)S(1)} %collective-permute-done.3.refs_2_), channel_id=1, source_target_pairs={{8,0},{16,24},{9,1},{17,25},{10,2},{18,26},{11,3},{19,27},{12,4},{... | collective-permute-start | bytes 3145736 | tf_op jit(solution)/shard_map/ppermute | solution.py:167
  89.3 175.4 %collective-permute-start.2 = (bf16[1024,512]{1,0:T(8,128)(2,1)S(1)}, bf16[1024,512]{1,0:T(8,128)(2,1)S(1)}, u32[]{:S(2)}, u32[]{:S(2)}) collective-permute-start(bf16[1024,512]{1,0:T(8,128)(2,1)S(1)} %collective-permute-done.1.refs_1_), channel_id=1, source_target_pairs={{8,0},{16,24},{9,1},{17,25},{10,2},{18,26},{11,3},{19,27},{12,4},{... | collective-permute-start | bytes 3145736 | tf_op jit(solution)/shard_map/ppermute | solution.py:167
  90.6 170.4 %collective-permute-start.22 = (bf16[384,1024]{1,0:T(8,128)(2,1)S(1)}, bf16[384,1024]{1,0:T(8,128)(2,1)S(1)}, u32[]{:S(2)}, u32[]{:S(2)}) collective-permute-start(bf16[384,1024]{1,0:T(8,128)(2,1)S(1)} %collective-permute-done.21.refs_2_), channel_id=1, source_target_pairs={{8,0},{16,24},{9,1},{17,25},{10,2},{18,26},{11,3},{19,27},{12,4},{... | collective-permute-start | bytes 2359304 | tf_op jit(solution)/shard_map/ppermute | solution.py:167
  164.8 67.4 %collective-permute-start.7 = (bf16[256,512]{1,0:T(8,128)(2,1)S(1)}, bf16[256,512]{1,0:T(8,128)(2,1)S(1)}, u32[]{:S(2)}, u32[]{:S(2)}) collective-permute-start(bf16[256,512]{1,0:T(8,128)(2,1)S(1)} %collective-permute-done.6.refs_1_), channel_id=1, source_target_pairs={{8,0},{16,24},{9,1},{17,25},{10,2},{18,26},{11,3},{19,27},{12,4},{... | collective-permute-start | bytes 786440 | tf_op jit(solution)/shard_map/ppermute | solution.py:167
  166.1 97.5 %collective-permute-start.17 = (bf16[384,1024]{1,0:T(8,128)(2,1)S(1)}, bf16[384,1024]{1,0:T(8,128)(2,1)S(1)}, u32[]{:S(2)}, u32[]{:S(2)}) collective-permute-start(bf16[384,1024]{1,0:T(8,128)(2,1)S(1)} %collective-permute-done.16.refs_1_), channel_id=1, source_target_pairs={{8,0},{16,24},{9,1},{17,25},{10,2},{18,26},{11,3},{19,27},{12,4},{... | collective-permute-start | bytes 2359304 | tf_op jit(solution)/shard_map/ppermute | solution.py:167
  232.3 17.9 %collective-permute-start.12 = (bf16[256,512]{1,0:T(8,128)(2,1)S(1)}, bf16[256,512]{1,0:T(8,128)(2,1)S(1)}, u32[]{:S(2)}, u32[]{:S(2)}) collective-permute-start(bf16[256,512]{1,0:T(8,128)(2,1)S(1)} %collective-permute-done.11.refs_1_), channel_id=1, source_target_pairs={{8,0},{16,24},{9,1},{17,25},{10,2},{18,26},{11,3},{19,27},{12,4},{... | collective-permute-start | bytes 786440 | tf_op jit(solution)/shard_map/ppermute | solution.py:167
  250.1 11.8 %collective-permute-start.20 = (bf16[128,1024]{1,0:T(8,128)(2,1)S(1)}, bf16[128,1024]{1,0:T(8,128)(2,1)S(1)}, u32[]{:S(2)}, u32[]{:S(2)}) collective-permute-start(bf16[128,1024]{1,0:T(8,128)(2,1)S(1)} %collective-permute-done.19.refs_1_), channel_id=1, source_target_pairs={{8,0},{16,24},{9,1},{17,25},{10,2},{18,26},{11,3},{19,27},{12,4},{... | collective-permute-start | bytes 786440 | tf_op jit(solution)/shard_map/ppermute | solution.py:167

commit v2 on v1

v2 whole, which is shorter than its diff:
```python
import functools

import jax
import jax.numpy as jnp
from jax import lax
from jax.experimental import pallas as pl
from jax.experimental.pallas import tpu as pltpu
from jax.sharding import PartitionSpec as P


mix_rate = 0.5
lanes = 128
sublanes = 8


in_vmem = pl.BlockSpec(memory_space=pltpu.VMEM)
in_hbm = pl.BlockSpec(memory_space=pltpu.HBM)


def merge_body(spans, *refs):
    count = len(spans)
    inputs = 3 * sum(span is not None for span in spans) + 2 * sum(span is None for span in spans)
    sources, outs = iter(refs[:inputs]), refs[inputs : inputs + count]
    held, sems = iter(refs[inputs + count : -1]), refs[-1]
    work = []
    used = 0

    def start(source, target):
        nonlocal used
        copy = pltpu.make_async_copy(source, target, sems.at[used])
        copy.start()
        used += 1
        return copy

    for span, out_ref in zip(spans, outs):
        if span is None:
            work.append((next(sources), next(sources), out_ref))
            continue
        first, blocks = span
        w_ref, low_ref, high_ref = (next(sources) for _ in range(3))
        w_held, low_held, high_held = (next(held) for _ in range(3))
        copies = [
            start(low_ref, low_held),
            start(high_ref.at[:, pl.ds(first, sum(blocks))], high_held),
        ]
        base = 0
        parts = []
        for block in blocks:
            part = pl.ds(base, block)
            copies.append(start(w_ref.at[:, pl.ds(first + base, block)], w_held.at[:, part]))
            parts.append(part)
            base += block
        work.append((w_held, low_held, high_held, copies, parts, out_ref))
    for item in work:
        if len(item) == 3:
            train_ref, step_ref, out_ref = item
            out_ref[...] = jnp.zeros_like(out_ref)
            out_ref[: train_ref.shape[0], :] = (train_ref[...] + step_ref[...]).astype(jnp.bfloat16)
            continue
        w_held, low_held, high_held, copies, parts, out_ref = item
        copies[0].wait()
        copies[1].wait()
        for part, copy in zip(parts, copies[2:]):
            copy.wait()
            delta = lax.dot_general(
                high_held[:, part],
                low_held[...],
                (((0,), (0,)), ((), ())),
                preferred_element_type=jnp.float32,
            )
            kept = w_held[:, part].T.astype(jnp.float32)
            out_ref[part, :] = (kept + mix_rate * delta).astype(jnp.bfloat16)


def merged(*tasks):
    spans, operands, specs, shapes, scratch, copies = [], [], [], [], [], 0
    for task in tasks:
        if len(task) == 2:
            used = task[0].size // lanes
            tall = -(-used // sublanes) * sublanes
            spans.append(None)
            operands += [a.reshape(used, lanes) for a in task]
            specs += [in_vmem] * 2
            shapes.append(jax.ShapeDtypeStruct((tall, lanes), jnp.bfloat16))
            continue
        w, low, high, first, last = task
        rows, total, rank = w.shape[0], last - first, low.shape[1]
        block = 2 * lanes
        blocks = [min(block, total - base) for base in range(0, total, block)]
        spans.append((first, blocks))
        operands += [pltpu.with_memory_space_constraint(a, pltpu.HBM) for a in (w, low.T, high)]
        specs += [in_hbm] * 3
        shapes.append(jax.ShapeDtypeStruct((total, rows), jnp.bfloat16))
        scratch += [
            pltpu.VMEM((rows, total), jnp.bfloat16),
            pltpu.VMEM((rank, rows), jnp.bfloat16),
            pltpu.VMEM((rank, total), jnp.bfloat16),
        ]
        copies += 2 + len(blocks)
    return pl.pallas_call(
        functools.partial(merge_body, spans),
        in_specs=specs,
        out_specs=[in_vmem] * len(shapes),
        out_shape=shapes,
        scratch_shapes=[*scratch, pltpu.SemaphoreType.DMA((copies,))],
        compiler_params=pltpu.CompilerParams(vmem_limit_bytes=12 << 20),
    )(*operands)


def place_body(count, moves, outs_at, *refs):
    sems = refs[-1]
    me = lax.axis_index("shard")
    sign = 1 - 2 * lax.rem(me, 2)
    for act in ("start", "wait"):
        for j, (piece, (out, axis, extent, base, offset)) in enumerate(zip(refs, moves)):
            owner = me + sign * offset

            @pl.when(jnp.logical_and(owner >= 0, owner < count))
            def _():
                start = pl.multiple_of(owner * extent + base, (sublanes, lanes)[axis])
                where = [slice(None), slice(None)]
                where[axis] = pl.ds(start, piece.shape[axis])
                copy = pltpu.make_async_copy(piece, refs[outs_at + out].at[tuple(where)], sems.at[j])
                getattr(copy, act)()


def place(outs, pieces, count):
    targets = list(dict.fromkeys(piece[0] for piece in pieces))
    arrays = [piece[-1] for piece in pieces]
    moves = [(targets.index(piece[0]), *piece[1:-1]) for piece in pieces]
    shapes = []
    for target in targets:
        _, axis, extent, _, _, array = next(piece for piece in pieces if piece[0] == target)
        shape = list(array.shape)
        shape[axis] = count * extent
        shapes.append(jax.ShapeDtypeStruct(tuple(shape), jnp.bfloat16))
    kept = [outs[target] for target in targets if target in outs]
    placed = pl.pallas_call(
        functools.partial(place_body, count, moves, len(arrays) + len(kept)),
        in_specs=[in_vmem] * len(arrays) + [in_hbm] * len(kept),
        out_specs=[in_hbm] * len(targets),
        out_shape=shapes,
        scratch_shapes=[pltpu.SemaphoreType.DMA((len(arrays),))],
        input_output_aliases={len(arrays) + j: j for j in range(len(kept))},
        compiler_params=pltpu.CompilerParams(vmem_limit_bytes=4 << 20),
    )(*arrays, *kept)
    outs.update(zip(targets, placed))


def hops(count):
    plan = []
    for k in range(1, count):
        for name, source, parity in (("a", "b", 0), ("b", "a", 1)):
            pairs = []
            for i in range(parity, count - 1, 2):
                if i + k < count:
                    pairs.append((i + 1, i))
                if i + 1 - k >= 0:
                    pairs.append((i, i + 1))
            if pairs:
                offset = k if parity == 0 else -k
                plan.append((f"{name}{k}", f"{source}{k - 1}", pairs, offset))
    return plan


chunk_names = ("mixed_head", "mixed_rest", "query", "norm", "key", "value")


def groups(count):
    whole = (chunk_names,)
    return [whole] * (count - 2) + [(chunk_names[:-2], chunk_names[-2:-1], chunk_names[-1:])]


def by_line(count, query, key, value, mixed, norms):
    rows, columns = query[0].shape[0], mixed[0].shape[1]
    pieces = {}
    (pieces["mixed_head"],) = merged((*mixed, 0, lanes))
    (pieces["mixed_rest"],) = merged((*mixed, lanes, columns))
    pieces["query"], pieces["key"], pieces["value"], row = merged(
        *((*weight, 0, weight[0].shape[1]) for weight in (query, key, value)), norms
    )
    pieces["norm"] = lax.all_gather(row, "width", axis=0, tiled=True)
    where = {
        "mixed_head": ("mixed", 0, columns, 0),
        "mixed_rest": ("mixed", 0, columns, lanes),
        "query": ("query", 1, rows, 0),
        "norm": ("norm", 0, pieces["norm"].shape[0], 0),
        "key": ("key", 1, rows, 0),
        "value": ("value", 1, rows, 0),
    }
    plan = hops(count)
    outs = {}
    held = {name: {"a0": piece, "b0": piece} for name, piece in pieces.items()}
    arrived = {name: [(*where[name], 0, piece)] for name, piece in pieces.items()}
    for k, parts in enumerate(groups(count), start=1):
        for hop, source, pairs, offset in plan:
            if int(hop[1:]) == k:
                for name in chunk_names:
                    held[name][hop] = lax.ppermute(held[name][source], "shard", pairs)
                    arrived[name].append((*where[name], offset, held[name][hop]))
        for part in parts:
            place(outs, [move for name in part for move in arrived[name]], count)
        arrived = {name: [] for name in chunk_names}
    used = norms[0].size // lanes
    serve_norm = outs["norm"].reshape(-1, row.shape[0], lanes)[:, :used].reshape(-1)
    return outs["query"], outs["key"], outs["value"], outs["mixed"], serve_norm


def by_gather(count, query, key, value, mixed, norms):
    finals = []
    for axis, (w, low, high) in ((0, query), (0, key), (0, value), (1, mixed)):
        result = w.astype(jnp.float32) + mix_rate * jnp.dot(
            low, high, preferred_element_type=jnp.float32
        )
        narrow = result.astype(jnp.bfloat16)
        finals.append(lax.all_gather(narrow, "shard", axis=axis, tiled=True).T)
    norm = (norms[0] + norms[1]).astype(jnp.bfloat16)
    serve_norm = lax.all_gather(norm, ("shard", "width"), axis=0, tiled=True)
    return *finals, serve_norm


def on_device(form, count, *args):
    weights = [args[3 * j : 3 * j + 3] for j in range(4)]
    return form(count, *weights, args[12:])


def solution(mesh):
    column_cut = (P(("shift", "shard"), "width"), P(("shift", "shard"), None), P("shift", "width"))
    row_cut = (P(("shift", "width"), "shard"), P(("shift", "width"), None), P("shift", "shard"))
    norm = P(("shift", "shard", "width"))
    count = mesh.shape["shard"]

    def step(*args):
        rows = args[0].shape[0] // (mesh.shape["shift"] * count)
        columns = args[9].shape[1] // count
        narrow = [args[j].shape[1] // mesh.shape["width"] for j in (0, 3, 6)]
        gains = args[12].shape[0] // (mesh.shape["shift"] * count * mesh.shape["width"])
        aligned = all(size % (2 * lanes) == 0 for size in (rows, columns, *narrow, gains))
        line = count > 2 and aligned
        program = jax.shard_map(
            functools.partial(on_device, by_line if line else by_gather, count),
            mesh=mesh,
            in_specs=(*column_cut, *column_cut, *column_cut, *row_cut, norm, norm),
            out_specs=(
                P(("shift", "width"), None),
                P(("shift", "width"), None),
                P(("shift", "width"), None),
                P("shift", "width"),
                P("shift"),
            ),
            check_vma=False,
        )
        return program(*args)

    return step
```

time: 266 us -> 239 us (0.90)
  waiting for transfers between devices: 203 us -> 184 us
  Pallas kernels: 21 us -> 12.6 us
    ppermute x30, waiting for transfers between devices: 203 us -> 184 us  [by_line(): held[name][hop] = lax.ppermute(held[name][source], 'shard', pairs)]
    pallas_call x24 -> x8, Pallas kernels: 21 us -> 12.6 us  [the longest x5 6.94 us: place(): pl.pallas_call(functools.partial(place_body, count, moves, len(arrays) +...]
  transfers between devices with their start and end apart: 30 -> 30, of which waited for: 9 -> 10; matrix products, arithmetic and copies ran while one was open for 0% -> 0% of each run, Pallas kernels for 7% -> 4%
where the time goes in v2:
time: 239 us; the launch traced here: 238 us
  waiting for transfers between devices  184 us (77%)
  starting transfers between devices  36.1 us (15%)
  Pallas kernels  12.6 us (5%)
    ppermute x30, waiting for transfers between devices, by_line(): held[name][hop] = lax.ppermute(held[name][source], 'shard', pairs)  184 us
    ppermute x30, starting transfers between devices, by_line(): held[name][hop] = lax.ppermute(held[name][source], 'shard', pairs)  36.1 us
    pallas_call x5, Pallas kernels, place(): pl.pallas_call(functools.partial(place_body, count, moves, len(arrays) +...  6.94 us
    pallas_call x3, Pallas kernels, merged(): pl.pallas_call(functools.partial(merge_body, spans), in_specs=specs, out_...  5.67 us
  transfers between devices with their start and end apart: 30, of which 10 were waited for; matrix products, arithmetic and copies ran while one was open for 0% of the time, Pallas kernels for 4%

profile of v2, /device:TPU:0, one launch (start us, length us, event | category | flops | bytes accessed | tf_op | source)
XLA Modules:
  0.0 237.8 jit_solution(2595597385585863299)
XLA Ops:
  2.0 2.7 %shard_map.175 = (bf16[1024,512]{1,0:T(8,128)(2,1)S(1)}, bf16[256,512]{1,0:T(8,128)(2,1)S(1)}, bf16[256,512]{1,0:T(8,128)(2,1)S(1)}, bf16[8,128]{1,0:T(8,128)(2,1)S(1)}) custom-call(bf16[512,1024]{1,0:T(8,128)(2,1)} %refs_0_.5, bf16[16,512]{1,0:T(8,128)(2,1)} %bitcast.13, bf16[16,1024]{1,0:T(8,128)(2,1)} %refs_2_.5, bf16[512,256]{1,0:T(8,128)(2,1)} %refs_3_.1, ...), custom_call_target="tpu_custom_call" | custom-call | tf_op jit(solution)/shard_map/pallas_call | solution.py:100
  4.7 3.1 %collective-permute-start.6 = (bf16[1024,512]{1,0:T(8,128)(2,1)S(1)}, bf16[1024,512]{1,0:T(8,128)(2,1)S(1)}, u32[]{:S(2)}, u32[]{:S(2)}) collective-permute-start(bf16[1024,512]{1,0:T(8,128)(2,1)S(1)} %get-tuple-element.22.refs_6_), channel_id=1, source_target_pairs={{8,0},{0,8},{24,16},{16,24},{9,1},{1,9},{25,17},{17,25},{10,2},{2,... | collective-permute-start | bytes 3145736 | tf_op jit(solution)/shard_map/ppermute | solution.py:199
  8.5 4.4 %collective-permute-start.22 = (bf16[256,512]{1,0:T(8,128)(2,1)S(1)}, bf16[256,512]{1,0:T(8,128)(2,1)S(1)}, u32[]{:S(2)}, u32[]{:S(2)}) collective-permute-start(bf16[256,512]{1,0:T(8,128)(2,1)S(1)} %get-tuple-element.24.refs_12_), channel_id=1, source_target_pairs={{8,0},{0,8},{24,16},{16,24},{9,1},{1,9},{25,17},{17,25},{10,2},{2,... | collective-permute-start | bytes 786440 | tf_op jit(solution)/shard_map/ppermute | solution.py:199
  12.9 1.8 all_gather.3.refs_9_
  15.5 21.2 %collective-permute-done.9.refs_10_ = bf16[16,128]{1,0:T(8,128)(2,1)S(1)} collective-permute-done((bf16[16,128]{1,0:T(8,128)(2,1)S(1)}, bf16[16,128]{1,0:T(8,128)(2,1)S(1)}, u32[]{:S(2)}, u32[]{:S(2)}) %collective-permute-start.9) | collective-permute-done | bytes 4128 | tf_op jit(solution)/shard_map/ppermute | solution.py:199
  37.4 1.3 collective-permute-start.19
  39.3 5.4 %collective-permute-done.19.refs_6_ = bf16[16,128]{1,0:T(8,128)(2,1)S(1)} collective-permute-done((bf16[16,128]{1,0:T(8,128)(2,1)S(1)}, bf16[16,128]{1,0:T(8,128)(2,1)S(1)}, u32[]{:S(2)}, u32[]{:S(2)}) %collective-permute-start.19) | collective-permute-done | bytes 4128 | tf_op jit(solution)/shard_map/ppermute | solution.py:199
  44.8 2.7 %collective-permute-start.26 = (bf16[256,512]{1,0:T(8,128)(2,1)S(1)}, bf16[256,512]{1,0:T(8,128)(2,1)S(1)}, u32[]{:S(2)}, u32[]{:S(2)}) collective-permute-start(bf16[256,512]{1,0:T(8,128)(2,1)S(1)} %get-tuple-element.25.refs_15_), channel_id=1, source_target_pairs={{8,0},{0,8},{24,16},{16,24},{9,1},{1,9},{25,17},{17,25},{10,2},{2,... | collective-permute-start | bytes 786440 | tf_op jit(solution)/shard_map/ppermute | solution.py:199
  47.5 1.3 shard_map.173.refs_0_
  48.8 1.7 shard_map.174.refs_3_
  50.6 2.1 collective-permute-start.3
  55.3 4.9 %collective-permute-done.refs_1_ = bf16[128,1024]{1,0:T(8,128)(2,1)S(1)} collective-permute-done((bf16[128,1024]{1,0:T(8,128)(2,1)S(1)}, bf16[128,1024]{1,0:T(8,128)(2,1)S(1)}, u32[]{:S(2)}, u32[]{:S(2)}) %collective-permute-start) | collective-permute-done | bytes 262176 | tf_op jit(solution)/shard_map/ppermute | solution.py:199
  63.1 1.3 collective-permute-start.21
  64.4 9.6 %collective-permute-done.3.refs_4_ = bf16[384,1024]{1,0:T(8,128)(2,1)S(1)} collective-permute-done((bf16[384,1024]{1,0:T(8,128)(2,1)S(1)}, bf16[384,1024]{1,0:T(8,128)(2,1)S(1)}, u32[]{:S(2)}, u32[]{:S(2)}) %collective-permute-start.3) | collective-permute-done | bytes 786464 | tf_op jit(solution)/shard_map/ppermute | solution.py:199
  74.7 53.7 %collective-permute-done.21.refs_8_ = bf16[256,512]{1,0:T(8,128)(2,1)S(1)} collective-permute-done((bf16[256,512]{1,0:T(8,128)(2,1)S(1)}, bf16[256,512]{1,0:T(8,128)(2,1)S(1)}, u32[]{:S(2)}, u32[]{:S(2)}) %collective-permute-start.21) | collective-permute-done | bytes 262176 | tf_op jit(solution)/shard_map/ppermute | solution.py:199
  128.3 1.3 collective-permute-start.25
  129.6 1.3 collective-permute-start.17
  130.9 8.5 %collective-permute-done.25.refs_10_ = bf16[256,512]{1,0:T(8,128)(2,1)S(1)} collective-permute-done((bf16[256,512]{1,0:T(8,128)(2,1)S(1)}, bf16[256,512]{1,0:T(8,128)(2,1)S(1)}, u32[]{:S(2)}, u32[]{:S(2)}) %collective-permute-start.25) | collective-permute-done | bytes 262176 | tf_op jit(solution)/shard_map/ppermute | solution.py:199
  140.1 1.3 collective-permute-start.15
  141.4 1.3 collective-permute-start.8
  142.7 1.3 collective-permute-start.13
  144.0 1.3 collective-permute-start.5
  145.3 61.5 %collective-permute-done.13.refs_0_ = bf16[128,1024]{1,0:T(8,128)(2,1)S(1)} collective-permute-done((bf16[128,1024]{1,0:T(8,128)(2,1)S(1)}, bf16[128,1024]{1,0:T(8,128)(2,1)S(1)}, u32[]{:S(2)}, u32[]{:S(2)}) %collective-permute-start.13) | collective-permute-done | bytes 262176 | tf_op jit(solution)/shard_map/ppermute | solution.py:199
  206.8 1.3 collective-permute-start.28
  208.1 16.6 %collective-permute-done.28.refs_0_ = bf16[256,512]{1,0:T(8,128)(2,1)S(1)} collective-permute-done((bf16[256,512]{1,0:T(8,128)(2,1)S(1)}, bf16[256,512]{1,0:T(8,128)(2,1)S(1)}, u32[]{:S(2)}, u32[]{:S(2)}) %collective-permute-start.28) | collective-permute-done | bytes 262176 | tf_op jit(solution)/shard_map/ppermute | solution.py:199
  224.7 1.3 collective-permute-start.29
  226.0 1.3 collective-permute-start.2
  227.3 1.3 collective-permute-start.11
  228.6 2.5 %shard_map.176 = (bf16[2048,1024]{1,0:T(8,128)(2,1)}, bf16[1024,2048]{1,0:T(8,128)(2,1)}, bf16[64,128]{1,0:T(8,128)(2,1)S(1)}, bf16[256,2048]{1,0:T(8,128)(2,1)}, bf16[256,2048]{1,0:T(8,128)(2,1)}) custom-call(bf16[128,1024]{1,0:T(8,128)(2,1)S(1)} %shard_map.173.refs_0_, bf16[128,1024]{1,0:T(8,128)(2,1)S(1)} %collective-permute-done.refs_1_, ...), custom_call_target="tpu_custom_call" | custom-call | tf_op jit(solution)/shard_map/pallas_call | solution.py:138
  231.1 1.6 shard_map.177
  234.2 1.6 collective-permute-done.11.refs_3_
  235.8 1.4 shard_map.178
  (42 shorter events, 13.0 us)
Async XLA Ops:
  0.6 0.7 copy-start
  1.3 0.7 copy-start.1
  4.7 56.2 %collective-permute-start.6 = (bf16[1024,512]{1,0:T(8,128)(2,1)S(1)}, bf16[1024,512]{1,0:T(8,128)(2,1)S(1)}, u32[]{:S(2)}, u32[]{:S(2)}) collective-permute-start(bf16[1024,512]{1,0:T(8,128)(2,1)S(1)} %get-tuple-element.22.refs_6_), channel_id=1, source_target_pairs={{8,0},{0,8},{24,16},{16,24},{9,1},{1,9},{25,17},{17,25},{10,2},{2,... | collective-permute-start | bytes 3145736 | tf_op jit(solution)/shard_map/ppermute | solution.py:199
  7.8 40.9 %collective-permute-start.20 = (bf16[256,512]{1,0:T(8,128)(2,1)S(1)}, bf16[256,512]{1,0:T(8,128)(2,1)S(1)}, u32[]{:S(2)}, u32[]{:S(2)}) collective-permute-start(bf16[256,512]{1,0:T(8,128)(2,1)S(1)} %get-tuple-element.24.refs_12_), channel_id=1, source_target_pairs={{16,8},{8,16},{17,9},{9,17},{18,10},{10,18},{19,11},{11,19},{20,12... | collective-permute-start | bytes 786440 | tf_op jit(solution)/shard_map/ppermute | solution.py:199
  8.5 42.1 %collective-permute-start.22 = (bf16[256,512]{1,0:T(8,128)(2,1)S(1)}, bf16[256,512]{1,0:T(8,128)(2,1)S(1)}, u32[]{:S(2)}, u32[]{:S(2)}) collective-permute-start(bf16[256,512]{1,0:T(8,128)(2,1)S(1)} %get-tuple-element.24.refs_12_), channel_id=1, source_target_pairs={{8,0},{0,8},{24,16},{16,24},{9,1},{1,9},{25,17},{17,25},{10,2},{2,... | collective-permute-start | bytes 786440 | tf_op jit(solution)/shard_map/ppermute | solution.py:199
  14.8 21.9 %collective-permute-start.9 = (bf16[16,128]{1,0:T(8,128)(2,1)S(1)}, bf16[16,128]{1,0:T(8,128)(2,1)S(1)}, u32[]{:S(2)}, u32[]{:S(2)}) collective-permute-start(bf16[16,128]{1,0:T(8,128)(2,1)S(1)} %all_gather.3.refs_9_), channel_id=1, source_target_pairs={{8,0},{0,8},{24,16},{16,24},{9,1},{1,9},{25,17},{17,25},{10,2},{2,... | collective-permute-start | bytes 12296 | tf_op jit(solution)/shard_map/ppermute | solution.py:199
  14.8 22.5 %collective-permute-start.18 = (bf16[16,128]{1,0:T(8,128)(2,1)S(1)}, bf16[16,128]{1,0:T(8,128)(2,1)S(1)}, u32[]{:S(2)}, u32[]{:S(2)}) collective-permute-start(bf16[16,128]{1,0:T(8,128)(2,1)S(1)} %all_gather.3.refs_9_), channel_id=1, source_target_pairs={{16,8},{8,16},{17,9},{9,17},{18,10},{10,18},{19,11},{11,19},{20,12... | collective-permute-start | bytes 12296 | tf_op jit(solution)/shard_map/ppermute | solution.py:199
  36.7 2.0 collective-permute-start.10
  37.4 7.4 %collective-permute-start.19 = (bf16[16,128]{1,0:T(8,128)(2,1)S(1)}, bf16[16,128]{1,0:T(8,128)(2,1)S(1)}, u32[]{:S(2)}, u32[]{:S(2)}) collective-permute-start(bf16[16,128]{1,0:T(8,128)(2,1)S(1)} %collective-permute-done.18.refs_11_), channel_id=1, source_target_pairs={{8,0},{16,24},{9,1},{17,25},{10,2},{18,26},{11,3},{19,27},{12,4},{... | collective-permute-start | bytes 12296 | tf_op jit(solution)/shard_map/ppermute | solution.py:199
  38.7 14.0 %collective-permute-start.24 = (bf16[256,512]{1,0:T(8,128)(2,1)S(1)}, bf16[256,512]{1,0:T(8,128)(2,1)S(1)}, u32[]{:S(2)}, u32[]{:S(2)}) collective-permute-start(bf16[256,512]{1,0:T(8,128)(2,1)S(1)} %get-tuple-element.25.refs_15_), channel_id=1, source_target_pairs={{16,8},{8,16},{17,9},{9,17},{18,10},{10,18},{19,11},{11,19},{20,12... | collective-permute-start | bytes 786440 | tf_op jit(solution)/shard_map/ppermute | solution.py:199
  44.8 9.9 %collective-permute-start.26 = (bf16[256,512]{1,0:T(8,128)(2,1)S(1)}, bf16[256,512]{1,0:T(8,128)(2,1)S(1)}, u32[]{:S(2)}, u32[]{:S(2)}) collective-permute-start(bf16[256,512]{1,0:T(8,128)(2,1)S(1)} %get-tuple-element.25.refs_15_), channel_id=1, source_target_pairs={{8,0},{0,8},{24,16},{16,24},{9,1},{1,9},{25,17},{17,25},{10,2},{2,... | collective-permute-start | bytes 786440 | tf_op jit(solution)/shard_map/ppermute | solution.py:199
  48.8 11.5 %collective-permute-start = (bf16[128,1024]{1,0:T(8,128)(2,1)S(1)}, bf16[128,1024]{1,0:T(8,128)(2,1)S(1)}, u32[]{:S(2)}, u32[]{:S(2)}) collective-permute-start(bf16[128,1024]{1,0:T(8,128)(2,1)S(1)} %shard_map.173.refs_0_), channel_id=1, source_target_pairs={{8,0},{0,8},{24,16},{16,24},{9,1},{1,9},{25,17},{17,25},{10,2},{2,... | collective-permute-start | bytes 786440 | tf_op jit(solution)/shard_map/ppermute | solution.py:199
  50.6 23.4 %collective-permute-start.3 = (bf16[384,1024]{1,0:T(8,128)(2,1)S(1)}, bf16[384,1024]{1,0:T(8,128)(2,1)S(1)}, u32[]{:S(2)}, u32[]{:S(2)}) collective-permute-start(bf16[384,1024]{1,0:T(8,128)(2,1)S(1)} %shard_map.174.refs_3_), channel_id=1, source_target_pairs={{8,0},{0,8},{24,16},{16,24},{9,1},{1,9},{25,17},{17,25},{10,2},{2,... | collective-permute-start | bytes 2359304 | tf_op jit(solution)/shard_map/ppermute | solution.py:199
  52.6 77.0 %collective-permute-start.16 = (bf16[1024,512]{1,0:T(8,128)(2,1)S(1)}, bf16[1024,512]{1,0:T(8,128)(2,1)S(1)}, u32[]{:S(2)}, u32[]{:S(2)}) collective-permute-start(bf16[1024,512]{1,0:T(8,128)(2,1)S(1)} %get-tuple-element.22.refs_6_), channel_id=1, source_target_pairs={{16,8},{8,16},{17,9},{9,17},{18,10},{10,18},{19,11},{11,19},{20,12... | collective-permute-start | bytes 3145736 | tf_op jit(solution)/shard_map/ppermute | solution.py:199
  54.6 7.0 %collective-permute-start.12 = (bf16[128,1024]{1,0:T(8,128)(2,1)S(1)}, bf16[128,1024]{1,0:T(8,128)(2,1)S(1)}, u32[]{:S(2)}, u32[]{:S(2)}) collective-permute-start(bf16[128,1024]{1,0:T(8,128)(2,1)S(1)} %shard_map.173.refs_0_), channel_id=1, source_target_pairs={{16,8},{8,16},{17,9},{9,17},{18,10},{10,18},{19,11},{11,19},{20,12... | collective-permute-start | bytes 786440 | tf_op jit(solution)/shard_map/ppermute | solution.py:199
  60.2 2.1 collective-permute-start.23
  60.9 80.5 %collective-permute-start.7 = (bf16[1024,512]{1,0:T(8,128)(2,1)S(1)}, bf16[1024,512]{1,0:T(8,128)(2,1)S(1)}, u32[]{:S(2)}, u32[]{:S(2)}) collective-permute-start(bf16[1024,512]{1,0:T(8,128)(2,1)S(1)} %collective-permute-done.6.refs_7_), channel_id=1, source_target_pairs={{16,8},{8,16},{17,9},{9,17},{18,10},{10,18},{19,11},{11,19},{20,12... | collective-permute-start | bytes 3145736 | tf_op jit(solution)/shard_map/ppermute | solution.py:199
  61.7 1.4 collective-permute-start.27
  62.4 77.7 %collective-permute-start.14 = (bf16[384,1024]{1,0:T(8,128)(2,1)S(1)}, bf16[384,1024]{1,0:T(8,128)(2,1)S(1)}, u32[]{:S(2)}, u32[]{:S(2)}) collective-permute-start(bf16[384,1024]{1,0:T(8,128)(2,1)S(1)} %shard_map.174.refs_3_), channel_id=1, source_target_pairs={{16,8},{8,16},{17,9},{9,17},{18,10},{10,18},{19,11},{11,19},{20,12... | collective-permute-start | bytes 2359304 | tf_op jit(solution)/shard_map/ppermute | solution.py:199
  63.1 65.2 %collective-permute-start.21 = (bf16[256,512]{1,0:T(8,128)(2,1)S(1)}, bf16[256,512]{1,0:T(8,128)(2,1)S(1)}, u32[]{:S(2)}, u32[]{:S(2)}) collective-permute-start(bf16[256,512]{1,0:T(8,128)(2,1)S(1)} %collective-permute-done.20.refs_14_), channel_id=1, source_target_pairs={{8,0},{16,24},{9,1},{17,25},{10,2},{18,26},{11,3},{19,27},{12,4},{... | collective-permute-start | bytes 786440 | tf_op jit(solution)/shard_map/ppermute | solution.py:199
  74.0 70.0 %collective-permute-start.4 = (bf16[384,1024]{1,0:T(8,128)(2,1)S(1)}, bf16[384,1024]{1,0:T(8,128)(2,1)S(1)}, u32[]{:S(2)}, u32[]{:S(2)}) collective-permute-start(bf16[384,1024]{1,0:T(8,128)(2,1)S(1)} %collective-permute-done.3.refs_4_), channel_id=1, source_target_pairs={{16,8},{8,16},{17,9},{9,17},{18,10},{10,18},{19,11},{11,19},{20,12... | collective-permute-start | bytes 2359304 | tf_op jit(solution)/shard_map/ppermute | solution.py:199
  128.3 11.1 %collective-permute-start.25 = (bf16[256,512]{1,0:T(8,128)(2,1)S(1)}, bf16[256,512]{1,0:T(8,128)(2,1)S(1)}, u32[]{:S(2)}, u32[]{:S(2)}) collective-permute-start(bf16[256,512]{1,0:T(8,128)(2,1)S(1)} %collective-permute-done.24.refs_17_), channel_id=1, source_target_pairs={{8,0},{16,24},{9,1},{17,25},{10,2},{18,26},{11,3},{19,27},{12,4},{... | collective-permute-start | bytes 786440 | tf_op jit(solution)/shard_map/ppermute | solution.py:199
  129.6 97.7 %collective-permute-start.17 = (bf16[1024,512]{1,0:T(8,128)(2,1)S(1)}, bf16[1024,512]{1,0:T(8,128)(2,1)S(1)}, u32[]{:S(2)}, u32[]{:S(2)}) collective-permute-start(bf16[1024,512]{1,0:T(8,128)(2,1)S(1)} %collective-permute-done.16.refs_8_), channel_id=1, source_target_pairs={{8,0},{16,24},{9,1},{17,25},{10,2},{18,26},{11,3},{19,27},{12,4},{... | collective-permute-start | bytes 3145736 | tf_op jit(solution)/shard_map/ppermute | solution.py:199
  139.4 3.3 %collective-permute-start.1 = (bf16[128,1024]{1,0:T(8,128)(2,1)S(1)}, bf16[128,1024]{1,0:T(8,128)(2,1)S(1)}, u32[]{:S(2)}, u32[]{:S(2)}) collective-permute-start(bf16[128,1024]{1,0:T(8,128)(2,1)S(1)} %collective-permute-done.refs_1_), channel_id=1, source_target_pairs={{16,8},{8,16},{17,9},{9,17},{18,10},{10,18},{19,11},{11,19},{20,12... | collective-permute-start | bytes 786440 | tf_op jit(solution)/shard_map/ppermute | solution.py:199
  140.1 85.9 %collective-permute-start.15 = (bf16[384,1024]{1,0:T(8,128)(2,1)S(1)}, bf16[384,1024]{1,0:T(8,128)(2,1)S(1)}, u32[]{:S(2)}, u32[]{:S(2)}) collective-permute-start(bf16[384,1024]{1,0:T(8,128)(2,1)S(1)} %collective-permute-done.14.refs_5_), channel_id=1, source_target_pairs={{8,0},{16,24},{9,1},{17,25},{10,2},{18,26},{11,3},{19,27},{12,4},{... | collective-permute-start | bytes 2359304 | tf_op jit(solution)/shard_map/ppermute | solution.py:199
  141.4 94.4 %collective-permute-start.8 = (bf16[1024,512]{1,0:T(8,128)(2,1)S(1)}, bf16[1024,512]{1,0:T(8,128)(2,1)S(1)}, u32[]{:S(2)}, u32[]{:S(2)}) collective-permute-start(bf16[1024,512]{1,0:T(8,128)(2,1)S(1)} %collective-permute-done.7.refs_5_), channel_id=1, source_target_pairs={{8,0},{16,24},{9,1},{17,25},{10,2},{18,26},{11,3},{19,27},{12,4},{... | collective-permute-start | bytes 3145736 | tf_op jit(solution)/shard_map/ppermute | solution.py:199
  142.7 64.1 %collective-permute-start.13 = (bf16[128,1024]{1,0:T(8,128)(2,1)S(1)}, bf16[128,1024]{1,0:T(8,128)(2,1)S(1)}, u32[]{:S(2)}, u32[]{:S(2)}) collective-permute-start(bf16[128,1024]{1,0:T(8,128)(2,1)S(1)} %collective-permute-done.12.refs_2_), channel_id=1, source_target_pairs={{8,0},{16,24},{9,1},{17,25},{10,2},{18,26},{11,3},{19,27},{12,4},{... | collective-permute-start | bytes 786440 | tf_op jit(solution)/shard_map/ppermute | solution.py:199
  144.0 91.8 %collective-permute-start.5 = (bf16[384,1024]{1,0:T(8,128)(2,1)S(1)}, bf16[384,1024]{1,0:T(8,128)(2,1)S(1)}, u32[]{:S(2)}, u32[]{:S(2)}) collective-permute-start(bf16[384,1024]{1,0:T(8,128)(2,1)S(1)} %collective-permute-done.4.refs_3_), channel_id=1, source_target_pairs={{8,0},{16,24},{9,1},{17,25},{10,2},{18,26},{11,3},{19,27},{12,4},{... | collective-permute-start | bytes 2359304 | tf_op jit(solution)/shard_map/ppermute | solution.py:199
  206.8 17.9 %collective-permute-start.28 = (bf16[256,512]{1,0:T(8,128)(2,1)S(1)}, bf16[256,512]{1,0:T(8,128)(2,1)S(1)}, u32[]{:S(2)}, u32[]{:S(2)}) collective-permute-start(bf16[256,512]{1,0:T(8,128)(2,1)S(1)} %collective-permute-done.23.refs_9_), channel_id=1, source_target_pairs={{8,0},{16,24},{9,1},{17,25},{10,2},{18,26},{11,3},{19,27},{12,4},{... | collective-permute-start | bytes 786440 | tf_op jit(solution)/shard_map/ppermute | solution.py:199
  224.7 8.8 %collective-permute-start.29 = (bf16[256,512]{1,0:T(8,128)(2,1)S(1)}, bf16[256,512]{1,0:T(8,128)(2,1)S(1)}, u32[]{:S(2)}, u32[]{:S(2)}) collective-permute-start(bf16[256,512]{1,0:T(8,128)(2,1)S(1)} %collective-permute-done.27.refs_11_), channel_id=1, source_target_pairs={{8,0},{16,24},{9,1},{17,25},{10,2},{18,26},{11,3},{19,27},{12,4},{... | collective-permute-start | bytes 786440 | tf_op jit(solution)/shard_map/ppermute | solution.py:199
  226.0 9.8 %collective-permute-start.2 = (bf16[128,1024]{1,0:T(8,128)(2,1)S(1)}, bf16[128,1024]{1,0:T(8,128)(2,1)S(1)}, u32[]{:S(2)}, u32[]{:S(2)}) collective-permute-start(bf16[128,1024]{1,0:T(8,128)(2,1)S(1)} %collective-permute-done.1.refs_1_), channel_id=1, source_target_pairs={{8,0},{16,24},{9,1},{17,25},{10,2},{18,26},{11,3},{19,27},{12,4},{... | collective-permute-start | bytes 786440 | tf_op jit(solution)/shard_map/ppermute | solution.py:199
  227.3 8.5 %collective-permute-start.11 = (bf16[16,128]{1,0:T(8,128)(2,1)S(1)}, bf16[16,128]{1,0:T(8,128)(2,1)S(1)}, u32[]{:S(2)}, u32[]{:S(2)}) collective-permute-start(bf16[16,128]{1,0:T(8,128)(2,1)S(1)} %collective-permute-done.10.refs_7_), channel_id=1, source_target_pairs={{8,0},{16,24},{9,1},{17,25},{10,2},{18,26},{11,3},{19,27},{12,4},{... | collective-permute-start | bytes 12296 | tf_op jit(solution)/shard_map/ppermute | solution.py:199

commit v3 on v2

--- a/solution.py
+++ b/solution.py
@@ -163,6 +163,34 @@
     return plan
 
 
+def pick_body(first_ref, second_ref, out_ref):
+    leads = lax.axis_index("width") == 0
+
+    @pl.when(leads)
+    def _():
+        out_ref[...] = first_ref[...]
+
+    @pl.when(jnp.logical_not(leads))
+    def _():
+        out_ref[...] = second_ref[...]
+
+
+def staggered(piece, pairs, cores):
+    def of(chosen):
+        return [(i * cores + core, j * cores + core) for i, j in pairs for core in chosen]
+
+    first = lax.ppermute(piece, ("shard", "width"), of(range(1)))
+    second = lax.ppermute(piece, ("shard", "width"), of(range(1, cores)))
+    return pl.pallas_call(
+        pick_body,
+        in_specs=[in_vmem] * 2,
+        out_specs=in_vmem,
+        out_shape=jax.ShapeDtypeStruct(piece.shape, piece.dtype),
+        compiler_params=pltpu.CompilerParams(vmem_limit_bytes=4 << 20),
+    )(first, second)
+
+
+head = 2 * lanes
 chunk_names = ("mixed_head", "mixed_rest", "query", "norm", "key", "value")
 
 
@@ -171,18 +199,18 @@
     return [whole] * (count - 2) + [(chunk_names[:-2], chunk_names[-2:-1], chunk_names[-1:])]
 
 
-def by_line(count, query, key, value, mixed, norms):
+def by_line(count, cores, query, key, value, mixed, norms):
     rows, columns = query[0].shape[0], mixed[0].shape[1]
     pieces = {}
-    (pieces["mixed_head"],) = merged((*mixed, 0, lanes))
-    (pieces["mixed_rest"],) = merged((*mixed, lanes, columns))
+    (pieces["mixed_head"],) = merged((*mixed, 0, head))
+    (pieces["mixed_rest"],) = merged((*mixed, head, columns))
     pieces["query"], pieces["key"], pieces["value"], row = merged(
         *((*weight, 0, weight[0].shape[1]) for weight in (query, key, value)), norms
     )
     pieces["norm"] = lax.all_gather(row, "width", axis=0, tiled=True)
     where = {
         "mixed_head": ("mixed", 0, columns, 0),
-        "mixed_rest": ("mixed", 0, columns, lanes),
+        "mixed_rest": ("mixed", 0, columns, head),
         "query": ("query", 1, rows, 0),
         "norm": ("norm", 0, pieces["norm"].shape[0], 0),
         "key": ("key", 1, rows, 0),
@@ -196,7 +224,10 @@
         for hop, source, pairs, offset in plan:
             if int(hop[1:]) == k:
                 for name in chunk_names:
-                    held[name][hop] = lax.ppermute(held[name][source], "shard", pairs)
+                    if (hop, name) == ("a1", "mixed_head"):
+                        held[name][hop] = staggered(held[name][source], pairs, cores)
+                    else:
+                        held[name][hop] = lax.ppermute(held[name][source], "shard", pairs)
                     arrived[name].append((*where[name], offset, held[name][hop]))
         for part in parts:
             place(outs, [move for name in part for move in arrived[name]], count)
@@ -206,7 +237,7 @@
     return outs["query"], outs["key"], outs["value"], outs["mixed"], serve_norm
 
 
-def by_gather(count, query, key, value, mixed, norms):
+def by_gather(count, cores, query, key, value, mixed, norms):
     finals = []
     for axis, (w, low, high) in ((0, query), (0, key), (0, value), (1, mixed)):
         result = w.astype(jnp.float32) + mix_rate * jnp.dot(
@@ -219,26 +250,26 @@
     return *finals, serve_norm
 
 
-def on_device(form, count, *args):
+def on_device(form, count, cores, *args):
     weights = [args[3 * j : 3 * j + 3] for j in range(4)]
-    return form(count, *weights, args[12:])
+    return form(count, cores, *weights, args[12:])
 
 
 def solution(mesh):
     column_cut = (P(("shift", "shard"), "width"), P(("shift", "shard"), None), P("shift", "width"))
     row_cut = (P(("shift", "width"), "shard"), P(("shift", "width"), None), P("shift", "shard"))
     norm = P(("shift", "shard", "width"))
-    count = mesh.shape["shard"]
+    count, cores = mesh.shape["shard"], mesh.shape["width"]
 
     def step(*args):
         rows = args[0].shape[0] // (mesh.shape["shift"] * count)
         columns = args[9].shape[1] // count
-        narrow = [args[j].shape[1] // mesh.shape["width"] for j in (0, 3, 6)]
-        gains = args[12].shape[0] // (mesh.shape["shift"] * count * mesh.shape["width"])
+        narrow = [args[j].shape[1] // cores for j in (0, 3, 6)]
+        gains = args[12].shape[0] // (mesh.shape["shift"] * count * cores)
         aligned = all(size % (2 * lanes) == 0 for size in (rows, columns, *narrow, gains))
-        line = count > 2 and aligned
+        line = count > 2 and cores > 1 and aligned and columns > head
         program = jax.shard_map(
-            functools.partial(on_device, by_line if line else by_gather, count),
+            functools.partial(on_device, by_line if line else by_gather, count, cores),
             mesh=mesh,
             in_specs=(*column_cut, *column_cut, *column_cut, *row_cut, norm, norm),
             out_specs=(

time: 239 us -> 241 us (level)
  starting transfers between devices: 36.1 us -> 43.4 us
  waiting for transfers between devices: 184 us -> 180 us
    ppermute x30 -> x29, starting transfers between devices: 36.1 us -> 40.8 us  [by_line(): held[name][hop] = lax.ppermute(held[name][source], 'shard', pairs)]
    ppermute x30 -> x29, waiting for transfers between devices: 184 us -> 180 us  [by_line(): held[name][hop] = lax.ppermute(held[name][source], 'shard', pairs)]
    ppermute x0 -> x2, starting transfers between devices: none -> 2.62 us  [the longest x1 1.92 us: staggered(): first = lax.ppermute(piece, ('shard', 'width'), of(range(1)))]
  transfers between devices with their start and end apart: 30 -> 31, of which waited for: 10 -> 10; matrix products, arithmetic and copies ran while one was open for 0% -> 0% of each run, Pallas kernels for 4% -> 4%
where the time goes in v3:
time: 241 us
  waiting for transfers between devices  180 us (75%)
  starting transfers between devices  43.4 us (18%)
  Pallas kernels  12.6 us (5%)
    ppermute x29, waiting for transfers between devices, by_line(): held[name][hop] = lax.ppermute(held[name][source], 'shard', pairs)  180 us
    ppermute x29, starting transfers between devices, by_line(): held[name][hop] = lax.ppermute(held[name][source], 'shard', pairs)  40.8 us
    pallas_call x5, Pallas kernels, place(): pl.pallas_call(functools.partial(place_body, count, moves, len(arrays) +...  6.92 us
    pallas_call x3, Pallas kernels, merged(): pl.pallas_call(functools.partial(merge_body, spans), in_specs=specs, out_...  5.58 us
  transfers between devices with their start and end apart: 31, of which 10 were waited for; matrix products, arithmetic and copies ran while one was open for 0% of the time, Pallas kernels for 4%

profile of v3, /device:TPU:0, one launch (start us, length us, event | category | flops | bytes accessed | tf_op | source)
XLA Modules:
  0.0 240.5 jit_solution(3097056507863876098)
XLA Ops:
  2.0 2.7 %shard_map.176 = (bf16[1024,512]{1,0:T(8,128)(2,1)S(1)}, bf16[256,512]{1,0:T(8,128)(2,1)S(1)}, bf16[256,512]{1,0:T(8,128)(2,1)S(1)}, bf16[8,128]{1,0:T(8,128)(2,1)S(1)}) custom-call(bf16[512,1024]{1,0:T(8,128)(2,1)} %refs_0_.5, bf16[16,512]{1,0:T(8,128)(2,1)} %bitcast.13, bf16[16,1024]{1,0:T(8,128)(2,1)} %refs_2_.5, bf16[512,256]{1,0:T(8,128)(2,1)} %refs_3_.1, ...), custom_call_target="tpu_custom_call" | custom-call | tf_op jit(solution)/shard_map/pallas_call | solution.py:100
  4.7 3.1 %collective-permute-start.7 = (bf16[1024,512]{1,0:T(8,128)(2,1)S(1)}, bf16[1024,512]{1,0:T(8,128)(2,1)S(1)}, u32[]{:S(2)}, u32[]{:S(2)}) collective-permute-start(bf16[1024,512]{1,0:T(8,128)(2,1)S(1)} %get-tuple-element.22.refs_6_), channel_id=1, source_target_pairs={{8,0},{0,8},{24,16},{16,24},{9,1},{1,9},{25,17},{17,25},{10,2},{2,... | collective-permute-start | bytes 3145736 | tf_op jit(solution)/shard_map/ppermute | solution.py:230
  7.8 1.8 all_gather.3.refs_9_
  11.1 20.0 %collective-permute-done.10.refs_10_ = bf16[16,128]{1,0:T(8,128)(2,1)S(1)} collective-permute-done((bf16[16,128]{1,0:T(8,128)(2,1)S(1)}, bf16[16,128]{1,0:T(8,128)(2,1)S(1)}, u32[]{:S(2)}, u32[]{:S(2)}) %collective-permute-start.10) | collective-permute-done | bytes 4128 | tf_op jit(solution)/shard_map/ppermute | solution.py:230
  31.7 1.3 collective-permute-start.20
  33.0 4.6 %collective-permute-start.23 = (bf16[256,512]{1,0:T(8,128)(2,1)S(1)}, bf16[256,512]{1,0:T(8,128)(2,1)S(1)}, u32[]{:S(2)}, u32[]{:S(2)}) collective-permute-start(bf16[256,512]{1,0:T(8,128)(2,1)S(1)} %get-tuple-element.24.refs_12_), channel_id=1, source_target_pairs={{8,0},{0,8},{24,16},{16,24},{9,1},{1,9},{25,17},{17,25},{10,2},{2,... | collective-permute-start | bytes 786440 | tf_op jit(solution)/shard_map/ppermute | solution.py:230
  37.7 1.4 shard_map.173.refs_0_
  39.1 1.9 collective-permute-start
  43.6 3.1 %collective-permute-start.27 = (bf16[256,512]{1,0:T(8,128)(2,1)S(1)}, bf16[256,512]{1,0:T(8,128)(2,1)S(1)}, u32[]{:S(2)}, u32[]{:S(2)}) collective-permute-start(bf16[256,512]{1,0:T(8,128)(2,1)S(1)} %get-tuple-element.25.refs_15_), channel_id=1, source_target_pairs={{8,0},{0,8},{24,16},{16,24},{9,1},{1,9},{25,17},{17,25},{10,2},{2,... | collective-permute-start | bytes 786440 | tf_op jit(solution)/shard_map/ppermute | solution.py:230
  47.4 12.3 %collective-permute-done.27.refs_16_ = bf16[256,512]{1,0:T(8,128)(2,1)S(1)} collective-permute-done((bf16[256,512]{1,0:T(8,128)(2,1)S(1)}, bf16[256,512]{1,0:T(8,128)(2,1)S(1)}, u32[]{:S(2)}, u32[]{:S(2)}) %collective-permute-start.27) | collective-permute-done | bytes 262176 | tf_op jit(solution)/shard_map/ppermute | solution.py:230
  60.4 1.4 shard_map.175.refs_3_
  62.6 6.2 %collective-permute-start.4 = (bf16[256,1024]{1,0:T(8,128)(2,1)S(1)}, bf16[256,1024]{1,0:T(8,128)(2,1)S(1)}, u32[]{:S(2)}, u32[]{:S(2)}) collective-permute-start(bf16[256,1024]{1,0:T(8,128)(2,1)S(1)} %shard_map.175.refs_3_), channel_id=1, source_target_pairs={{8,0},{0,8},{24,16},{16,24},{9,1},{1,9},{25,17},{17,25},{10,2},{2,... | collective-permute-start | bytes 1572872 | tf_op jit(solution)/shard_map/ppermute | solution.py:230
  70.9 8.0 %collective-permute-done.4.refs_4_ = bf16[256,1024]{1,0:T(8,128)(2,1)S(1)} collective-permute-done((bf16[256,1024]{1,0:T(8,128)(2,1)S(1)}, bf16[256,1024]{1,0:T(8,128)(2,1)S(1)}, u32[]{:S(2)}, u32[]{:S(2)}) %collective-permute-start.4) | collective-permute-done | bytes 524320 | tf_op jit(solution)/shard_map/ppermute | solution.py:230
  78.9 1.3 collective-permute-start.22
  81.0 1.3 collective-permute-start.26
  82.3 28.6 %collective-permute-done.22.refs_8_ = bf16[256,512]{1,0:T(8,128)(2,1)S(1)} collective-permute-done((bf16[256,512]{1,0:T(8,128)(2,1)S(1)}, bf16[256,512]{1,0:T(8,128)(2,1)S(1)}, u32[]{:S(2)}, u32[]{:S(2)}) %collective-permute-start.22) | collective-permute-done | bytes 262176 | tf_op jit(solution)/shard_map/ppermute | solution.py:230
  110.9 1.3 collective-permute-start.29
  112.2 1.3 collective-permute-start.18
  113.5 31.0 %collective-permute-done.26.refs_10_ = bf16[256,512]{1,0:T(8,128)(2,1)S(1)} collective-permute-done((bf16[256,512]{1,0:T(8,128)(2,1)S(1)}, bf16[256,512]{1,0:T(8,128)(2,1)S(1)}, u32[]{:S(2)}, u32[]{:S(2)}) %collective-permute-start.26) | collective-permute-done | bytes 262176 | tf_op jit(solution)/shard_map/ppermute | solution.py:230
  144.6 1.3 collective-permute-start.14
  145.9 4.3 %collective-permute-done.29.refs_0_ = bf16[256,512]{1,0:T(8,128)(2,1)S(1)} collective-permute-done((bf16[256,512]{1,0:T(8,128)(2,1)S(1)}, bf16[256,512]{1,0:T(8,128)(2,1)S(1)}, u32[]{:S(2)}, u32[]{:S(2)}) %collective-permute-start.29) | collective-permute-done | bytes 262176 | tf_op jit(solution)/shard_map/ppermute | solution.py:230
  150.9 1.3 collective-permute-start.9
  152.2 1.3 collective-permute-start.16
  153.5 30.4 %collective-permute-done.14.refs_0_ = bf16[256,1024]{1,0:T(8,128)(2,1)S(1)} collective-permute-done((bf16[256,1024]{1,0:T(8,128)(2,1)S(1)}, bf16[256,1024]{1,0:T(8,128)(2,1)S(1)}, u32[]{:S(2)}, u32[]{:S(2)}) %collective-permute-start.14) | collective-permute-done | bytes 524320 | tf_op jit(solution)/shard_map/ppermute | solution.py:230
  183.9 1.3 collective-permute-start.3
  185.2 1.3 collective-permute-start.6
  186.5 31.1 %collective-permute-done.16.refs_2_ = bf16[256,1024]{1,0:T(8,128)(2,1)S(1)} collective-permute-done((bf16[256,1024]{1,0:T(8,128)(2,1)S(1)}, bf16[256,1024]{1,0:T(8,128)(2,1)S(1)}, u32[]{:S(2)}, u32[]{:S(2)}) %collective-permute-start.16) | collective-permute-done | bytes 524320 | tf_op jit(solution)/shard_map/ppermute | solution.py:230
  218.9 1.3 collective-permute-start.12
  220.2 2.5 %shard_map.177 = (bf16[2048,1024]{1,0:T(8,128)(2,1)}, bf16[1024,2048]{1,0:T(8,128)(2,1)}, bf16[64,128]{1,0:T(8,128)(2,1)S(1)}, bf16[256,2048]{1,0:T(8,128)(2,1)}, bf16[256,2048]{1,0:T(8,128)(2,1)}) custom-call(bf16[256,1024]{1,0:T(8,128)(2,1)S(1)} %shard_map.173.refs_0_, bf16[256,1024]{1,0:T(8,128)(2,1)S(1)} %shard_map.174.refs_1_, ...), custom_call_target="tpu_custom_call" | custom-call | tf_op jit(solution)/shard_map/pallas_call | solution.py:138
  222.7 1.6 shard_map.178
  225.1 12.7 %collective-permute-done.30.refs_0_ = bf16[256,512]{1,0:T(8,128)(2,1)S(1)} collective-permute-done((bf16[256,512]{1,0:T(8,128)(2,1)S(1)}, bf16[256,512]{1,0:T(8,128)(2,1)S(1)}, u32[]{:S(2)}, u32[]{:S(2)}) %collective-permute-start.30) | collective-permute-done | bytes 262176 | tf_op jit(solution)/shard_map/ppermute | solution.py:230
  238.5 1.4 shard_map.179
  (45 shorter events, 14.9 us)
Async XLA Ops:
  0.6 0.7 copy-start
  4.7 64.1 %collective-permute-start.7 = (bf16[1024,512]{1,0:T(8,128)(2,1)S(1)}, bf16[1024,512]{1,0:T(8,128)(2,1)S(1)}, u32[]{:S(2)}, u32[]{:S(2)}) collective-permute-start(bf16[1024,512]{1,0:T(8,128)(2,1)S(1)} %get-tuple-element.22.refs_6_), channel_id=1, source_target_pairs={{8,0},{0,8},{24,16},{16,24},{9,1},{1,9},{25,17},{17,25},{10,2},{2,... | collective-permute-start | bytes 3145736 | tf_op jit(solution)/shard_map/ppermute | solution.py:230
  9.6 21.4 %collective-permute-start.10 = (bf16[16,128]{1,0:T(8,128)(2,1)S(1)}, bf16[16,128]{1,0:T(8,128)(2,1)S(1)}, u32[]{:S(2)}, u32[]{:S(2)}) collective-permute-start(bf16[16,128]{1,0:T(8,128)(2,1)S(1)} %all_gather.3.refs_9_), channel_id=1, source_target_pairs={{8,0},{0,8},{24,16},{16,24},{9,1},{1,9},{25,17},{17,25},{10,2},{2,... | collective-permute-start | bytes 12296 | tf_op jit(solution)/shard_map/ppermute | solution.py:230
  9.7 22.0 %collective-permute-start.19 = (bf16[16,128]{1,0:T(8,128)(2,1)S(1)}, bf16[16,128]{1,0:T(8,128)(2,1)S(1)}, u32[]{:S(2)}, u32[]{:S(2)}) collective-permute-start(bf16[16,128]{1,0:T(8,128)(2,1)S(1)} %all_gather.3.refs_9_), channel_id=1, source_target_pairs={{16,8},{8,16},{17,9},{9,17},{18,10},{10,18},{19,11},{11,19},{20,12... | collective-permute-start | bytes 12296 | tf_op jit(solution)/shard_map/ppermute | solution.py:230
  10.4 31.4 %collective-permute-start.21 = (bf16[256,512]{1,0:T(8,128)(2,1)S(1)}, bf16[256,512]{1,0:T(8,128)(2,1)S(1)}, u32[]{:S(2)}, u32[]{:S(2)}) collective-permute-start(bf16[256,512]{1,0:T(8,128)(2,1)S(1)} %get-tuple-element.24.refs_12_), channel_id=1, source_target_pairs={{16,8},{8,16},{17,9},{9,17},{18,10},{10,18},{19,11},{11,19},{20,12... | collective-permute-start | bytes 786440 | tf_op jit(solution)/shard_map/ppermute | solution.py:230
  31.1 8.0 %collective-permute-start.11 = (bf16[16,128]{1,0:T(8,128)(2,1)S(1)}, bf16[16,128]{1,0:T(8,128)(2,1)S(1)}, u32[]{:S(2)}, u32[]{:S(2)}) collective-permute-start(bf16[16,128]{1,0:T(8,128)(2,1)S(1)} %collective-permute-done.10.refs_10_), channel_id=1, source_target_pairs={{16,8},{8,16},{17,9},{9,17},{18,10},{10,18},{19,11},{11,19},{20,12... | collective-permute-start | bytes 12296 | tf_op jit(solution)/shard_map/ppermute | solution.py:230
  31.7 9.3 %collective-permute-start.20 = (bf16[16,128]{1,0:T(8,128)(2,1)S(1)}, bf16[16,128]{1,0:T(8,128)(2,1)S(1)}, u32[]{:S(2)}, u32[]{:S(2)}) collective-permute-start(bf16[16,128]{1,0:T(8,128)(2,1)S(1)} %collective-permute-done.19.refs_11_), channel_id=1, source_target_pairs={{8,0},{16,24},{9,1},{17,25},{10,2},{18,26},{11,3},{19,27},{12,4},{... | collective-permute-start | bytes 12296 | tf_op jit(solution)/shard_map/ppermute | solution.py:230
  33.0 10.6 %collective-permute-start.23 = (bf16[256,512]{1,0:T(8,128)(2,1)S(1)}, bf16[256,512]{1,0:T(8,128)(2,1)S(1)}, u32[]{:S(2)}, u32[]{:S(2)}) collective-permute-start(bf16[256,512]{1,0:T(8,128)(2,1)S(1)} %get-tuple-element.24.refs_12_), channel_id=1, source_target_pairs={{8,0},{0,8},{24,16},{16,24},{9,1},{1,9},{25,17},{17,25},{10,2},{2,... | collective-permute-start | bytes 786440 | tf_op jit(solution)/shard_map/ppermute | solution.py:230
  39.1 22.8 %collective-permute-start = (bf16[256,1024]{1,0:T(8,128)(2,1)S(1)}, bf16[256,1024]{1,0:T(8,128)(2,1)S(1)}, u32[]{:S(2)}, u32[]{:S(2)}) collective-permute-start(bf16[256,1024]{1,0:T(8,128)(2,1)S(1)} %shard_map.173.refs_0_), channel_id=1, source_target_pairs={{8,0},{0,8},{24,16},{16,24},{9,1},{1,9},{25,17},{17,25},{10,2},{2,... | collective-permute-start | bytes 1572872 | tf_op jit(solution)/shard_map/ppermute | solution.py:182
  41.1 21.5 %collective-permute-start.1 = (bf16[256,1024]{1,0:T(8,128)(2,1)S(1)}, bf16[256,1024]{1,0:T(8,128)(2,1)S(1)}, u32[]{:S(2)}, u32[]{:S(2)}) collective-permute-start(bf16[256,1024]{1,0:T(8,128)(2,1)S(1)} %shard_map.173.refs_0_), channel_id=1, source_target_pairs={{12,4},{4,12},{28,20},{20,28},{13,5},{5,13},{29,21},{21,29},{14,6}... | collective-permute-start | bytes 1572872 | tf_op jit(solution)/shard_map/ppermute | solution.py:183
  41.8 4.9 %collective-permute-start.25 = (bf16[256,512]{1,0:T(8,128)(2,1)S(1)}, bf16[256,512]{1,0:T(8,128)(2,1)S(1)}, u32[]{:S(2)}, u32[]{:S(2)}) collective-permute-start(bf16[256,512]{1,0:T(8,128)(2,1)S(1)} %get-tuple-element.25.refs_15_), channel_id=1, source_target_pairs={{16,8},{8,16},{17,9},{9,17},{18,10},{10,18},{19,11},{11,19},{20,12... | collective-permute-start | bytes 786440 | tf_op jit(solution)/shard_map/ppermute | solution.py:230
  43.6 16.1 %collective-permute-start.27 = (bf16[256,512]{1,0:T(8,128)(2,1)S(1)}, bf16[256,512]{1,0:T(8,128)(2,1)S(1)}, u32[]{:S(2)}, u32[]{:S(2)}) collective-permute-start(bf16[256,512]{1,0:T(8,128)(2,1)S(1)} %get-tuple-element.25.refs_15_), channel_id=1, source_target_pairs={{8,0},{0,8},{24,16},{16,24},{9,1},{1,9},{25,17},{17,25},{10,2},{2,... | collective-permute-start | bytes 786440 | tf_op jit(solution)/shard_map/ppermute | solution.py:230
  46.7 65.5 %collective-permute-start.17 = (bf16[1024,512]{1,0:T(8,128)(2,1)S(1)}, bf16[1024,512]{1,0:T(8,128)(2,1)S(1)}, u32[]{:S(2)}, u32[]{:S(2)}) collective-permute-start(bf16[1024,512]{1,0:T(8,128)(2,1)S(1)} %get-tuple-element.22.refs_6_), channel_id=1, source_target_pairs={{16,8},{8,16},{17,9},{9,17},{18,10},{10,18},{19,11},{11,19},{20,12... | collective-permute-start | bytes 3145736 | tf_op jit(solution)/shard_map/ppermute | solution.py:230
  59.7 9.8 %collective-permute-start.13 = (bf16[256,1024]{1,0:T(8,128)(2,1)S(1)}, bf16[256,1024]{1,0:T(8,128)(2,1)S(1)}, u32[]{:S(2)}, u32[]{:S(2)}) collective-permute-start(bf16[256,1024]{1,0:T(8,128)(2,1)S(1)} %shard_map.173.refs_0_), channel_id=1, source_target_pairs={{16,8},{8,16},{17,9},{9,17},{18,10},{10,18},{19,11},{11,19},{20,12... | collective-permute-start | bytes 1572872 | tf_op jit(solution)/shard_map/ppermute | solution.py:230
  61.9 8.4 %collective-permute-start.15 = (bf16[256,1024]{1,0:T(8,128)(2,1)S(1)}, bf16[256,1024]{1,0:T(8,128)(2,1)S(1)}, u32[]{:S(2)}, u32[]{:S(2)}) collective-permute-start(bf16[256,1024]{1,0:T(8,128)(2,1)S(1)} %shard_map.175.refs_3_), channel_id=1, source_target_pairs={{16,8},{8,16},{17,9},{9,17},{18,10},{10,18},{19,11},{11,19},{20,12... | collective-permute-start | bytes 1572872 | tf_op jit(solution)/shard_map/ppermute | solution.py:230
  62.6 16.3 %collective-permute-start.4 = (bf16[256,1024]{1,0:T(8,128)(2,1)S(1)}, bf16[256,1024]{1,0:T(8,128)(2,1)S(1)}, u32[]{:S(2)}, u32[]{:S(2)}) collective-permute-start(bf16[256,1024]{1,0:T(8,128)(2,1)S(1)} %shard_map.175.refs_3_), channel_id=1, source_target_pairs={{8,0},{0,8},{24,16},{16,24},{9,1},{1,9},{25,17},{17,25},{10,2},{2,... | collective-permute-start | bytes 1572872 | tf_op jit(solution)/shard_map/ppermute | solution.py:230
  68.8 82.1 %collective-permute-start.8 = (bf16[1024,512]{1,0:T(8,128)(2,1)S(1)}, bf16[1024,512]{1,0:T(8,128)(2,1)S(1)}, u32[]{:S(2)}, u32[]{:S(2)}) collective-permute-start(bf16[1024,512]{1,0:T(8,128)(2,1)S(1)} %collective-permute-done.7.refs_7_), channel_id=1, source_target_pairs={{16,8},{8,16},{17,9},{9,17},{18,10},{10,18},{19,11},{11,19},{20,12... | collective-permute-start | bytes 3145736 | tf_op jit(solution)/shard_map/ppermute | solution.py:230
  69.5 10.7 %collective-permute-start.24 = (bf16[256,512]{1,0:T(8,128)(2,1)S(1)}, bf16[256,512]{1,0:T(8,128)(2,1)S(1)}, u32[]{:S(2)}, u32[]{:S(2)}) collective-permute-start(bf16[256,512]{1,0:T(8,128)(2,1)S(1)} %collective-permute-done.23.refs_13_), channel_id=1, source_target_pairs={{16,8},{8,16},{17,9},{9,17},{18,10},{10,18},{19,11},{11,19},{20,12... | collective-permute-start | bytes 786440 | tf_op jit(solution)/shard_map/ppermute | solution.py:230
  70.2 10.7 %collective-permute-start.28 = (bf16[256,512]{1,0:T(8,128)(2,1)S(1)}, bf16[256,512]{1,0:T(8,128)(2,1)S(1)}, u32[]{:S(2)}, u32[]{:S(2)}) collective-permute-start(bf16[256,512]{1,0:T(8,128)(2,1)S(1)} %collective-permute-done.27.refs_16_), channel_id=1, source_target_pairs={{16,8},{8,16},{17,9},{9,17},{18,10},{10,18},{19,11},{11,19},{20,12... | collective-permute-start | bytes 786440 | tf_op jit(solution)/shard_map/ppermute | solution.py:230
  78.9 32.0 %collective-permute-start.22 = (bf16[256,512]{1,0:T(8,128)(2,1)S(1)}, bf16[256,512]{1,0:T(8,128)(2,1)S(1)}, u32[]{:S(2)}, u32[]{:S(2)}) collective-permute-start(bf16[256,512]{1,0:T(8,128)(2,1)S(1)} %collective-permute-done.21.refs_14_), channel_id=1, source_target_pairs={{8,0},{16,24},{9,1},{17,25},{10,2},{18,26},{11,3},{19,27},{12,4},{... | collective-permute-start | bytes 786440 | tf_op jit(solution)/shard_map/ppermute | solution.py:230
  80.3 71.9 %collective-permute-start.2 = (bf16[256,1024]{1,0:T(8,128)(2,1)S(1)}, bf16[256,1024]{1,0:T(8,128)(2,1)S(1)}, u32[]{:S(2)}, u32[]{:S(2)}) collective-permute-start(bf16[256,1024]{1,0:T(8,128)(2,1)S(1)} %shard_map.174.refs_1_), channel_id=1, source_target_pairs={{16,8},{8,16},{17,9},{9,17},{18,10},{10,18},{19,11},{11,19},{20,12... | collective-permute-start | bytes 1572872 | tf_op jit(solution)/shard_map/ppermute | solution.py:230
  81.0 63.6 %collective-permute-start.26 = (bf16[256,512]{1,0:T(8,128)(2,1)S(1)}, bf16[256,512]{1,0:T(8,128)(2,1)S(1)}, u32[]{:S(2)}, u32[]{:S(2)}) collective-permute-start(bf16[256,512]{1,0:T(8,128)(2,1)S(1)} %collective-permute-done.25.refs_17_), channel_id=1, source_target_pairs={{8,0},{16,24},{9,1},{17,25},{10,2},{18,26},{11,3},{19,27},{12,4},{... | collective-permute-start | bytes 786440 | tf_op jit(solution)/shard_map/ppermute | solution.py:230
  110.9 39.3 %collective-permute-start.29 = (bf16[256,512]{1,0:T(8,128)(2,1)S(1)}, bf16[256,512]{1,0:T(8,128)(2,1)S(1)}, u32[]{:S(2)}, u32[]{:S(2)}) collective-permute-start(bf16[256,512]{1,0:T(8,128)(2,1)S(1)} %collective-permute-done.24.refs_9_), channel_id=1, source_target_pairs={{8,0},{16,24},{9,1},{17,25},{10,2},{18,26},{11,3},{19,27},{12,4},{... | collective-permute-start | bytes 786440 | tf_op jit(solution)/shard_map/ppermute | solution.py:230
  112.2 106.7 %collective-permute-start.18 = (bf16[1024,512]{1,0:T(8,128)(2,1)S(1)}, bf16[1024,512]{1,0:T(8,128)(2,1)S(1)}, u32[]{:S(2)}, u32[]{:S(2)}) collective-permute-start(bf16[1024,512]{1,0:T(8,128)(2,1)S(1)} %collective-permute-done.17.refs_8_), channel_id=1, source_target_pairs={{8,0},{16,24},{9,1},{17,25},{10,2},{18,26},{11,3},{19,27},{12,4},{... | collective-permute-start | bytes 3145736 | tf_op jit(solution)/shard_map/ppermute | solution.py:230
  144.6 39.3 %collective-permute-start.14 = (bf16[256,1024]{1,0:T(8,128)(2,1)S(1)}, bf16[256,1024]{1,0:T(8,128)(2,1)S(1)}, u32[]{:S(2)}, u32[]{:S(2)}) collective-permute-start(bf16[256,1024]{1,0:T(8,128)(2,1)S(1)} %collective-permute-done.13.refs_2_), channel_id=1, source_target_pairs={{8,0},{16,24},{9,1},{17,25},{10,2},{18,26},{11,3},{19,27},{12,4},{... | collective-permute-start | bytes 1572872 | tf_op jit(solution)/shard_map/ppermute | solution.py:230
  150.2 35.0 %collective-permute-start.5 = (bf16[256,1024]{1,0:T(8,128)(2,1)S(1)}, bf16[256,1024]{1,0:T(8,128)(2,1)S(1)}, u32[]{:S(2)}, u32[]{:S(2)}) collective-permute-start(bf16[256,1024]{1,0:T(8,128)(2,1)S(1)} %collective-permute-done.4.refs_4_), channel_id=1, source_target_pairs={{16,8},{8,16},{17,9},{9,17},{18,10},{10,18},{19,11},{11,19},{20,12... | collective-permute-start | bytes 1572872 | tf_op jit(solution)/shard_map/ppermute | solution.py:230
  150.9 87.6 %collective-permute-start.9 = (bf16[1024,512]{1,0:T(8,128)(2,1)S(1)}, bf16[1024,512]{1,0:T(8,128)(2,1)S(1)}, u32[]{:S(2)}, u32[]{:S(2)}) collective-permute-start(bf16[1024,512]{1,0:T(8,128)(2,1)S(1)} %collective-permute-done.8.refs_5_), channel_id=1, source_target_pairs={{8,0},{16,24},{9,1},{17,25},{10,2},{18,26},{11,3},{19,27},{12,4},{... | collective-permute-start | bytes 3145736 | tf_op jit(solution)/shard_map/ppermute | solution.py:230
  152.2 65.4 %collective-permute-start.16 = (bf16[256,1024]{1,0:T(8,128)(2,1)S(1)}, bf16[256,1024]{1,0:T(8,128)(2,1)S(1)}, u32[]{:S(2)}, u32[]{:S(2)}) collective-permute-start(bf16[256,1024]{1,0:T(8,128)(2,1)S(1)} %collective-permute-done.15.refs_5_), channel_id=1, source_target_pairs={{8,0},{16,24},{9,1},{17,25},{10,2},{18,26},{11,3},{19,27},{12,4},{... | collective-permute-start | bytes 1572872 | tf_op jit(solution)/shard_map/ppermute | solution.py:230
  183.9 54.6 %collective-permute-start.3 = (bf16[256,1024]{1,0:T(8,128)(2,1)S(1)}, bf16[256,1024]{1,0:T(8,128)(2,1)S(1)}, u32[]{:S(2)}, u32[]{:S(2)}) collective-permute-start(bf16[256,1024]{1,0:T(8,128)(2,1)S(1)} %collective-permute-done.2.refs_1_), channel_id=1, source_target_pairs={{8,0},{16,24},{9,1},{17,25},{10,2},{18,26},{11,3},{19,27},{12,4},{... | collective-permute-start | bytes 1572872 | tf_op jit(solution)/shard_map/ppermute | solution.py:230
  185.2 53.3 %collective-permute-start.6 = (bf16[256,1024]{1,0:T(8,128)(2,1)S(1)}, bf16[256,1024]{1,0:T(8,128)(2,1)S(1)}, u32[]{:S(2)}, u32[]{:S(2)}) collective-permute-start(bf16[256,1024]{1,0:T(8,128)(2,1)S(1)} %collective-permute-done.5.refs_3_), channel_id=1, source_target_pairs={{8,0},{16,24},{9,1},{17,25},{10,2},{18,26},{11,3},{19,27},{12,4},{... | collective-permute-start | bytes 1572872 | tf_op jit(solution)/shard_map/ppermute | solution.py:230
  217.6 20.2 %collective-permute-start.30 = (bf16[256,512]{1,0:T(8,128)(2,1)S(1)}, bf16[256,512]{1,0:T(8,128)(2,1)S(1)}, u32[]{:S(2)}, u32[]{:S(2)}) collective-permute-start(bf16[256,512]{1,0:T(8,128)(2,1)S(1)} %collective-permute-done.28.refs_11_), channel_id=1, source_target_pairs={{8,0},{16,24},{9,1},{17,25},{10,2},{18,26},{11,3},{19,27},{12,4},{... | collective-permute-start | bytes 786440 | tf_op jit(solution)/shard_map/ppermute | solution.py:230
  218.9 19.6 %collective-permute-start.12 = (bf16[16,128]{1,0:T(8,128)(2,1)S(1)}, bf16[16,128]{1,0:T(8,128)(2,1)S(1)}, u32[]{:S(2)}, u32[]{:S(2)}) collective-permute-start(bf16[16,128]{1,0:T(8,128)(2,1)S(1)} %collective-permute-done.11.refs_7_), channel_id=1, source_target_pairs={{8,0},{16,24},{9,1},{17,25},{10,2},{18,26},{11,3},{19,27},{12,4},{... | collective-permute-start | bytes 12296 | tf_op jit(solution)/shard_map/ppermute | solution.py:230
  (1 other events, 0.7 us)

commit v4 on v2

--- a/solution.py
+++ b/solution.py
@@ -17,47 +17,20 @@
 in_hbm = pl.BlockSpec(memory_space=pltpu.HBM)
 
 
-def merge_body(spans, *refs):
-    count = len(spans)
-    inputs = 3 * sum(span is not None for span in spans) + 2 * sum(span is None for span in spans)
-    sources, outs = iter(refs[:inputs]), refs[inputs : inputs + count]
-    held, sems = iter(refs[inputs + count : -1]), refs[-1]
-    work = []
-    used = 0
-
-    def start(source, target):
-        nonlocal used
-        copy = pltpu.make_async_copy(source, target, sems.at[used])
+def merge_into(out_ref, first, w_ref, low_ref, high_ref, w_held, low_held, high_held, sems):
+    total = out_ref.shape[0]
+    copies = [
+        pltpu.make_async_copy(low_ref, low_held, sems.at[0]),
+        pltpu.make_async_copy(high_ref.at[:, pl.ds(first, total)], high_held, sems.at[1]),
+    ]
+    parts = [pl.ds(base, size) for base, size in blocks(total)]
+    for j, (base, size) in enumerate(blocks(total)):
+        source = w_ref.at[:, pl.ds(first + base, size)]
+        copies.append(pltpu.make_async_copy(source, w_held.at[:, parts[j]], sems.at[2 + j]))
+    for copy in copies:
         copy.start()
-        used += 1
-        return copy
-
-    for span, out_ref in zip(spans, outs):
-        if span is None:
-            work.append((next(sources), next(sources), out_ref))
-            continue
-        first, blocks = span
-        w_ref, low_ref, high_ref = (next(sources) for _ in range(3))
-        w_held, low_held, high_held = (next(held) for _ in range(3))
-        copies = [
-            start(low_ref, low_held),
-            start(high_ref.at[:, pl.ds(first, sum(blocks))], high_held),
-        ]
-        base = 0
-        parts = []
-        for block in blocks:
-            part = pl.ds(base, block)
-            copies.append(start(w_ref.at[:, pl.ds(first + base, block)], w_held.at[:, part]))
-            parts.append(part)
-            base += block
-        work.append((w_held, low_held, high_held, copies, parts, out_ref))
-    for item in work:
-        if len(item) == 3:
-            train_ref, step_ref, out_ref = item
-            out_ref[...] = jnp.zeros_like(out_ref)
-            out_ref[: train_ref.shape[0], :] = (train_ref[...] + step_ref[...]).astype(jnp.bfloat16)
-            continue
-        w_held, low_held, high_held, copies, parts, out_ref = item
+
+    def finish():
         copies[0].wait()
         copies[1].wait()
         for part, copy in zip(parts, copies[2:]):
@@ -71,40 +44,99 @@
             kept = w_held[:, part].T.astype(jnp.float32)
             out_ref[part, :] = (kept + mix_rate * delta).astype(jnp.bfloat16)
 
-
-def merged(*tasks):
-    spans, operands, specs, shapes, scratch, copies = [], [], [], [], [], 0
-    for task in tasks:
-        if len(task) == 2:
-            used = task[0].size // lanes
-            tall = -(-used // sublanes) * sublanes
-            spans.append(None)
-            operands += [a.reshape(used, lanes) for a in task]
-            specs += [in_vmem] * 2
-            shapes.append(jax.ShapeDtypeStruct((tall, lanes), jnp.bfloat16))
-            continue
-        w, low, high, first, last = task
-        rows, total, rank = w.shape[0], last - first, low.shape[1]
-        block = 2 * lanes
-        blocks = [min(block, total - base) for base in range(0, total, block)]
-        spans.append((first, blocks))
-        operands += [pltpu.with_memory_space_constraint(a, pltpu.HBM) for a in (w, low.T, high)]
-        specs += [in_hbm] * 3
-        shapes.append(jax.ShapeDtypeStruct((total, rows), jnp.bfloat16))
-        scratch += [
-            pltpu.VMEM((rows, total), jnp.bfloat16),
-            pltpu.VMEM((rank, rows), jnp.bfloat16),
-            pltpu.VMEM((rank, total), jnp.bfloat16),
+    return finish
+
+
+def blocks(total):
+    size = 2 * lanes
+    return [(base, min(size, total - base)) for base in range(0, total, size)]
+
+
+def scratch_of(w, low, total):
+    rows, rank = w.shape[0], low.shape[1]
+    return [
+        pltpu.VMEM((rows, total), jnp.bfloat16),
+        pltpu.VMEM((rank, rows), jnp.bfloat16),
+        pltpu.VMEM((rank, total), jnp.bfloat16),
+        pltpu.SemaphoreType.DMA((2 + len(blocks(total)),)),
+    ]
+
+
+def operands_of(w, low, high):
+    return [pltpu.with_memory_space_constraint(a, pltpu.HBM) for a in (w, low.T, high)]
+
+
+merge_params = pltpu.CompilerParams(vmem_limit_bytes=12 << 20)
+
+
+def leads():
+    return lax.axis_index("width") == 0
+
+
+def merged_head(w, low, high, head):
+    rows, columns = w.shape
+
+    def body(w_ref, low_ref, high_ref, head_ref, rest_ref, *scratch):
+        merge_into(head_ref, 0, w_ref, low_ref, high_ref, *scratch[:4])()
+
+        @pl.when(jnp.logical_not(leads()))
+        def _():
+            merge_into(rest_ref, head, w_ref, low_ref, high_ref, *scratch[4:])()
+
+    return pl.pallas_call(
+        body,
+        in_specs=[in_hbm] * 3,
+        out_specs=[in_vmem] * 2,
+        out_shape=[jax.ShapeDtypeStruct((n, rows), jnp.bfloat16) for n in (head, columns - head)],
+        scratch_shapes=scratch_of(w, low, head) + scratch_of(w, low, columns - head),
+        compiler_params=merge_params,
+    )(*operands_of(w, low, high))
+
+
+def merged_rest(rest, w, low, high, head):
+    def body(w_ref, low_ref, high_ref, _, rest_ref, *scratch):
+        @pl.when(leads())
+        def _():
+            merge_into(rest_ref, head, w_ref, low_ref, high_ref, *scratch)()
+
+    return pl.pallas_call(
+        body,
+        in_specs=[in_hbm] * 3 + [in_vmem],
+        out_specs=in_vmem,
+        out_shape=jax.ShapeDtypeStruct(rest.shape, rest.dtype),
+        scratch_shapes=scratch_of(w, low, rest.shape[0]),
+        input_output_aliases={3: 0},
+        compiler_params=merge_params,
+    )(*operands_of(w, low, high), rest)
+
+
+def merged_others(weights, norms):
+    used = norms[0].size // lanes
+    tall = -(-used // sublanes) * sublanes
+    count = len(weights)
+
+    def body(*refs):
+        inputs, (train_ref, step_ref) = refs[: 3 * count], refs[3 * count : 3 * count + 2]
+        outs, row_ref = refs[3 * count + 2 :][:count], refs[4 * count + 2]
+        scratch = refs[4 * count + 3 :]
+        finishes = [
+            merge_into(outs[j], 0, *inputs[3 * j : 3 * j + 3], *scratch[4 * j : 4 * j + 4])
+            for j in range(count)
         ]
-        copies += 2 + len(blocks)
+        row_ref[...] = jnp.zeros_like(row_ref)
+        row_ref[:used, :] = (train_ref[...] + step_ref[...]).astype(jnp.bfloat16)
+        for finish in finishes:
+            finish()
+
+    shapes = [jax.ShapeDtypeStruct(w.shape[::-1], jnp.bfloat16) for w, _, _ in weights]
     return pl.pallas_call(
-        functools.partial(merge_body, spans),
-        in_specs=specs,
-        out_specs=[in_vmem] * len(shapes),
-        out_shape=shapes,
-        scratch_shapes=[*scratch, pltpu.SemaphoreType.DMA((copies,))],
-        compiler_params=pltpu.CompilerParams(vmem_limit_bytes=12 << 20),
-    )(*operands)
+        body,
+        in_specs=[in_hbm] * (3 * count) + [in_vmem] * 2,
+        out_specs=[in_vmem] * (count + 1),
+        out_shape=[*shapes, jax.ShapeDtypeStruct((tall, lanes), jnp.bfloat16)],
+        scratch_shapes=[ref for w, low, _ in weights for ref in scratch_of(w, low, w.shape[1])],
+        compiler_params=merge_params,
+    )(*(a for weight in weights for a in operands_of(*weight)), *(a.reshape(used, lanes) for a in norms))
 
 
 def place_body(count, moves, outs_at, *refs):
@@ -163,6 +195,7 @@
     return plan
 
 
+head = lanes
 chunk_names = ("mixed_head", "mixed_rest", "query", "norm", "key", "value")
 
 
@@ -174,15 +207,13 @@
 def by_line(count, query, key, value, mixed, norms):
     rows, columns = query[0].shape[0], mixed[0].shape[1]
     pieces = {}
-    (pieces["mixed_head"],) = merged((*mixed, 0, lanes))
-    (pieces["mixed_rest"],) = merged((*mixed, lanes, columns))
-    pieces["query"], pieces["key"], pieces["value"], row = merged(
-        *((*weight, 0, weight[0].shape[1]) for weight in (query, key, value)), norms
-    )
+    pieces["mixed_head"], rest = merged_head(*mixed, head)
+    pieces["mixed_rest"] = merged_rest(rest, *mixed, head)
+    pieces["query"], pieces["key"], pieces["value"], row = merged_others((query, key, value), norms)
     pieces["norm"] = lax.all_gather(row, "width", axis=0, tiled=True)
     where = {
         "mixed_head": ("mixed", 0, columns, 0),
-        "mixed_rest": ("mixed", 0, columns, lanes),
+        "mixed_rest": ("mixed", 0, columns, head),
         "query": ("query", 1, rows, 0),
         "norm": ("norm", 0, pieces["norm"].shape[0], 0),
         "key": ("key", 1, rows, 0),

time: 239 us -> 239 us (level)
  no operation moved by 1% of the time
where the time goes in v4:
time: 239 us; the launch traced here: 238 us
  waiting for transfers between devices  184 us (77%)
  starting transfers between devices  36.1 us (15%)
  Pallas kernels  12.7 us (5%)
    ppermute x30, waiting for transfers between devices, by_line(): held[name][hop] = lax.ppermute(held[name][source], 'shard', pairs)  184 us
    ppermute x30, starting transfers between devices, by_line(): held[name][hop] = lax.ppermute(held[name][source], 'shard', pairs)  36.1 us
    pallas_call x5, Pallas kernels, place(): pl.pallas_call(functools.partial(place_body, count, moves, len(arrays) +...  6.94 us
  transfers between devices with their start and end apart: 30, of which 10 were waited for; matrix products, arithmetic and copies ran while one was open for 0% of the time, Pallas kernels for 4%

profile of v4, /device:TPU:0, one launch (start us, length us, event | category | flops | bytes accessed | tf_op | source)
XLA Modules:
  0.0 237.8 jit_solution(470172826081289852)
XLA Ops:
  2.0 2.7 %shard_map.175 = (bf16[1024,512]{1,0:T(8,128)(2,1)S(1)}, bf16[256,512]{1,0:T(8,128)(2,1)S(1)}, bf16[256,512]{1,0:T(8,128)(2,1)S(1)}, bf16[8,128]{1,0:T(8,128)(2,1)S(1)}) custom-call(bf16[512,1024]{1,0:T(8,128)(2,1)} %refs_0_.1, bf16[16,512]{1,0:T(8,128)(2,1)} %bitcast.13, bf16[16,1024]{1,0:T(8,128)(2,1)} %refs_2_.1, bf16[512,256]{1,0:T(8,128)(2,1)} %refs_3_.1, ...), custom_call_target="tpu_custom_call" | custom-call | tf_op jit(solution)/shard_map/pallas_call | solution.py:132
  4.7 3.1 %collective-permute-start.6 = (bf16[1024,512]{1,0:T(8,128)(2,1)S(1)}, bf16[1024,512]{1,0:T(8,128)(2,1)S(1)}, u32[]{:S(2)}, u32[]{:S(2)}) collective-permute-start(bf16[1024,512]{1,0:T(8,128)(2,1)S(1)} %get-tuple-element.26.refs_6_), channel_id=1, source_target_pairs={{8,0},{0,8},{24,16},{16,24},{9,1},{1,9},{25,17},{17,25},{10,2},{2,... | collective-permute-start | bytes 3145736 | tf_op jit(solution)/shard_map/ppermute | solution.py:230
  8.5 4.5 %collective-permute-start.22 = (bf16[256,512]{1,0:T(8,128)(2,1)S(1)}, bf16[256,512]{1,0:T(8,128)(2,1)S(1)}, u32[]{:S(2)}, u32[]{:S(2)}) collective-permute-start(bf16[256,512]{1,0:T(8,128)(2,1)S(1)} %get-tuple-element.28.refs_12_), channel_id=1, source_target_pairs={{8,0},{0,8},{24,16},{16,24},{9,1},{1,9},{25,17},{17,25},{10,2},{2,... | collective-permute-start | bytes 786440 | tf_op jit(solution)/shard_map/ppermute | solution.py:230
  12.9 1.8 all_gather.3.refs_9_
  15.5 21.2 %collective-permute-done.9.refs_10_ = bf16[16,128]{1,0:T(8,128)(2,1)S(1)} collective-permute-done((bf16[16,128]{1,0:T(8,128)(2,1)S(1)}, bf16[16,128]{1,0:T(8,128)(2,1)S(1)}, u32[]{:S(2)}, u32[]{:S(2)}) %collective-permute-start.9) | collective-permute-done | bytes 4128 | tf_op jit(solution)/shard_map/ppermute | solution.py:230
  37.4 1.3 collective-permute-start.19
  39.3 5.4 %collective-permute-done.19.refs_6_ = bf16[16,128]{1,0:T(8,128)(2,1)S(1)} collective-permute-done((bf16[16,128]{1,0:T(8,128)(2,1)S(1)}, bf16[16,128]{1,0:T(8,128)(2,1)S(1)}, u32[]{:S(2)}, u32[]{:S(2)}) %collective-permute-start.19) | collective-permute-done | bytes 4128 | tf_op jit(solution)/shard_map/ppermute | solution.py:230
  44.8 2.7 %collective-permute-start.26 = (bf16[256,512]{1,0:T(8,128)(2,1)S(1)}, bf16[256,512]{1,0:T(8,128)(2,1)S(1)}, u32[]{:S(2)}, u32[]{:S(2)}) collective-permute-start(bf16[256,512]{1,0:T(8,128)(2,1)S(1)} %get-tuple-element.29.refs_15_), channel_id=1, source_target_pairs={{8,0},{0,8},{24,16},{16,24},{9,1},{1,9},{25,17},{17,25},{10,2},{2,... | collective-permute-start | bytes 786440 | tf_op jit(solution)/shard_map/ppermute | solution.py:230
  47.5 1.3 shard_map.173
  48.9 1.7 shard_map.174.refs_3_
  50.6 2.1 collective-permute-start.3
  54.8 4.9 %collective-permute-done.refs_1_ = bf16[128,1024]{1,0:T(8,128)(2,1)S(1)} collective-permute-done((bf16[128,1024]{1,0:T(8,128)(2,1)S(1)}, bf16[128,1024]{1,0:T(8,128)(2,1)S(1)}, u32[]{:S(2)}, u32[]{:S(2)}) %collective-permute-start) | collective-permute-done | bytes 262176 | tf_op jit(solution)/shard_map/ppermute | solution.py:230
  62.6 1.3 collective-permute-start.21
  63.9 10.4 %collective-permute-done.3.refs_4_ = bf16[384,1024]{1,0:T(8,128)(2,1)S(1)} collective-permute-done((bf16[384,1024]{1,0:T(8,128)(2,1)S(1)}, bf16[384,1024]{1,0:T(8,128)(2,1)S(1)}, u32[]{:S(2)}, u32[]{:S(2)}) %collective-permute-start.3) | collective-permute-done | bytes 786464 | tf_op jit(solution)/shard_map/ppermute | solution.py:230
  75.0 53.4 %collective-permute-done.21.refs_8_ = bf16[256,512]{1,0:T(8,128)(2,1)S(1)} collective-permute-done((bf16[256,512]{1,0:T(8,128)(2,1)S(1)}, bf16[256,512]{1,0:T(8,128)(2,1)S(1)}, u32[]{:S(2)}, u32[]{:S(2)}) %collective-permute-start.21) | collective-permute-done | bytes 262176 | tf_op jit(solution)/shard_map/ppermute | solution.py:230
  128.4 1.3 collective-permute-start.25
  129.7 1.3 collective-permute-start.17
  131.0 8.5 %collective-permute-done.25.refs_10_ = bf16[256,512]{1,0:T(8,128)(2,1)S(1)} collective-permute-done((bf16[256,512]{1,0:T(8,128)(2,1)S(1)}, bf16[256,512]{1,0:T(8,128)(2,1)S(1)}, u32[]{:S(2)}, u32[]{:S(2)}) %collective-permute-start.25) | collective-permute-done | bytes 262176 | tf_op jit(solution)/shard_map/ppermute | solution.py:230
  140.1 1.3 collective-permute-start.15
  141.4 1.3 collective-permute-start.8
  142.7 1.3 collective-permute-start.13
  144.1 1.3 collective-permute-start.5
  145.4 61.5 %collective-permute-done.13.refs_0_ = bf16[128,1024]{1,0:T(8,128)(2,1)S(1)} collective-permute-done((bf16[128,1024]{1,0:T(8,128)(2,1)S(1)}, bf16[128,1024]{1,0:T(8,128)(2,1)S(1)}, u32[]{:S(2)}, u32[]{:S(2)}) %collective-permute-start.13) | collective-permute-done | bytes 262176 | tf_op jit(solution)/shard_map/ppermute | solution.py:230
  206.8 1.3 collective-permute-start.28
  208.1 16.6 %collective-permute-done.28.refs_0_ = bf16[256,512]{1,0:T(8,128)(2,1)S(1)} collective-permute-done((bf16[256,512]{1,0:T(8,128)(2,1)S(1)}, bf16[256,512]{1,0:T(8,128)(2,1)S(1)}, u32[]{:S(2)}, u32[]{:S(2)}) %collective-permute-start.28) | collective-permute-done | bytes 262176 | tf_op jit(solution)/shard_map/ppermute | solution.py:230
  224.7 1.3 collective-permute-start.29
  226.0 1.3 collective-permute-start.2
  227.3 1.3 collective-permute-start.11
  228.6 2.5 %shard_map.176 = (bf16[2048,1024]{1,0:T(8,128)(2,1)}, bf16[1024,2048]{1,0:T(8,128)(2,1)}, bf16[64,128]{1,0:T(8,128)(2,1)S(1)}, bf16[256,2048]{1,0:T(8,128)(2,1)}, bf16[256,2048]{1,0:T(8,128)(2,1)}) custom-call(bf16[128,1024]{1,0:T(8,128)(2,1)S(1)} %get-tuple-element.24.refs_0_, bf16[128,1024]{1,0:T(8,128)(2,1)S(1)} %collective-permute-done.refs_1_, ...), custom_call_target="tpu_custom_call" | custom-call | tf_op jit(solution)/shard_map/pallas_call | solution.py:170
  231.1 1.6 shard_map.177
  234.3 1.6 collective-permute-done.11.refs_3_
  235.9 1.4 shard_map.178
  (42 shorter events, 12.5 us)
Async XLA Ops:
  0.6 0.7 copy-start
  1.3 0.7 copy-start.1
  4.7 55.8 %collective-permute-start.6 = (bf16[1024,512]{1,0:T(8,128)(2,1)S(1)}, bf16[1024,512]{1,0:T(8,128)(2,1)S(1)}, u32[]{:S(2)}, u32[]{:S(2)}) collective-permute-start(bf16[1024,512]{1,0:T(8,128)(2,1)S(1)} %get-tuple-element.26.refs_6_), channel_id=1, source_target_pairs={{8,0},{0,8},{24,16},{16,24},{9,1},{1,9},{25,17},{17,25},{10,2},{2,... | collective-permute-start | bytes 3145736 | tf_op jit(solution)/shard_map/ppermute | solution.py:230
  7.8 41.0 %collective-permute-start.20 = (bf16[256,512]{1,0:T(8,128)(2,1)S(1)}, bf16[256,512]{1,0:T(8,128)(2,1)S(1)}, u32[]{:S(2)}, u32[]{:S(2)}) collective-permute-start(bf16[256,512]{1,0:T(8,128)(2,1)S(1)} %get-tuple-element.28.refs_12_), channel_id=1, source_target_pairs={{16,8},{8,16},{17,9},{9,17},{18,10},{10,18},{19,11},{11,19},{20,12... | collective-permute-start | bytes 786440 | tf_op jit(solution)/shard_map/ppermute | solution.py:230
  8.5 42.1 %collective-permute-start.22 = (bf16[256,512]{1,0:T(8,128)(2,1)S(1)}, bf16[256,512]{1,0:T(8,128)(2,1)S(1)}, u32[]{:S(2)}, u32[]{:S(2)}) collective-permute-start(bf16[256,512]{1,0:T(8,128)(2,1)S(1)} %get-tuple-element.28.refs_12_), channel_id=1, source_target_pairs={{8,0},{0,8},{24,16},{16,24},{9,1},{1,9},{25,17},{17,25},{10,2},{2,... | collective-permute-start | bytes 786440 | tf_op jit(solution)/shard_map/ppermute | solution.py:230
  14.8 21.9 %collective-permute-start.9 = (bf16[16,128]{1,0:T(8,128)(2,1)S(1)}, bf16[16,128]{1,0:T(8,128)(2,1)S(1)}, u32[]{:S(2)}, u32[]{:S(2)}) collective-permute-start(bf16[16,128]{1,0:T(8,128)(2,1)S(1)} %all_gather.3.refs_9_), channel_id=1, source_target_pairs={{8,0},{0,8},{24,16},{16,24},{9,1},{1,9},{25,17},{17,25},{10,2},{2,... | collective-permute-start | bytes 12296 | tf_op jit(solution)/shard_map/ppermute | solution.py:230
  14.8 22.5 %collective-permute-start.18 = (bf16[16,128]{1,0:T(8,128)(2,1)S(1)}, bf16[16,128]{1,0:T(8,128)(2,1)S(1)}, u32[]{:S(2)}, u32[]{:S(2)}) collective-permute-start(bf16[16,128]{1,0:T(8,128)(2,1)S(1)} %all_gather.3.refs_9_), channel_id=1, source_target_pairs={{16,8},{8,16},{17,9},{9,17},{18,10},{10,18},{19,11},{11,19},{20,12... | collective-permute-start | bytes 12296 | tf_op jit(solution)/shard_map/ppermute | solution.py:230
  36.7 2.0 collective-permute-start.10
  37.4 7.4 %collective-permute-start.19 = (bf16[16,128]{1,0:T(8,128)(2,1)S(1)}, bf16[16,128]{1,0:T(8,128)(2,1)S(1)}, u32[]{:S(2)}, u32[]{:S(2)}) collective-permute-start(bf16[16,128]{1,0:T(8,128)(2,1)S(1)} %collective-permute-done.18.refs_11_), channel_id=1, source_target_pairs={{8,0},{16,24},{9,1},{17,25},{10,2},{18,26},{11,3},{19,27},{12,4},{... | collective-permute-start | bytes 12296 | tf_op jit(solution)/shard_map/ppermute | solution.py:230
  38.7 14.0 %collective-permute-start.24 = (bf16[256,512]{1,0:T(8,128)(2,1)S(1)}, bf16[256,512]{1,0:T(8,128)(2,1)S(1)}, u32[]{:S(2)}, u32[]{:S(2)}) collective-permute-start(bf16[256,512]{1,0:T(8,128)(2,1)S(1)} %get-tuple-element.29.refs_15_), channel_id=1, source_target_pairs={{16,8},{8,16},{17,9},{9,17},{18,10},{10,18},{19,11},{11,19},{20,12... | collective-permute-start | bytes 786440 | tf_op jit(solution)/shard_map/ppermute | solution.py:230
  44.8 9.4 %collective-permute-start.26 = (bf16[256,512]{1,0:T(8,128)(2,1)S(1)}, bf16[256,512]{1,0:T(8,128)(2,1)S(1)}, u32[]{:S(2)}, u32[]{:S(2)}) collective-permute-start(bf16[256,512]{1,0:T(8,128)(2,1)S(1)} %get-tuple-element.29.refs_15_), channel_id=1, source_target_pairs={{8,0},{0,8},{24,16},{16,24},{9,1},{1,9},{25,17},{17,25},{10,2},{2,... | collective-permute-start | bytes 786440 | tf_op jit(solution)/shard_map/ppermute | solution.py:230
  48.8 11.0 %collective-permute-start = (bf16[128,1024]{1,0:T(8,128)(2,1)S(1)}, bf16[128,1024]{1,0:T(8,128)(2,1)S(1)}, u32[]{:S(2)}, u32[]{:S(2)}) collective-permute-start(bf16[128,1024]{1,0:T(8,128)(2,1)S(1)} %get-tuple-element.24.refs_0_), channel_id=1, source_target_pairs={{8,0},{0,8},{24,16},{16,24},{9,1},{1,9},{25,17},{17,25},{10,2},{2,... | collective-permute-start | bytes 786440 | tf_op jit(solution)/shard_map/ppermute | solution.py:230
  50.6 23.7 %collective-permute-start.3 = (bf16[384,1024]{1,0:T(8,128)(2,1)S(1)}, bf16[384,1024]{1,0:T(8,128)(2,1)S(1)}, u32[]{:S(2)}, u32[]{:S(2)}) collective-permute-start(bf16[384,1024]{1,0:T(8,128)(2,1)S(1)} %shard_map.174.refs_3_), channel_id=1, source_target_pairs={{8,0},{0,8},{24,16},{16,24},{9,1},{1,9},{25,17},{17,25},{10,2},{2,... | collective-permute-start | bytes 2359304 | tf_op jit(solution)/shard_map/ppermute | solution.py:230
  52.7 77.0 %collective-permute-start.16 = (bf16[1024,512]{1,0:T(8,128)(2,1)S(1)}, bf16[1024,512]{1,0:T(8,128)(2,1)S(1)}, u32[]{:S(2)}, u32[]{:S(2)}) collective-permute-start(bf16[1024,512]{1,0:T(8,128)(2,1)S(1)} %get-tuple-element.26.refs_6_), channel_id=1, source_target_pairs={{16,8},{8,16},{17,9},{9,17},{18,10},{10,18},{19,11},{11,19},{20,12... | collective-permute-start | bytes 3145736 | tf_op jit(solution)/shard_map/ppermute | solution.py:230
  54.2 7.0 %collective-permute-start.12 = (bf16[128,1024]{1,0:T(8,128)(2,1)S(1)}, bf16[128,1024]{1,0:T(8,128)(2,1)S(1)}, u32[]{:S(2)}, u32[]{:S(2)}) collective-permute-start(bf16[128,1024]{1,0:T(8,128)(2,1)S(1)} %get-tuple-element.24.refs_0_), channel_id=1, source_target_pairs={{16,8},{8,16},{17,9},{9,17},{18,10},{10,18},{19,11},{11,19},{20,12... | collective-permute-start | bytes 786440 | tf_op jit(solution)/shard_map/ppermute | solution.py:230
  59.8 2.1 collective-permute-start.23
  60.5 81.0 %collective-permute-start.7 = (bf16[1024,512]{1,0:T(8,128)(2,1)S(1)}, bf16[1024,512]{1,0:T(8,128)(2,1)S(1)}, u32[]{:S(2)}, u32[]{:S(2)}) collective-permute-start(bf16[1024,512]{1,0:T(8,128)(2,1)S(1)} %collective-permute-done.6.refs_7_), channel_id=1, source_target_pairs={{16,8},{8,16},{17,9},{9,17},{18,10},{10,18},{19,11},{11,19},{20,12... | collective-permute-start | bytes 3145736 | tf_op jit(solution)/shard_map/ppermute | solution.py:230
  61.2 1.4 collective-permute-start.27
  61.9 78.2 %collective-permute-start.14 = (bf16[384,1024]{1,0:T(8,128)(2,1)S(1)}, bf16[384,1024]{1,0:T(8,128)(2,1)S(1)}, u32[]{:S(2)}, u32[]{:S(2)}) collective-permute-start(bf16[384,1024]{1,0:T(8,128)(2,1)S(1)} %shard_map.174.refs_3_), channel_id=1, source_target_pairs={{16,8},{8,16},{17,9},{9,17},{18,10},{10,18},{19,11},{11,19},{20,12... | collective-permute-start | bytes 2359304 | tf_op jit(solution)/shard_map/ppermute | solution.py:230
  62.6 65.7 %collective-permute-start.21 = (bf16[256,512]{1,0:T(8,128)(2,1)S(1)}, bf16[256,512]{1,0:T(8,128)(2,1)S(1)}, u32[]{:S(2)}, u32[]{:S(2)}) collective-permute-start(bf16[256,512]{1,0:T(8,128)(2,1)S(1)} %collective-permute-done.20.refs_14_), channel_id=1, source_target_pairs={{8,0},{16,24},{9,1},{17,25},{10,2},{18,26},{11,3},{19,27},{12,4},{... | collective-permute-start | bytes 786440 | tf_op jit(solution)/shard_map/ppermute | solution.py:230
  74.3 69.7 %collective-permute-start.4 = (bf16[384,1024]{1,0:T(8,128)(2,1)S(1)}, bf16[384,1024]{1,0:T(8,128)(2,1)S(1)}, u32[]{:S(2)}, u32[]{:S(2)}) collective-permute-start(bf16[384,1024]{1,0:T(8,128)(2,1)S(1)} %collective-permute-done.3.refs_4_), channel_id=1, source_target_pairs={{16,8},{8,16},{17,9},{9,17},{18,10},{10,18},{19,11},{11,19},{20,12... | collective-permute-start | bytes 2359304 | tf_op jit(solution)/shard_map/ppermute | solution.py:230
  128.4 11.1 %collective-permute-start.25 = (bf16[256,512]{1,0:T(8,128)(2,1)S(1)}, bf16[256,512]{1,0:T(8,128)(2,1)S(1)}, u32[]{:S(2)}, u32[]{:S(2)}) collective-permute-start(bf16[256,512]{1,0:T(8,128)(2,1)S(1)} %collective-permute-done.24.refs_17_), channel_id=1, source_target_pairs={{8,0},{16,24},{9,1},{17,25},{10,2},{18,26},{11,3},{19,27},{12,4},{... | collective-permute-start | bytes 786440 | tf_op jit(solution)/shard_map/ppermute | solution.py:230
  129.7 97.7 %collective-permute-start.17 = (bf16[1024,512]{1,0:T(8,128)(2,1)S(1)}, bf16[1024,512]{1,0:T(8,128)(2,1)S(1)}, u32[]{:S(2)}, u32[]{:S(2)}) collective-permute-start(bf16[1024,512]{1,0:T(8,128)(2,1)S(1)} %collective-permute-done.16.refs_8_), channel_id=1, source_target_pairs={{8,0},{16,24},{9,1},{17,25},{10,2},{18,26},{11,3},{19,27},{12,4},{... | collective-permute-start | bytes 3145736 | tf_op jit(solution)/shard_map/ppermute | solution.py:230
  139.4 3.3 %collective-permute-start.1 = (bf16[128,1024]{1,0:T(8,128)(2,1)S(1)}, bf16[128,1024]{1,0:T(8,128)(2,1)S(1)}, u32[]{:S(2)}, u32[]{:S(2)}) collective-permute-start(bf16[128,1024]{1,0:T(8,128)(2,1)S(1)} %collective-permute-done.refs_1_), channel_id=1, source_target_pairs={{16,8},{8,16},{17,9},{9,17},{18,10},{10,18},{19,11},{11,19},{20,12... | collective-permute-start | bytes 786440 | tf_op jit(solution)/shard_map/ppermute | solution.py:230
  140.1 85.9 %collective-permute-start.15 = (bf16[384,1024]{1,0:T(8,128)(2,1)S(1)}, bf16[384,1024]{1,0:T(8,128)(2,1)S(1)}, u32[]{:S(2)}, u32[]{:S(2)}) collective-permute-start(bf16[384,1024]{1,0:T(8,128)(2,1)S(1)} %collective-permute-done.14.refs_5_), channel_id=1, source_target_pairs={{8,0},{16,24},{9,1},{17,25},{10,2},{18,26},{11,3},{19,27},{12,4},{... | collective-permute-start | bytes 2359304 | tf_op jit(solution)/shard_map/ppermute | solution.py:230
  141.4 94.4 %collective-permute-start.8 = (bf16[1024,512]{1,0:T(8,128)(2,1)S(1)}, bf16[1024,512]{1,0:T(8,128)(2,1)S(1)}, u32[]{:S(2)}, u32[]{:S(2)}) collective-permute-start(bf16[1024,512]{1,0:T(8,128)(2,1)S(1)} %collective-permute-done.7.refs_5_), channel_id=1, source_target_pairs={{8,0},{16,24},{9,1},{17,25},{10,2},{18,26},{11,3},{19,27},{12,4},{... | collective-permute-start | bytes 3145736 | tf_op jit(solution)/shard_map/ppermute | solution.py:230
  142.7 64.1 %collective-permute-start.13 = (bf16[128,1024]{1,0:T(8,128)(2,1)S(1)}, bf16[128,1024]{1,0:T(8,128)(2,1)S(1)}, u32[]{:S(2)}, u32[]{:S(2)}) collective-permute-start(bf16[128,1024]{1,0:T(8,128)(2,1)S(1)} %collective-permute-done.12.refs_2_), channel_id=1, source_target_pairs={{8,0},{16,24},{9,1},{17,25},{10,2},{18,26},{11,3},{19,27},{12,4},{... | collective-permute-start | bytes 786440 | tf_op jit(solution)/shard_map/ppermute | solution.py:230
  144.1 91.8 %collective-permute-start.5 = (bf16[384,1024]{1,0:T(8,128)(2,1)S(1)}, bf16[384,1024]{1,0:T(8,128)(2,1)S(1)}, u32[]{:S(2)}, u32[]{:S(2)}) collective-permute-start(bf16[384,1024]{1,0:T(8,128)(2,1)S(1)} %collective-permute-done.4.refs_3_), channel_id=1, source_target_pairs={{8,0},{16,24},{9,1},{17,25},{10,2},{18,26},{11,3},{19,27},{12,4},{... | collective-permute-start | bytes 2359304 | tf_op jit(solution)/shard_map/ppermute | solution.py:230
  206.8 17.9 %collective-permute-start.28 = (bf16[256,512]{1,0:T(8,128)(2,1)S(1)}, bf16[256,512]{1,0:T(8,128)(2,1)S(1)}, u32[]{:S(2)}, u32[]{:S(2)}) collective-permute-start(bf16[256,512]{1,0:T(8,128)(2,1)S(1)} %collective-permute-done.23.refs_9_), channel_id=1, source_target_pairs={{8,0},{16,24},{9,1},{17,25},{10,2},{18,26},{11,3},{19,27},{12,4},{... | collective-permute-start | bytes 786440 | tf_op jit(solution)/shard_map/ppermute | solution.py:230
  224.7 8.8 %collective-permute-start.29 = (bf16[256,512]{1,0:T(8,128)(2,1)S(1)}, bf16[256,512]{1,0:T(8,128)(2,1)S(1)}, u32[]{:S(2)}, u32[]{:S(2)}) collective-permute-start(bf16[256,512]{1,0:T(8,128)(2,1)S(1)} %collective-permute-done.27.refs_11_), channel_id=1, source_target_pairs={{8,0},{16,24},{9,1},{17,25},{10,2},{18,26},{11,3},{19,27},{12,4},{... | collective-permute-start | bytes 786440 | tf_op jit(solution)/shard_map/ppermute | solution.py:230
  226.0 9.8 %collective-permute-start.2 = (bf16[128,1024]{1,0:T(8,128)(2,1)S(1)}, bf16[128,1024]{1,0:T(8,128)(2,1)S(1)}, u32[]{:S(2)}, u32[]{:S(2)}) collective-permute-start(bf16[128,1024]{1,0:T(8,128)(2,1)S(1)} %collective-permute-done.1.refs_1_), channel_id=1, source_target_pairs={{8,0},{16,24},{9,1},{17,25},{10,2},{18,26},{11,3},{19,27},{12,4},{... | collective-permute-start | bytes 786440 | tf_op jit(solution)/shard_map/ppermute | solution.py:230
  227.3 8.5 %collective-permute-start.11 = (bf16[16,128]{1,0:T(8,128)(2,1)S(1)}, bf16[16,128]{1,0:T(8,128)(2,1)S(1)}, u32[]{:S(2)}, u32[]{:S(2)}) collective-permute-start(bf16[16,128]{1,0:T(8,128)(2,1)S(1)} %collective-permute-done.10.refs_7_), channel_id=1, source_target_pairs={{8,0},{16,24},{9,1},{17,25},{10,2},{18,26},{11,3},{19,27},{12,4},{... | collective-permute-start | bytes 12296 | tf_op jit(solution)/shard_map/ppermute | solution.py:230

commit v5 on v4

v5 whole, which is shorter than its diff:
```python
import functools

import jax
import jax.numpy as jnp
from jax import lax
from jax.experimental import pallas as pl
from jax.experimental.pallas import tpu as pltpu
from jax.sharding import PartitionSpec as P


mix_rate = 0.5
lanes = 128
sublanes = 8


in_vmem = pl.BlockSpec(memory_space=pltpu.VMEM)
in_hbm = pl.BlockSpec(memory_space=pltpu.HBM)


def blocks(total):
    size = 2 * lanes
    return [(base, min(size, total - base)) for base in range(0, total, size)]


def merge_into(out_ref, offset, total, first, w_ref, low_ref, high_ref, w_held, low_held, high_held, sems):
    copies = [
        pltpu.make_async_copy(low_ref, low_held, sems.at[0]),
        pltpu.make_async_copy(high_ref.at[:, pl.ds(first, total)], high_held, sems.at[1]),
    ]
    for j, (base, size) in enumerate(blocks(total)):
        source, target = w_ref.at[:, pl.ds(first + base, size)], w_held.at[:, pl.ds(base, size)]
        copies.append(pltpu.make_async_copy(source, target, sems.at[2 + j]))
    for copy in copies:
        copy.start()

    def finish():
        copies[0].wait()
        copies[1].wait()
        width = out_ref.shape[1]
        for (base, size), copy in zip(blocks(total), copies[2:]):
            copy.wait()
            part = pl.ds(base, size)
            delta = lax.dot_general(
                high_held[:, part],
                low_held[...],
                (((0,), (0,)), ((), ())),
                preferred_element_type=jnp.float32,
            )
            kept = w_held[:, part].T.astype(jnp.float32)
            result = (kept + mix_rate * delta).astype(jnp.bfloat16)
            for h in range(w_held.shape[0] // width):
                row = offset + h * total + base
                out_ref[pl.ds(row, size), :] = result[:, h * width : (h + 1) * width]

    return finish


def scratch_of(w, low, total):
    rows, rank = w.shape[0], low.shape[1]
    return [
        pltpu.VMEM((rows, total), jnp.bfloat16),
        pltpu.VMEM((rank, rows), jnp.bfloat16),
        pltpu.VMEM((rank, total), jnp.bfloat16),
        pltpu.SemaphoreType.DMA((2 + len(blocks(total)),)),
    ]


def hbm(*arrays):
    return [pltpu.with_memory_space_constraint(a, pltpu.HBM) for a in arrays]


def tiles(rows):
    return -(-rows // sublanes) * sublanes


merge_params = pltpu.CompilerParams(vmem_limit_bytes=12 << 20)


def merged_head(w, low, high, head):
    def body(w_ref, low_ref, high_ref, out_ref, *scratch):
        merge_into(out_ref, 0, head, 0, w_ref, low_ref, high_ref, *scratch)()

    return pl.pallas_call(
        body,
        in_specs=[in_hbm] * 3,
        out_specs=in_vmem,
        out_shape=jax.ShapeDtypeStruct((head, w.shape[0]), jnp.bfloat16),
        scratch_shapes=scratch_of(w, low, head),
        compiler_params=merge_params,
    )(*hbm(w, low.T, high))


def merged_body(mixed, query, norms, head):
    rest = mixed[0].shape[1] - head
    width = query[0].shape[0]
    below = rest * (mixed[0].shape[0] // width)
    used = norms[0].size // lanes
    held = 4

    def body(wm, lm, hm, wq, lq, hq, train, step, out_ref, row_ref, *scratch):
        finish_mixed = merge_into(out_ref, 0, rest, head, wm, lm, hm, *scratch[:held])
        finish_query = merge_into(
            out_ref, below, wq.shape[1], 0, wq, lq, hq, *scratch[held : 2 * held]
        )
        train_held, step_held, sems = scratch[2 * held :]
        copies = [
            pltpu.make_async_copy(train, train_held, sems.at[0]),
            pltpu.make_async_copy(step, step_held, sems.at[1]),
        ]
        for copy in copies:
            copy.start()
        finish_mixed()
        finish_query()
        for copy in copies:
            copy.wait()
        row_ref[...] = jnp.zeros_like(row_ref)
        row_ref[:used, :] = (train_held[...] + step_held[...]).astype(jnp.bfloat16)

    return pl.pallas_call(
        body,
        in_specs=[in_hbm] * 8,
        out_specs=[in_vmem] * 2,
        out_shape=[
            jax.ShapeDtypeStruct((below + query[0].shape[1], width), jnp.bfloat16),
            jax.ShapeDtypeStruct((tiles(used), lanes), jnp.bfloat16),
        ],
        scratch_shapes=[
            *scratch_of(mixed[0], mixed[1], rest),
            *scratch_of(query[0], query[1], query[0].shape[1]),
            *[pltpu.VMEM((used, lanes), jnp.float32)] * 2,
            pltpu.SemaphoreType.DMA((2,)),
        ],
        compiler_params=merge_params,
    )(
        *hbm(mixed[0], mixed[1].T, mixed[2], query[0], query[1].T, query[2]),
        *hbm(*(a.reshape(used, lanes) for a in norms)),
    )


def merged_tail(key, value, rows_of_cores, cores, used):
    under = key[0].shape[1] * (key[0].shape[0] // lanes)
    packed = tiles(cores * used)
    held = 4

    def body(wk, lk, hk, wv, lv, hv, rows_ref, key_ref, value_ref, *scratch):
        finish_key = merge_into(key_ref, 0, wk.shape[1], 0, wk, lk, hk, *scratch[:held])
        finish_value = merge_into(value_ref, 0, wv.shape[1], 0, wv, lv, hv, *scratch[held : 2 * held])
        packed_ref = scratch[2 * held]
        packed_ref[...] = jnp.zeros_like(packed_ref)
        rows = rows_ref[...].astype(jnp.float32)
        tall = rows.shape[0] // cores
        for core in range(cores):
            packed_ref[core * used : (core + 1) * used, :] = rows[core * tall : core * tall + used]
        key_ref[pl.ds(under, packed), :] = packed_ref[...].astype(jnp.bfloat16)
        finish_key()
        finish_value()

    return pl.pallas_call(
        body,
        in_specs=[in_hbm] * 6 + [in_vmem],
        out_specs=[in_vmem] * 2,
        out_shape=[
            jax.ShapeDtypeStruct((under + packed, lanes), jnp.bfloat16),
            jax.ShapeDtypeStruct(value[0].shape[::-1], jnp.bfloat16),
        ],
        scratch_shapes=[
            *scratch_of(key[0], key[1], key[0].shape[1]),
            *scratch_of(value[0], value[1], value[0].shape[1]),
            pltpu.VMEM((packed, lanes), jnp.float32),
        ],
        compiler_params=merge_params,
    )(*hbm(key[0], key[1].T, key[2], value[0], value[1].T, value[2]), rows_of_cores)


def place_body(count, moves, pieces_at, outs_at, *refs):
    sems = refs[-1]
    me = lax.axis_index("shard")
    sign = 1 - 2 * lax.rem(me, 2)
    for act in ("start", "wait"):
        for j, (piece, out, low, rows, tall, down, wide, right, offset) in enumerate(moves):
            owner = me + sign * offset

            @pl.when(jnp.logical_and(owner >= 0, owner < count))
            def _():
                source = refs[pieces_at + piece].at[pl.ds(low, rows)]
                row = pl.multiple_of(owner * tall + down, sublanes)
                column = pl.multiple_of(owner * wide + right, lanes)
                target = refs[outs_at + out].at[pl.ds(row, rows), pl.ds(column, source.shape[1])]
                getattr(pltpu.make_async_copy(source, target, sems.at[j]), act)()


def place(outs, shapes, pieces, count):
    targets = list(dict.fromkeys(region[0] for regions, _, _ in pieces for region in regions))
    arrays = [array for _, _, array in pieces]
    moves = [
        (j, targets.index(region[0]), *region[1:], offset)
        for j, (regions, offset, _) in enumerate(pieces)
        for region in regions
    ]
    kept = [outs[target] for target in targets if target in outs]
    placed = pl.pallas_call(
        functools.partial(place_body, count, moves, 0, len(arrays) + len(kept)),
        in_specs=[in_vmem] * len(arrays) + [in_hbm] * len(kept),
        out_specs=[in_hbm] * len(targets),
        out_shape=[jax.ShapeDtypeStruct(shapes[target], jnp.bfloat16) for target in targets],
        scratch_shapes=[pltpu.SemaphoreType.DMA((len(moves),))],
        input_output_aliases={len(arrays) + j: j for j in range(len(kept))},
        compiler_params=pltpu.CompilerParams(vmem_limit_bytes=4 << 20),
    )(*arrays, *kept)
    outs.update(zip(targets, placed))


def hops(count):
    plan = []
    for k in range(1, count):
        for name, source, parity in (("a", "b", 0), ("b", "a", 1)):
            pairs = []
            for i in range(parity, count - 1, 2):
                if i + k < count:
                    pairs.append((i + 1, i))
                if i + 1 - k >= 0:
                    pairs.append((i, i + 1))
            if pairs:
                offset = k if parity == 0 else -k
                plan.append((f"{name}{k}", f"{source}{k - 1}", pairs, offset))
    return plan


head = lanes
chunk_names = ("head", "body", "key", "value")


def groups(count):
    whole = (chunk_names,)
    return [whole] * (count - 2) + [(chunk_names[:-2], chunk_names[-2:-1], chunk_names[-1:])]


def by_line(count, cores, query, key, value, mixed, norms):
    rows, columns = query[0].shape[0], mixed[0].shape[1]
    used = norms[0].size // lanes
    packed = tiles(cores * used)
    pieces = {}
    pieces["head"] = merged_head(*mixed, head)
    pieces["body"], row = merged_body(mixed, query, norms, head)
    rows_of_cores = lax.all_gather(row, "width", axis=0, tiled=True)
    pieces["key"], pieces["value"] = merged_tail(key, value, rows_of_cores, cores, used)
    rest, halves = columns - head, mixed[0].shape[0] // rows
    wide = {name: weight[0].shape[1] for name, weight in (("query", query), ("key", key), ("value", value))}
    regions = {
        "head": [("mixed", 0, head, columns, 0, 0, 0)],
        "body": [("mixed", h * rest, rest, columns, head, 0, h * rows) for h in range(halves)]
        + [("query", halves * rest, wide["query"], 0, 0, rows, 0)],
        "key": [("key", b * wide["key"], wide["key"], 0, 0, rows, b * lanes) for b in range(rows // lanes)]
        + [("norm", wide["key"] * (rows // lanes), packed, packed, 0, 0, 0)],
        "value": [("value", 0, wide["value"], 0, 0, rows, 0)],
    }
    shapes = {name: (size, count * rows) for name, size in wide.items()}
    shapes["mixed"] = (count * columns, mixed[0].shape[0])
    shapes["norm"] = (count * packed, lanes)
    plan = hops(count)
    outs = {}
    held = {name: {"a0": piece, "b0": piece} for name, piece in pieces.items()}
    arrived = {name: [(regions[name], 0, piece)] for name, piece in pieces.items()}
    for k, parts in enumerate(groups(count), start=1):
        for hop, source, pairs, offset in plan:
            if int(hop[1:]) == k:
                for name in chunk_names:
                    held[name][hop] = lax.ppermute(held[name][source], "shard", pairs)
                    arrived[name].append((regions[name], offset, held[name][hop]))
        for part in parts:
            place(outs, shapes, [piece for name in part for piece in arrived[name]], count)
        arrived = {name: [] for name in chunk_names}
    serve_norm = outs["norm"].reshape(count, packed, lanes)[:, : cores * used].reshape(-1)
    return outs["query"], outs["key"], outs["value"], outs["mixed"], serve_norm


def by_gather(count, cores, query, key, value, mixed, norms):
    finals = []
    for axis, (w, low, high) in ((0, query), (0, key), (0, value), (1, mixed)):
        result = w.astype(jnp.float32) + mix_rate * jnp.dot(
            low, high, preferred_element_type=jnp.float32
        )
        narrow = result.astype(jnp.bfloat16)
        finals.append(lax.all_gather(narrow, "shard", axis=axis, tiled=True).T)
    norm = (norms[0] + norms[1]).astype(jnp.bfloat16)
    serve_norm = lax.all_gather(norm, ("shard", "width"), axis=0, tiled=True)
    return *finals, serve_norm


def on_device(form, count, cores, *args):
    weights = [args[3 * j : 3 * j + 3] for j in range(4)]
    return form(count, cores, *weights, args[12:])


def solution(mesh):
    column_cut = (P(("shift", "shard"), "width"), P(("shift", "shard"), None), P("shift", "width"))
    row_cut = (P(("shift", "width"), "shard"), P(("shift", "width"), None), P("shift", "shard"))
    norm = P(("shift", "shard", "width"))
    count, cores = mesh.shape["shard"], mesh.shape["width"]

    def step(*args):
        rows = args[0].shape[0] // (mesh.shape["shift"] * count)
        columns = args[9].shape[1] // count
        narrow = [args[j].shape[1] // cores for j in (0, 3, 6)]
        gains = args[12].shape[0] // (mesh.shape["shift"] * count * cores)
        aligned = all(size % (2 * lanes) == 0 for size in (rows, columns, *narrow, gains))
        tall = args[9].shape[0] // (mesh.shape["shift"] * cores)
        line = count > 2 and aligned and tall % rows == 0
        program = jax.shard_map(
            functools.partial(on_device, by_line if line else by_gather, count, cores),
            mesh=mesh,
            in_specs=(*column_cut, *column_cut, *column_cut, *row_cut, norm, norm),
            out_specs=(
                P(("shift", "width"), None),
                P(("shift", "width"), None),
                P(("shift", "width"), None),
                P("shift", "width"),
                P("shift"),
            ),
            check_vma=False,
        )
        return program(*args)

    return step
```

time: 239 us -> 188 us (0.79)
  waiting for transfers between devices: 184 us -> 106 us
  starting transfers between devices: 36.1 us -> 64.5 us
    ppermute x30 -> x20, waiting for transfers between devices: 184 us -> 106 us  [by_line(): held[name][hop] = lax.ppermute(held[name][source], 'shard', pairs)]
    ppermute x30 -> x20, starting transfers between devices: 36.1 us -> 64.5 us  [by_line(): held[name][hop] = lax.ppermute(held[name][source], 'shard', pairs)]
  transfers between devices with their start and end apart: 30 -> 20, of which waited for: 10 -> 8; matrix products, arithmetic and copies ran while one was open for 0% -> 0% of each run, Pallas kernels for 4% -> 5%
where the time goes in v5:
time: 188 us; the launch traced here: 187 us
  waiting for transfers between devices  106 us (56%)
  starting transfers between devices  64.5 us (34%)
  Pallas kernels  13 us (7%)
    ppermute x20, waiting for transfers between devices, by_line(): held[name][hop] = lax.ppermute(held[name][source], 'shard', pairs)  106 us
    ppermute x20, starting transfers between devices, by_line(): held[name][hop] = lax.ppermute(held[name][source], 'shard', pairs)  64.5 us
    pallas_call x5, Pallas kernels, place(): pl.pallas_call(functools.partial(place_body, count, moves, 0, len(arrays)...  7.1 us
  transfers between devices with their start and end apart: 20, of which 8 were waited for; matrix products, arithmetic and copies ran while one was open for 0% of the time, Pallas kernels for 5%

profile of v5, /device:TPU:0, one launch (start us, length us, event | category | flops | bytes accessed | tf_op | source)
XLA Modules:
  0.0 187.1 jit_solution(5093559283030350535)
XLA Ops:
  0.6 3.1 %shard_map.174 = (bf16[1792,512]{1,0:T(8,128)(2,1)S(1)}, bf16[8,128]{1,0:T(8,128)(2,1)S(1)}) custom-call(bf16[1024,512]{1,0:T(8,128)(2,1)} %wm.1, bf16[16,1024]{1,0:T(8,128)(2,1)} %bitcast.9, bf16[16,512]{1,0:T(8,128)(2,1)} %hm.1, bf16[512,1024]{1,0:T(8,128)(2,1)} %wq.1, bf16[16,512]{1,0:T(8,128)(2,1)} %bitcast.11, bf16[16,1024]{1,0:T(8,128)(2,1)} %hq.1, ...), custom_call_target="tpu_custom_call" | custom-call | tf_op jit(solution)/shard_map/pallas_call | solution.py:119
  3.7 3.1 %collective-permute-start.3 = (bf16[1792,512]{1,0:T(8,128)(2,1)S(1)}, bf16[1792,512]{1,0:T(8,128)(2,1)S(1)}, u32[]{:S(2)}, u32[]{:S(2)}) collective-permute-start(bf16[1792,512]{1,0:T(8,128)(2,1)S(1)} %get-tuple-element.23.refs_3_), channel_id=1, source_target_pairs={{8,0},{0,8},{24,16},{16,24},{9,1},{1,9},{25,17},{17,25},{10,2},{2,... | collective-permute-start | bytes 5505032 | tf_op jit(solution)/shard_map/ppermute | solution.py:268
  6.8 0.8 collective-permute-start.8
  7.6 39.2 %collective-permute-done.3.refs_4_ = bf16[1792,512]{1,0:T(8,128)(2,1)S(1)} collective-permute-done((bf16[1792,512]{1,0:T(8,128)(2,1)S(1)}, bf16[1792,512]{1,0:T(8,128)(2,1)S(1)}, u32[]{:S(2)}, u32[]{:S(2)}) %collective-permute-start.3) | collective-permute-done | bytes 1835040 | tf_op jit(solution)/shard_map/ppermute | solution.py:268
  46.8 0.8 collective-permute-start.4
  47.6 1.3 collective-permute-start.9
  48.9 1.3 collective-permute-start.5
  50.2 1.8 all_gather.3.rows_ref
  52.1 1.6 shard_map.175
  53.7 0.7 collective-permute-start.14
  54.4 45.4 %collective-permute-start.16 = (bf16[256,512]{1,0:T(8,128)(2,1)S(1)}, bf16[256,512]{1,0:T(8,128)(2,1)S(1)}, u32[]{:S(2)}, u32[]{:S(2)}) collective-permute-start(bf16[256,512]{1,0:T(8,128)(2,1)S(1)} %get-tuple-element.26.refs_9_), channel_id=1, source_target_pairs={{8,0},{0,8},{24,16},{16,24},{9,1},{1,9},{25,17},{17,25},{10,2},{2,... | collective-permute-start | bytes 786440 | tf_op jit(solution)/shard_map/ppermute | solution.py:268
  99.8 1.3 shard_map.173.refs_0_
  101.1 0.7 collective-permute-start.6
  101.8 37.3 %collective-permute-done.16.refs_10_ = bf16[256,512]{1,0:T(8,128)(2,1)S(1)} collective-permute-done((bf16[256,512]{1,0:T(8,128)(2,1)S(1)}, bf16[256,512]{1,0:T(8,128)(2,1)S(1)}, u32[]{:S(2)}, u32[]{:S(2)}) %collective-permute-start.16) | collective-permute-done | bytes 262176 | tf_op jit(solution)/shard_map/ppermute | solution.py:268
  139.8 3.0 %collective-permute-done.refs_1_ = bf16[128,1024]{1,0:T(8,128)(2,1)S(1)} collective-permute-done((bf16[128,1024]{1,0:T(8,128)(2,1)S(1)}, bf16[128,1024]{1,0:T(8,128)(2,1)S(1)}, u32[]{:S(2)}, u32[]{:S(2)}) %collective-permute-start) | collective-permute-done | bytes 262176 | tf_op jit(solution)/shard_map/ppermute | solution.py:268
  143.5 1.3 collective-permute-start.15
  144.8 6.2 %collective-permute-done.12.refs_7_ = bf16[1032,128]{1,0:T(8,128)(2,1)S(1)} collective-permute-done((bf16[1032,128]{1,0:T(8,128)(2,1)S(1)}, bf16[1032,128]{1,0:T(8,128)(2,1)S(1)}, u32[]{:S(2)}, u32[]{:S(2)}) %collective-permute-start.12) | collective-permute-done | bytes 264224 | tf_op jit(solution)/shard_map/ppermute | solution.py:268
  151.6 0.7 collective-permute-start.13
  152.3 2.5 %collective-permute-done.15.refs_6_ = bf16[256,512]{1,0:T(8,128)(2,1)S(1)} collective-permute-done((bf16[256,512]{1,0:T(8,128)(2,1)S(1)}, bf16[256,512]{1,0:T(8,128)(2,1)S(1)}, u32[]{:S(2)}, u32[]{:S(2)}) %collective-permute-start.15) | collective-permute-done | bytes 262176 | tf_op jit(solution)/shard_map/ppermute | solution.py:268
  154.8 1.3 collective-permute-start.11
  156.1 1.3 collective-permute-start.7
  157.4 1.3 collective-permute-start.18
  158.7 13.8 %collective-permute-done.7.refs_0_ = bf16[128,1024]{1,0:T(8,128)(2,1)S(1)} collective-permute-done((bf16[128,1024]{1,0:T(8,128)(2,1)S(1)}, bf16[128,1024]{1,0:T(8,128)(2,1)S(1)}, u32[]{:S(2)}, u32[]{:S(2)}) %collective-permute-start.7) | collective-permute-done | bytes 262176 | tf_op jit(solution)/shard_map/ppermute | solution.py:268
  172.5 1.3 collective-permute-start.19
  173.7 1.3 collective-permute-start.2
  175.0 2.6 %shard_map.176 = (bf16[2048,1024]{1,0:T(8,128)(2,1)}, bf16[1024,2048]{1,0:T(8,128)(2,1)}, bf16[256,2048]{1,0:T(8,128)(2,1)}, bf16[32,128]{1,0:T(8,128)(2,1)S(1)}, bf16[256,2048]{1,0:T(8,128)(2,1)}) custom-call(bf16[128,1024]{1,0:T(8,128)(2,1)S(1)} %shard_map.173.refs_0_, bf16[128,1024]{1,0:T(8,128)(2,1)S(1)} %collective-permute-done.refs_1_, ...), custom_call_target="tpu_custom_call" | custom-call | tf_op jit(solution)/shard_map/pallas_call | solution.py:201
  177.7 1.7 shard_map.177
  179.4 0.8 shard_map.179
  180.7 2.2 %collective-permute-done.19.refs_0_ = bf16[256,512]{1,0:T(8,128)(2,1)S(1)} collective-permute-done((bf16[256,512]{1,0:T(8,128)(2,1)S(1)}, bf16[256,512]{1,0:T(8,128)(2,1)S(1)}, u32[]{:S(2)}, u32[]{:S(2)}) %collective-permute-start.19) | collective-permute-done | bytes 262176 | tf_op jit(solution)/shard_map/ppermute | solution.py:268
  182.9 0.7 shard_map.180
  183.7 2.1 %collective-permute-done.2.refs_0_ = bf16[128,1024]{1,0:T(8,128)(2,1)S(1)} collective-permute-done((bf16[128,1024]{1,0:T(8,128)(2,1)S(1)}, bf16[128,1024]{1,0:T(8,128)(2,1)S(1)}, u32[]{:S(2)}, u32[]{:S(2)}) %collective-permute-start.2) | collective-permute-done | bytes 262176 | tf_op jit(solution)/shard_map/ppermute | solution.py:268
  185.8 1.3 shard_map.178
  (18 shorter events, 2.7 us)
Async XLA Ops:
  3.7 43.1 %collective-permute-start.3 = (bf16[1792,512]{1,0:T(8,128)(2,1)S(1)}, bf16[1792,512]{1,0:T(8,128)(2,1)S(1)}, u32[]{:S(2)}, u32[]{:S(2)}) collective-permute-start(bf16[1792,512]{1,0:T(8,128)(2,1)S(1)} %get-tuple-element.23.refs_3_), channel_id=1, source_target_pairs={{8,0},{0,8},{24,16},{16,24},{9,1},{1,9},{25,17},{17,25},{10,2},{2,... | collective-permute-start | bytes 5505032 | tf_op jit(solution)/shard_map/ppermute | solution.py:268
  6.8 40.8 %collective-permute-start.8 = (bf16[1792,512]{1,0:T(8,128)(2,1)S(1)}, bf16[1792,512]{1,0:T(8,128)(2,1)S(1)}, u32[]{:S(2)}, u32[]{:S(2)}) collective-permute-start(bf16[1792,512]{1,0:T(8,128)(2,1)S(1)} %get-tuple-element.23.refs_3_), channel_id=1, source_target_pairs={{16,8},{8,16},{17,9},{9,17},{18,10},{10,18},{19,11},{11,19},{20,12... | collective-permute-start | bytes 5505032 | tf_op jit(solution)/shard_map/ppermute | solution.py:268
  46.8 2.1 %collective-permute-start.4 = (bf16[1792,512]{1,0:T(8,128)(2,1)S(1)}, bf16[1792,512]{1,0:T(8,128)(2,1)S(1)}, u32[]{:S(2)}, u32[]{:S(2)}) collective-permute-start(bf16[1792,512]{1,0:T(8,128)(2,1)S(1)} %collective-permute-done.3.refs_4_), channel_id=1, source_target_pairs={{16,8},{8,16},{17,9},{9,17},{18,10},{10,18},{19,11},{11,19},{20,12... | collective-permute-start | bytes 5505032 | tf_op jit(solution)/shard_map/ppermute | solution.py:268
  47.6 130.0 %collective-permute-start.9 = (bf16[1792,512]{1,0:T(8,128)(2,1)S(1)}, bf16[1792,512]{1,0:T(8,128)(2,1)S(1)}, u32[]{:S(2)}, u32[]{:S(2)}) collective-permute-start(bf16[1792,512]{1,0:T(8,128)(2,1)S(1)} %collective-permute-done.8.refs_5_), channel_id=1, source_target_pairs={{8,0},{16,24},{9,1},{17,25},{10,2},{18,26},{11,3},{19,27},{12,4},{... | collective-permute-start | bytes 5505032 | tf_op jit(solution)/shard_map/ppermute | solution.py:268
  48.9 136.8 %collective-permute-start.5 = (bf16[1792,512]{1,0:T(8,128)(2,1)S(1)}, bf16[1792,512]{1,0:T(8,128)(2,1)S(1)}, u32[]{:S(2)}, u32[]{:S(2)}) collective-permute-start(bf16[1792,512]{1,0:T(8,128)(2,1)S(1)} %collective-permute-done.4.refs_3_), channel_id=1, source_target_pairs={{8,0},{16,24},{9,1},{17,25},{10,2},{18,26},{11,3},{19,27},{12,4},{... | collective-permute-start | bytes 5505032 | tf_op jit(solution)/shard_map/ppermute | solution.py:268
  53.7 47.4 %collective-permute-start.14 = (bf16[256,512]{1,0:T(8,128)(2,1)S(1)}, bf16[256,512]{1,0:T(8,128)(2,1)S(1)}, u32[]{:S(2)}, u32[]{:S(2)}) collective-permute-start(bf16[256,512]{1,0:T(8,128)(2,1)S(1)} %get-tuple-element.26.refs_9_), channel_id=1, source_target_pairs={{16,8},{8,16},{17,9},{9,17},{18,10},{10,18},{19,11},{11,19},{20,12... | collective-permute-start | bytes 786440 | tf_op jit(solution)/shard_map/ppermute | solution.py:268
  54.4 84.7 %collective-permute-start.16 = (bf16[256,512]{1,0:T(8,128)(2,1)S(1)}, bf16[256,512]{1,0:T(8,128)(2,1)S(1)}, u32[]{:S(2)}, u32[]{:S(2)}) collective-permute-start(bf16[256,512]{1,0:T(8,128)(2,1)S(1)} %get-tuple-element.26.refs_9_), channel_id=1, source_target_pairs={{8,0},{0,8},{24,16},{16,24},{9,1},{1,9},{25,17},{17,25},{10,2},{2,... | collective-permute-start | bytes 786440 | tf_op jit(solution)/shard_map/ppermute | solution.py:268
  101.0 41.7 %collective-permute-start = (bf16[128,1024]{1,0:T(8,128)(2,1)S(1)}, bf16[128,1024]{1,0:T(8,128)(2,1)S(1)}, u32[]{:S(2)}, u32[]{:S(2)}) collective-permute-start(bf16[128,1024]{1,0:T(8,128)(2,1)S(1)} %shard_map.173.refs_0_), channel_id=1, source_target_pairs={{8,0},{0,8},{24,16},{16,24},{9,1},{1,9},{25,17},{17,25},{10,2},{2,... | collective-permute-start | bytes 786440 | tf_op jit(solution)/shard_map/ppermute | solution.py:268
  101.1 41.6 %collective-permute-start.6 = (bf16[128,1024]{1,0:T(8,128)(2,1)S(1)}, bf16[128,1024]{1,0:T(8,128)(2,1)S(1)}, u32[]{:S(2)}, u32[]{:S(2)}) collective-permute-start(bf16[128,1024]{1,0:T(8,128)(2,1)S(1)} %shard_map.173.refs_0_), channel_id=1, source_target_pairs={{16,8},{8,16},{17,9},{9,17},{18,10},{10,18},{19,11},{11,19},{20,12... | collective-permute-start | bytes 786440 | tf_op jit(solution)/shard_map/ppermute | solution.py:268
  139.1 4.3 %collective-permute-start.10 = (bf16[1032,128]{1,0:T(8,128)(2,1)S(1)}, bf16[1032,128]{1,0:T(8,128)(2,1)S(1)}, u32[]{:S(2)}, u32[]{:S(2)}) collective-permute-start(bf16[1032,128]{1,0:T(8,128)(2,1)S(1)} %get-tuple-element.25.refs_6_), channel_id=1, source_target_pairs={{16,8},{8,16},{17,9},{9,17},{18,10},{10,18},{19,11},{11,19},{20,12... | collective-permute-start | bytes 792584 | tf_op jit(solution)/shard_map/ppermute | solution.py:268
  142.8 8.2 %collective-permute-start.12 = (bf16[1032,128]{1,0:T(8,128)(2,1)S(1)}, bf16[1032,128]{1,0:T(8,128)(2,1)S(1)}, u32[]{:S(2)}, u32[]{:S(2)}) collective-permute-start(bf16[1032,128]{1,0:T(8,128)(2,1)S(1)} %get-tuple-element.25.refs_6_), channel_id=1, source_target_pairs={{8,0},{0,8},{24,16},{16,24},{9,1},{1,9},{25,17},{17,25},{10,2},{2,... | collective-permute-start | bytes 792584 | tf_op jit(solution)/shard_map/ppermute | solution.py:268
  142.8 8.9 %collective-permute-start.17 = (bf16[256,512]{1,0:T(8,128)(2,1)S(1)}, bf16[256,512]{1,0:T(8,128)(2,1)S(1)}, u32[]{:S(2)}, u32[]{:S(2)}) collective-permute-start(bf16[256,512]{1,0:T(8,128)(2,1)S(1)} %collective-permute-done.16.refs_10_), channel_id=1, source_target_pairs={{16,8},{8,16},{17,9},{9,17},{18,10},{10,18},{19,11},{11,19},{20,12... | collective-permute-start | bytes 786440 | tf_op jit(solution)/shard_map/ppermute | solution.py:268
  143.5 11.3 %collective-permute-start.15 = (bf16[256,512]{1,0:T(8,128)(2,1)S(1)}, bf16[256,512]{1,0:T(8,128)(2,1)S(1)}, u32[]{:S(2)}, u32[]{:S(2)}) collective-permute-start(bf16[256,512]{1,0:T(8,128)(2,1)S(1)} %collective-permute-done.14.refs_11_), channel_id=1, source_target_pairs={{8,0},{16,24},{9,1},{17,25},{10,2},{18,26},{11,3},{19,27},{12,4},{... | collective-permute-start | bytes 786440 | tf_op jit(solution)/shard_map/ppermute | solution.py:268
  151.0 5.1 %collective-permute-start.1 = (bf16[128,1024]{1,0:T(8,128)(2,1)S(1)}, bf16[128,1024]{1,0:T(8,128)(2,1)S(1)}, u32[]{:S(2)}, u32[]{:S(2)}) collective-permute-start(bf16[128,1024]{1,0:T(8,128)(2,1)S(1)} %collective-permute-done.refs_1_), channel_id=1, source_target_pairs={{16,8},{8,16},{17,9},{9,17},{18,10},{10,18},{19,11},{11,19},{20,12... | collective-permute-start | bytes 786440 | tf_op jit(solution)/shard_map/ppermute | solution.py:268
  151.6 5.7 %collective-permute-start.13 = (bf16[1032,128]{1,0:T(8,128)(2,1)S(1)}, bf16[1032,128]{1,0:T(8,128)(2,1)S(1)}, u32[]{:S(2)}, u32[]{:S(2)}) collective-permute-start(bf16[1032,128]{1,0:T(8,128)(2,1)S(1)} %collective-permute-done.12.refs_7_), channel_id=1, source_target_pairs={{16,8},{8,16},{17,9},{9,17},{18,10},{10,18},{19,11},{11,19},{20,12... | collective-permute-start | bytes 792584 | tf_op jit(solution)/shard_map/ppermute | solution.py:268
  154.8 19.0 %collective-permute-start.11 = (bf16[1032,128]{1,0:T(8,128)(2,1)S(1)}, bf16[1032,128]{1,0:T(8,128)(2,1)S(1)}, u32[]{:S(2)}, u32[]{:S(2)}) collective-permute-start(bf16[1032,128]{1,0:T(8,128)(2,1)S(1)} %collective-permute-done.10.refs_8_), channel_id=1, source_target_pairs={{8,0},{16,24},{9,1},{17,25},{10,2},{18,26},{11,3},{19,27},{12,4},{... | collective-permute-start | bytes 792584 | tf_op jit(solution)/shard_map/ppermute | solution.py:268
  156.1 16.4 %collective-permute-start.7 = (bf16[128,1024]{1,0:T(8,128)(2,1)S(1)}, bf16[128,1024]{1,0:T(8,128)(2,1)S(1)}, u32[]{:S(2)}, u32[]{:S(2)}) collective-permute-start(bf16[128,1024]{1,0:T(8,128)(2,1)S(1)} %collective-permute-done.6.refs_2_), channel_id=1, source_target_pairs={{8,0},{16,24},{9,1},{17,25},{10,2},{18,26},{11,3},{19,27},{12,4},{... | collective-permute-start | bytes 786440 | tf_op jit(solution)/shard_map/ppermute | solution.py:268
  157.4 22.0 %collective-permute-start.18 = (bf16[1032,128]{1,0:T(8,128)(2,1)S(1)}, bf16[1032,128]{1,0:T(8,128)(2,1)S(1)}, u32[]{:S(2)}, u32[]{:S(2)}) collective-permute-start(bf16[1032,128]{1,0:T(8,128)(2,1)S(1)} %collective-permute-done.13.refs_5_), channel_id=1, source_target_pairs={{8,0},{16,24},{9,1},{17,25},{10,2},{18,26},{11,3},{19,27},{12,4},{... | collective-permute-start | bytes 792584 | tf_op jit(solution)/shard_map/ppermute | solution.py:268
  172.5 10.5 %collective-permute-start.19 = (bf16[256,512]{1,0:T(8,128)(2,1)S(1)}, bf16[256,512]{1,0:T(8,128)(2,1)S(1)}, u32[]{:S(2)}, u32[]{:S(2)}) collective-permute-start(bf16[256,512]{1,0:T(8,128)(2,1)S(1)} %collective-permute-done.17.refs_7_), channel_id=1, source_target_pairs={{8,0},{16,24},{9,1},{17,25},{10,2},{18,26},{11,3},{19,27},{12,4},{... | collective-permute-start | bytes 786440 | tf_op jit(solution)/shard_map/ppermute | solution.py:268
  173.7 12.0 %collective-permute-start.2 = (bf16[128,1024]{1,0:T(8,128)(2,1)S(1)}, bf16[128,1024]{1,0:T(8,128)(2,1)S(1)}, u32[]{:S(2)}, u32[]{:S(2)}) collective-permute-start(bf16[128,1024]{1,0:T(8,128)(2,1)S(1)} %collective-permute-done.1.refs_1_), channel_id=1, source_target_pairs={{8,0},{16,24},{9,1},{17,25},{10,2},{18,26},{11,3},{19,27},{12,4},{... | collective-permute-start | bytes 786440 | tf_op jit(solution)/shard_map/ppermute | solution.py:268

commit v6 on v5

--- a/solution.py
+++ b/solution.py
@@ -77,15 +77,44 @@
 
 
 def merged_head(w, low, high, head):
-    def body(w_ref, low_ref, high_ref, out_ref, *scratch):
-        merge_into(out_ref, 0, head, 0, w_ref, low_ref, high_ref, *scratch)()
+    rows, rank = w.shape[0], low.shape[1]
+    count = 4 if rows % (4 * lanes) == 0 else 1
+    parts = [pl.ds(j * (rows // count), rows // count) for j in range(count)]
+    ahead = pl.ds(0, head)
+
+    def body(w_ref, low_ref, high_ref, out_ref, w_held, low_held, high_held, sems):
+        copies = [
+            pltpu.make_async_copy(w_ref.at[part, ahead], w_held.at[part], sems.at[j])
+            for j, part in enumerate(parts)
+        ]
+        copies.append(pltpu.make_async_copy(low_ref, low_held, sems.at[count]))
+        copies.append(pltpu.make_async_copy(high_ref.at[:, ahead], high_held, sems.at[count + 1]))
+        for copy in copies:
+            copy.start()
+        copies[-1].wait()
+        copies[-2].wait()
+        for part, copy in zip(parts, copies):
+            delta = lax.dot_general(
+                high_held[...],
+                low_held[:, part],
+                (((0,), (0,)), ((), ())),
+                preferred_element_type=jnp.float32,
+            )
+            copy.wait()
+            kept = w_held[part, :].T.astype(jnp.float32)
+            out_ref[:, part] = (kept + mix_rate * delta).astype(jnp.bfloat16)
 
     return pl.pallas_call(
         body,
         in_specs=[in_hbm] * 3,
         out_specs=in_vmem,
-        out_shape=jax.ShapeDtypeStruct((head, w.shape[0]), jnp.bfloat16),
-        scratch_shapes=scratch_of(w, low, head),
+        out_shape=jax.ShapeDtypeStruct((head, rows), jnp.bfloat16),
+        scratch_shapes=[
+            pltpu.VMEM((rows, head), jnp.bfloat16),
+            pltpu.VMEM((rank, rows), jnp.bfloat16),
+            pltpu.VMEM((rank, head), jnp.bfloat16),
+            pltpu.SemaphoreType.DMA((count + 2,)),
+        ],
         compiler_params=merge_params,
     )(*hbm(w, low.T, high))
 

time: 188 us -> 188 us (level)
  no operation moved by 1% of the time
where the time goes in v6:
time: 188 us; the launch traced here: 187 us
  waiting for transfers between devices  106 us (56%)
  starting transfers between devices  64.5 us (34%)
  Pallas kernels  13.6 us (7%)
    ppermute x20, waiting for transfers between devices, by_line(): held[name][hop] = lax.ppermute(held[name][source], 'shard', pairs)  106 us
    ppermute x20, starting transfers between devices, by_line(): held[name][hop] = lax.ppermute(held[name][source], 'shard', pairs)  64.5 us
    pallas_call x5, Pallas kernels, place(): pl.pallas_call(functools.partial(place_body, count, moves, 0, len(arrays)...  7.1 us
  transfers between devices with their start and end apart: 20, of which 8 were waited for; matrix products, arithmetic and copies ran while one was open for 0% of the time, Pallas kernels for 5%

profile of v6, /device:TPU:0, one launch (start us, length us, event | category | flops | bytes accessed | tf_op | source)
XLA Modules:
  0.0 187.1 jit_solution(13310034219084434258)
XLA Ops:
  0.6 3.1 %shard_map.174 = (bf16[1792,512]{1,0:T(8,128)(2,1)S(1)}, bf16[8,128]{1,0:T(8,128)(2,1)S(1)}) custom-call(bf16[1024,512]{1,0:T(8,128)(2,1)} %wm.1, bf16[16,1024]{1,0:T(8,128)(2,1)} %bitcast.9, bf16[16,512]{1,0:T(8,128)(2,1)} %hm.1, bf16[512,1024]{1,0:T(8,128)(2,1)} %wq.1, bf16[16,512]{1,0:T(8,128)(2,1)} %bitcast.11, bf16[16,1024]{1,0:T(8,128)(2,1)} %hq.1, ...), custom_call_target="tpu_custom_call" | custom-call | tf_op jit(solution)/shard_map/pallas_call | solution.py:148
  3.7 3.1 %collective-permute-start.3 = (bf16[1792,512]{1,0:T(8,128)(2,1)S(1)}, bf16[1792,512]{1,0:T(8,128)(2,1)S(1)}, u32[]{:S(2)}, u32[]{:S(2)}) collective-permute-start(bf16[1792,512]{1,0:T(8,128)(2,1)S(1)} %get-tuple-element.23.refs_3_), channel_id=1, source_target_pairs={{8,0},{0,8},{24,16},{16,24},{9,1},{1,9},{25,17},{17,25},{10,2},{2,... | collective-permute-start | bytes 5505032 | tf_op jit(solution)/shard_map/ppermute | solution.py:297
  6.8 0.8 collective-permute-start.8
  7.6 39.2 %collective-permute-done.3.refs_4_ = bf16[1792,512]{1,0:T(8,128)(2,1)S(1)} collective-permute-done((bf16[1792,512]{1,0:T(8,128)(2,1)S(1)}, bf16[1792,512]{1,0:T(8,128)(2,1)S(1)}, u32[]{:S(2)}, u32[]{:S(2)}) %collective-permute-start.3) | collective-permute-done | bytes 1835040 | tf_op jit(solution)/shard_map/ppermute | solution.py:297
  46.8 0.8 collective-permute-start.4
  47.6 1.3 collective-permute-start.9
  48.9 1.3 collective-permute-start.5
  50.2 1.8 all_gather.3.rows_ref
  52.1 1.6 shard_map.175
  53.7 0.7 collective-permute-start.14
  54.4 45.4 %collective-permute-start.16 = (bf16[256,512]{1,0:T(8,128)(2,1)S(1)}, bf16[256,512]{1,0:T(8,128)(2,1)S(1)}, u32[]{:S(2)}, u32[]{:S(2)}) collective-permute-start(bf16[256,512]{1,0:T(8,128)(2,1)S(1)} %get-tuple-element.26.refs_9_), channel_id=1, source_target_pairs={{8,0},{0,8},{24,16},{16,24},{9,1},{1,9},{25,17},{17,25},{10,2},{2,... | collective-permute-start | bytes 786440 | tf_op jit(solution)/shard_map/ppermute | solution.py:297
  99.8 1.8 shard_map.173.refs_0_
  101.7 0.7 collective-permute-start.6
  102.4 36.7 %collective-permute-done.16.refs_10_ = bf16[256,512]{1,0:T(8,128)(2,1)S(1)} collective-permute-done((bf16[256,512]{1,0:T(8,128)(2,1)S(1)}, bf16[256,512]{1,0:T(8,128)(2,1)S(1)}, u32[]{:S(2)}, u32[]{:S(2)}) %collective-permute-start.16) | collective-permute-done | bytes 262176 | tf_op jit(solution)/shard_map/ppermute | solution.py:297
  139.8 3.0 %collective-permute-done.refs_1_ = bf16[128,1024]{1,0:T(8,128)(2,1)S(1)} collective-permute-done((bf16[128,1024]{1,0:T(8,128)(2,1)S(1)}, bf16[128,1024]{1,0:T(8,128)(2,1)S(1)}, u32[]{:S(2)}, u32[]{:S(2)}) %collective-permute-start) | collective-permute-done | bytes 262176 | tf_op jit(solution)/shard_map/ppermute | solution.py:297
  143.5 1.3 collective-permute-start.15
  144.8 6.2 %collective-permute-done.12.refs_7_ = bf16[1032,128]{1,0:T(8,128)(2,1)S(1)} collective-permute-done((bf16[1032,128]{1,0:T(8,128)(2,1)S(1)}, bf16[1032,128]{1,0:T(8,128)(2,1)S(1)}, u32[]{:S(2)}, u32[]{:S(2)}) %collective-permute-start.12) | collective-permute-done | bytes 264224 | tf_op jit(solution)/shard_map/ppermute | solution.py:297
  151.6 0.7 collective-permute-start.13
  152.3 2.5 %collective-permute-done.15.refs_6_ = bf16[256,512]{1,0:T(8,128)(2,1)S(1)} collective-permute-done((bf16[256,512]{1,0:T(8,128)(2,1)S(1)}, bf16[256,512]{1,0:T(8,128)(2,1)S(1)}, u32[]{:S(2)}, u32[]{:S(2)}) %collective-permute-start.15) | collective-permute-done | bytes 262176 | tf_op jit(solution)/shard_map/ppermute | solution.py:297
  154.8 1.3 collective-permute-start.11
  156.1 1.3 collective-permute-start.7
  157.4 1.3 collective-permute-start.18
  158.7 13.8 %collective-permute-done.7.refs_0_ = bf16[128,1024]{1,0:T(8,128)(2,1)S(1)} collective-permute-done((bf16[128,1024]{1,0:T(8,128)(2,1)S(1)}, bf16[128,1024]{1,0:T(8,128)(2,1)S(1)}, u32[]{:S(2)}, u32[]{:S(2)}) %collective-permute-start.7) | collective-permute-done | bytes 262176 | tf_op jit(solution)/shard_map/ppermute | solution.py:297
  172.5 1.3 collective-permute-start.19
  173.7 1.3 collective-permute-start.2
  175.0 2.6 %shard_map.176 = (bf16[2048,1024]{1,0:T(8,128)(2,1)}, bf16[1024,2048]{1,0:T(8,128)(2,1)}, bf16[256,2048]{1,0:T(8,128)(2,1)}, bf16[32,128]{1,0:T(8,128)(2,1)S(1)}, bf16[256,2048]{1,0:T(8,128)(2,1)}) custom-call(bf16[128,1024]{1,0:T(8,128)(2,1)S(1)} %shard_map.173.refs_0_, bf16[128,1024]{1,0:T(8,128)(2,1)S(1)} %collective-permute-done.refs_1_, ...), custom_call_target="tpu_custom_call" | custom-call | tf_op jit(solution)/shard_map/pallas_call | solution.py:230
  177.7 1.7 shard_map.177
  179.4 0.8 shard_map.179
  180.7 2.2 %collective-permute-done.19.refs_0_ = bf16[256,512]{1,0:T(8,128)(2,1)S(1)} collective-permute-done((bf16[256,512]{1,0:T(8,128)(2,1)S(1)}, bf16[256,512]{1,0:T(8,128)(2,1)S(1)}, u32[]{:S(2)}, u32[]{:S(2)}) %collective-permute-start.19) | collective-permute-done | bytes 262176 | tf_op jit(solution)/shard_map/ppermute | solution.py:297
  182.9 0.7 shard_map.180
  183.7 2.1 %collective-permute-done.2.refs_0_ = bf16[128,1024]{1,0:T(8,128)(2,1)S(1)} collective-permute-done((bf16[128,1024]{1,0:T(8,128)(2,1)S(1)}, bf16[128,1024]{1,0:T(8,128)(2,1)S(1)}, u32[]{:S(2)}, u32[]{:S(2)}) %collective-permute-start.2) | collective-permute-done | bytes 262176 | tf_op jit(solution)/shard_map/ppermute | solution.py:297
  185.8 1.3 shard_map.178
  (18 shorter events, 2.7 us)
Async XLA Ops:
  3.7 43.1 %collective-permute-start.3 = (bf16[1792,512]{1,0:T(8,128)(2,1)S(1)}, bf16[1792,512]{1,0:T(8,128)(2,1)S(1)}, u32[]{:S(2)}, u32[]{:S(2)}) collective-permute-start(bf16[1792,512]{1,0:T(8,128)(2,1)S(1)} %get-tuple-element.23.refs_3_), channel_id=1, source_target_pairs={{8,0},{0,8},{24,16},{16,24},{9,1},{1,9},{25,17},{17,25},{10,2},{2,... | collective-permute-start | bytes 5505032 | tf_op jit(solution)/shard_map/ppermute | solution.py:297
  6.8 40.8 %collective-permute-start.8 = (bf16[1792,512]{1,0:T(8,128)(2,1)S(1)}, bf16[1792,512]{1,0:T(8,128)(2,1)S(1)}, u32[]{:S(2)}, u32[]{:S(2)}) collective-permute-start(bf16[1792,512]{1,0:T(8,128)(2,1)S(1)} %get-tuple-element.23.refs_3_), channel_id=1, source_target_pairs={{16,8},{8,16},{17,9},{9,17},{18,10},{10,18},{19,11},{11,19},{20,12... | collective-permute-start | bytes 5505032 | tf_op jit(solution)/shard_map/ppermute | solution.py:297
  46.8 2.1 %collective-permute-start.4 = (bf16[1792,512]{1,0:T(8,128)(2,1)S(1)}, bf16[1792,512]{1,0:T(8,128)(2,1)S(1)}, u32[]{:S(2)}, u32[]{:S(2)}) collective-permute-start(bf16[1792,512]{1,0:T(8,128)(2,1)S(1)} %collective-permute-done.3.refs_4_), channel_id=1, source_target_pairs={{16,8},{8,16},{17,9},{9,17},{18,10},{10,18},{19,11},{11,19},{20,12... | collective-permute-start | bytes 5505032 | tf_op jit(solution)/shard_map/ppermute | solution.py:297
  47.6 130.0 %collective-permute-start.9 = (bf16[1792,512]{1,0:T(8,128)(2,1)S(1)}, bf16[1792,512]{1,0:T(8,128)(2,1)S(1)}, u32[]{:S(2)}, u32[]{:S(2)}) collective-permute-start(bf16[1792,512]{1,0:T(8,128)(2,1)S(1)} %collective-permute-done.8.refs_5_), channel_id=1, source_target_pairs={{8,0},{16,24},{9,1},{17,25},{10,2},{18,26},{11,3},{19,27},{12,4},{... | collective-permute-start | bytes 5505032 | tf_op jit(solution)/shard_map/ppermute | solution.py:297
  48.9 136.8 %collective-permute-start.5 = (bf16[1792,512]{1,0:T(8,128)(2,1)S(1)}, bf16[1792,512]{1,0:T(8,128)(2,1)S(1)}, u32[]{:S(2)}, u32[]{:S(2)}) collective-permute-start(bf16[1792,512]{1,0:T(8,128)(2,1)S(1)} %collective-permute-done.4.refs_3_), channel_id=1, source_target_pairs={{8,0},{16,24},{9,1},{17,25},{10,2},{18,26},{11,3},{19,27},{12,4},{... | collective-permute-start | bytes 5505032 | tf_op jit(solution)/shard_map/ppermute | solution.py:297
  53.7 48.0 %collective-permute-start.14 = (bf16[256,512]{1,0:T(8,128)(2,1)S(1)}, bf16[256,512]{1,0:T(8,128)(2,1)S(1)}, u32[]{:S(2)}, u32[]{:S(2)}) collective-permute-start(bf16[256,512]{1,0:T(8,128)(2,1)S(1)} %get-tuple-element.26.refs_9_), channel_id=1, source_target_pairs={{16,8},{8,16},{17,9},{9,17},{18,10},{10,18},{19,11},{11,19},{20,12... | collective-permute-start | bytes 786440 | tf_op jit(solution)/shard_map/ppermute | solution.py:297
  54.4 84.7 %collective-permute-start.16 = (bf16[256,512]{1,0:T(8,128)(2,1)S(1)}, bf16[256,512]{1,0:T(8,128)(2,1)S(1)}, u32[]{:S(2)}, u32[]{:S(2)}) collective-permute-start(bf16[256,512]{1,0:T(8,128)(2,1)S(1)} %get-tuple-element.26.refs_9_), channel_id=1, source_target_pairs={{8,0},{0,8},{24,16},{16,24},{9,1},{1,9},{25,17},{17,25},{10,2},{2,... | collective-permute-start | bytes 786440 | tf_op jit(solution)/shard_map/ppermute | solution.py:297
  101.6 41.2 %collective-permute-start = (bf16[128,1024]{1,0:T(8,128)(2,1)S(1)}, bf16[128,1024]{1,0:T(8,128)(2,1)S(1)}, u32[]{:S(2)}, u32[]{:S(2)}) collective-permute-start(bf16[128,1024]{1,0:T(8,128)(2,1)S(1)} %shard_map.173.refs_0_), channel_id=1, source_target_pairs={{8,0},{0,8},{24,16},{16,24},{9,1},{1,9},{25,17},{17,25},{10,2},{2,... | collective-permute-start | bytes 786440 | tf_op jit(solution)/shard_map/ppermute | solution.py:297
  101.7 41.1 %collective-permute-start.6 = (bf16[128,1024]{1,0:T(8,128)(2,1)S(1)}, bf16[128,1024]{1,0:T(8,128)(2,1)S(1)}, u32[]{:S(2)}, u32[]{:S(2)}) collective-permute-start(bf16[128,1024]{1,0:T(8,128)(2,1)S(1)} %shard_map.173.refs_0_), channel_id=1, source_target_pairs={{16,8},{8,16},{17,9},{9,17},{18,10},{10,18},{19,11},{11,19},{20,12... | collective-permute-start | bytes 786440 | tf_op jit(solution)/shard_map/ppermute | solution.py:297
  139.1 4.3 %collective-permute-start.10 = (bf16[1032,128]{1,0:T(8,128)(2,1)S(1)}, bf16[1032,128]{1,0:T(8,128)(2,1)S(1)}, u32[]{:S(2)}, u32[]{:S(2)}) collective-permute-start(bf16[1032,128]{1,0:T(8,128)(2,1)S(1)} %get-tuple-element.25.refs_6_), channel_id=1, source_target_pairs={{16,8},{8,16},{17,9},{9,17},{18,10},{10,18},{19,11},{11,19},{20,12... | collective-permute-start | bytes 792584 | tf_op jit(solution)/shard_map/ppermute | solution.py:297
  142.8 8.2 %collective-permute-start.12 = (bf16[1032,128]{1,0:T(8,128)(2,1)S(1)}, bf16[1032,128]{1,0:T(8,128)(2,1)S(1)}, u32[]{:S(2)}, u32[]{:S(2)}) collective-permute-start(bf16[1032,128]{1,0:T(8,128)(2,1)S(1)} %get-tuple-element.25.refs_6_), channel_id=1, source_target_pairs={{8,0},{0,8},{24,16},{16,24},{9,1},{1,9},{25,17},{17,25},{10,2},{2,... | collective-permute-start | bytes 792584 | tf_op jit(solution)/shard_map/ppermute | solution.py:297
  142.8 8.9 %collective-permute-start.17 = (bf16[256,512]{1,0:T(8,128)(2,1)S(1)}, bf16[256,512]{1,0:T(8,128)(2,1)S(1)}, u32[]{:S(2)}, u32[]{:S(2)}) collective-permute-start(bf16[256,512]{1,0:T(8,128)(2,1)S(1)} %collective-permute-done.16.refs_10_), channel_id=1, source_target_pairs={{16,8},{8,16},{17,9},{9,17},{18,10},{10,18},{19,11},{11,19},{20,12... | collective-permute-start | bytes 786440 | tf_op jit(solution)/shard_map/ppermute | solution.py:297
  143.5 11.3 %collective-permute-start.15 = (bf16[256,512]{1,0:T(8,128)(2,1)S(1)}, bf16[256,512]{1,0:T(8,128)(2,1)S(1)}, u32[]{:S(2)}, u32[]{:S(2)}) collective-permute-start(bf16[256,512]{1,0:T(8,128)(2,1)S(1)} %collective-permute-done.14.refs_11_), channel_id=1, source_target_pairs={{8,0},{16,24},{9,1},{17,25},{10,2},{18,26},{11,3},{19,27},{12,4},{... | collective-permute-start | bytes 786440 | tf_op jit(solution)/shard_map/ppermute | solution.py:297
  151.0 5.1 %collective-permute-start.1 = (bf16[128,1024]{1,0:T(8,128)(2,1)S(1)}, bf16[128,1024]{1,0:T(8,128)(2,1)S(1)}, u32[]{:S(2)}, u32[]{:S(2)}) collective-permute-start(bf16[128,1024]{1,0:T(8,128)(2,1)S(1)} %collective-permute-done.refs_1_), channel_id=1, source_target_pairs={{16,8},{8,16},{17,9},{9,17},{18,10},{10,18},{19,11},{11,19},{20,12... | collective-permute-start | bytes 786440 | tf_op jit(solution)/shard_map/ppermute | solution.py:297
  151.6 5.7 %collective-permute-start.13 = (bf16[1032,128]{1,0:T(8,128)(2,1)S(1)}, bf16[1032,128]{1,0:T(8,128)(2,1)S(1)}, u32[]{:S(2)}, u32[]{:S(2)}) collective-permute-start(bf16[1032,128]{1,0:T(8,128)(2,1)S(1)} %collective-permute-done.12.refs_7_), channel_id=1, source_target_pairs={{16,8},{8,16},{17,9},{9,17},{18,10},{10,18},{19,11},{11,19},{20,12... | collective-permute-start | bytes 792584 | tf_op jit(solution)/shard_map/ppermute | solution.py:297
  154.8 19.0 %collective-permute-start.11 = (bf16[1032,128]{1,0:T(8,128)(2,1)S(1)}, bf16[1032,128]{1,0:T(8,128)(2,1)S(1)}, u32[]{:S(2)}, u32[]{:S(2)}) collective-permute-start(bf16[1032,128]{1,0:T(8,128)(2,1)S(1)} %collective-permute-done.10.refs_8_), channel_id=1, source_target_pairs={{8,0},{16,24},{9,1},{17,25},{10,2},{18,26},{11,3},{19,27},{12,4},{... | collective-permute-start | bytes 792584 | tf_op jit(solution)/shard_map/ppermute | solution.py:297
  156.1 16.4 %collective-permute-start.7 = (bf16[128,1024]{1,0:T(8,128)(2,1)S(1)}, bf16[128,1024]{1,0:T(8,128)(2,1)S(1)}, u32[]{:S(2)}, u32[]{:S(2)}) collective-permute-start(bf16[128,1024]{1,0:T(8,128)(2,1)S(1)} %collective-permute-done.6.refs_2_), channel_id=1, source_target_pairs={{8,0},{16,24},{9,1},{17,25},{10,2},{18,26},{11,3},{19,27},{12,4},{... | collective-permute-start | bytes 786440 | tf_op jit(solution)/shard_map/ppermute | solution.py:297
  157.4 22.0 %collective-permute-start.18 = (bf16[1032,128]{1,0:T(8,128)(2,1)S(1)}, bf16[1032,128]{1,0:T(8,128)(2,1)S(1)}, u32[]{:S(2)}, u32[]{:S(2)}) collective-permute-start(bf16[1032,128]{1,0:T(8,128)(2,1)S(1)} %collective-permute-done.13.refs_5_), channel_id=1, source_target_pairs={{8,0},{16,24},{9,1},{17,25},{10,2},{18,26},{11,3},{19,27},{12,4},{... | collective-permute-start | bytes 792584 | tf_op jit(solution)/shard_map/ppermute | solution.py:297
  172.5 10.5 %collective-permute-start.19 = (bf16[256,512]{1,0:T(8,128)(2,1)S(1)}, bf16[256,512]{1,0:T(8,128)(2,1)S(1)}, u32[]{:S(2)}, u32[]{:S(2)}) collective-permute-start(bf16[256,512]{1,0:T(8,128)(2,1)S(1)} %collective-permute-done.17.refs_7_), channel_id=1, source_target_pairs={{8,0},{16,24},{9,1},{17,25},{10,2},{18,26},{11,3},{19,27},{12,4},{... | collective-permute-start | bytes 786440 | tf_op jit(solution)/shard_map/ppermute | solution.py:297
  173.7 12.0 %collective-permute-start.2 = (bf16[128,1024]{1,0:T(8,128)(2,1)S(1)}, bf16[128,1024]{1,0:T(8,128)(2,1)S(1)}, u32[]{:S(2)}, u32[]{:S(2)}) collective-permute-start(bf16[128,1024]{1,0:T(8,128)(2,1)S(1)} %collective-permute-done.1.refs_1_), channel_id=1, source_target_pairs={{8,0},{16,24},{9,1},{17,25},{10,2},{18,26},{11,3},{19,27},{12,4},{... | collective-permute-start | bytes 786440 | tf_op jit(solution)/shard_map/ppermute | solution.py:297

commit v7 on v5

--- a/solution.py
+++ b/solution.py
@@ -77,8 +77,27 @@
 
 
 def merged_head(w, low, high, head):
-    def body(w_ref, low_ref, high_ref, out_ref, *scratch):
-        merge_into(out_ref, 0, head, 0, w_ref, low_ref, high_ref, *scratch)()
+    ahead = pl.ds(0, head)
+
+    def body(w_ref, low_ref, high_ref, out_ref, w_held, low_held, high_held, sems):
+        copies = [
+            pltpu.make_async_copy(w_ref.at[:, ahead], w_held, sems.at[0]),
+            pltpu.make_async_copy(low_ref, low_held, sems.at[1]),
+            pltpu.make_async_copy(high_ref.at[:, ahead], high_held, sems.at[2]),
+        ]
+        for copy in copies:
+            copy.start()
+        copies[1].wait()
+        copies[2].wait()
+        delta = lax.dot_general(
+            high_held[...],
+            low_held[...],
+            (((0,), (0,)), ((), ())),
+            preferred_element_type=jnp.float32,
+        )
+        copies[0].wait()
+        kept = w_held[...].T.astype(jnp.float32)
+        out_ref[...] = (kept + mix_rate * delta).astype(jnp.bfloat16)
 
     return pl.pallas_call(
         body,

time: 188 us -> 188 us (level)
  no operation moved by 1% of the time
where the time goes in v7:
time: 188 us; the launch traced here: 187 us
  waiting for transfers between devices  106 us (56%)
  starting transfers between devices  64.5 us (34%)
  Pallas kernels  13 us (7%)
    ppermute x20, waiting for transfers between devices, by_line(): held[name][hop] = lax.ppermute(held[name][source], 'shard', pairs)  106 us
    ppermute x20, starting transfers between devices, by_line(): held[name][hop] = lax.ppermute(held[name][source], 'shard', pairs)  64.5 us
    pallas_call x5, Pallas kernels, place(): pl.pallas_call(functools.partial(place_body, count, moves, 0, len(arrays)...  7.1 us
  transfers between devices with their start and end apart: 20, of which 8 were waited for; matrix products, arithmetic and copies ran while one was open for 0% of the time, Pallas kernels for 5%

profile of v7, /device:TPU:0, one launch (start us, length us, event | category | flops | bytes accessed | tf_op | source)
XLA Modules:
  0.0 187.1 jit_solution(1238319399195294064)
XLA Ops:
  0.6 3.1 %shard_map.174 = (bf16[1792,512]{1,0:T(8,128)(2,1)S(1)}, bf16[8,128]{1,0:T(8,128)(2,1)S(1)}) custom-call(bf16[1024,512]{1,0:T(8,128)(2,1)} %wm.1, bf16[16,1024]{1,0:T(8,128)(2,1)} %bitcast.9, bf16[16,512]{1,0:T(8,128)(2,1)} %hm.1, bf16[512,1024]{1,0:T(8,128)(2,1)} %wq.1, bf16[16,512]{1,0:T(8,128)(2,1)} %bitcast.11, bf16[16,1024]{1,0:T(8,128)(2,1)} %hq.1, ...), custom_call_target="tpu_custom_call" | custom-call | tf_op jit(solution)/shard_map/pallas_call | solution.py:138
  3.7 3.1 %collective-permute-start.3 = (bf16[1792,512]{1,0:T(8,128)(2,1)S(1)}, bf16[1792,512]{1,0:T(8,128)(2,1)S(1)}, u32[]{:S(2)}, u32[]{:S(2)}) collective-permute-start(bf16[1792,512]{1,0:T(8,128)(2,1)S(1)} %get-tuple-element.23.refs_3_), channel_id=1, source_target_pairs={{8,0},{0,8},{24,16},{16,24},{9,1},{1,9},{25,17},{17,25},{10,2},{2,... | collective-permute-start | bytes 5505032 | tf_op jit(solution)/shard_map/ppermute | solution.py:287
  6.8 0.8 collective-permute-start.8
  7.6 39.2 %collective-permute-done.3.refs_4_ = bf16[1792,512]{1,0:T(8,128)(2,1)S(1)} collective-permute-done((bf16[1792,512]{1,0:T(8,128)(2,1)S(1)}, bf16[1792,512]{1,0:T(8,128)(2,1)S(1)}, u32[]{:S(2)}, u32[]{:S(2)}) %collective-permute-start.3) | collective-permute-done | bytes 1835040 | tf_op jit(solution)/shard_map/ppermute | solution.py:287
  46.8 0.8 collective-permute-start.4
  47.6 1.3 collective-permute-start.9
  48.9 1.3 collective-permute-start.5
  50.2 1.8 all_gather.3.rows_ref
  52.1 1.6 shard_map.175
  53.7 0.7 collective-permute-start.14
  54.4 45.4 %collective-permute-start.16 = (bf16[256,512]{1,0:T(8,128)(2,1)S(1)}, bf16[256,512]{1,0:T(8,128)(2,1)S(1)}, u32[]{:S(2)}, u32[]{:S(2)}) collective-permute-start(bf16[256,512]{1,0:T(8,128)(2,1)S(1)} %get-tuple-element.26.refs_9_), channel_id=1, source_target_pairs={{8,0},{0,8},{24,16},{16,24},{9,1},{1,9},{25,17},{17,25},{10,2},{2,... | collective-permute-start | bytes 786440 | tf_op jit(solution)/shard_map/ppermute | solution.py:287
  99.8 1.3 shard_map.173.refs_0_
  101.1 0.7 collective-permute-start.6
  101.8 37.3 %collective-permute-done.16.refs_10_ = bf16[256,512]{1,0:T(8,128)(2,1)S(1)} collective-permute-done((bf16[256,512]{1,0:T(8,128)(2,1)S(1)}, bf16[256,512]{1,0:T(8,128)(2,1)S(1)}, u32[]{:S(2)}, u32[]{:S(2)}) %collective-permute-start.16) | collective-permute-done | bytes 262176 | tf_op jit(solution)/shard_map/ppermute | solution.py:287
  139.8 3.0 %collective-permute-done.refs_1_ = bf16[128,1024]{1,0:T(8,128)(2,1)S(1)} collective-permute-done((bf16[128,1024]{1,0:T(8,128)(2,1)S(1)}, bf16[128,1024]{1,0:T(8,128)(2,1)S(1)}, u32[]{:S(2)}, u32[]{:S(2)}) %collective-permute-start) | collective-permute-done | bytes 262176 | tf_op jit(solution)/shard_map/ppermute | solution.py:287
  143.5 1.3 collective-permute-start.15
  144.8 6.2 %collective-permute-done.12.refs_7_ = bf16[1032,128]{1,0:T(8,128)(2,1)S(1)} collective-permute-done((bf16[1032,128]{1,0:T(8,128)(2,1)S(1)}, bf16[1032,128]{1,0:T(8,128)(2,1)S(1)}, u32[]{:S(2)}, u32[]{:S(2)}) %collective-permute-start.12) | collective-permute-done | bytes 264224 | tf_op jit(solution)/shard_map/ppermute | solution.py:287
  151.6 0.7 collective-permute-start.13
  152.3 2.5 %collective-permute-done.15.refs_6_ = bf16[256,512]{1,0:T(8,128)(2,1)S(1)} collective-permute-done((bf16[256,512]{1,0:T(8,128)(2,1)S(1)}, bf16[256,512]{1,0:T(8,128)(2,1)S(1)}, u32[]{:S(2)}, u32[]{:S(2)}) %collective-permute-start.15) | collective-permute-done | bytes 262176 | tf_op jit(solution)/shard_map/ppermute | solution.py:287
  154.8 1.3 collective-permute-start.11
  156.1 1.3 collective-permute-start.7
  157.4 1.3 collective-permute-start.18
  158.7 13.8 %collective-permute-done.7.refs_0_ = bf16[128,1024]{1,0:T(8,128)(2,1)S(1)} collective-permute-done((bf16[128,1024]{1,0:T(8,128)(2,1)S(1)}, bf16[128,1024]{1,0:T(8,128)(2,1)S(1)}, u32[]{:S(2)}, u32[]{:S(2)}) %collective-permute-start.7) | collective-permute-done | bytes 262176 | tf_op jit(solution)/shard_map/ppermute | solution.py:287
  172.5 1.3 collective-permute-start.19
  173.7 1.3 collective-permute-start.2
  175.0 2.6 %shard_map.176 = (bf16[2048,1024]{1,0:T(8,128)(2,1)}, bf16[1024,2048]{1,0:T(8,128)(2,1)}, bf16[256,2048]{1,0:T(8,128)(2,1)}, bf16[32,128]{1,0:T(8,128)(2,1)S(1)}, bf16[256,2048]{1,0:T(8,128)(2,1)}) custom-call(bf16[128,1024]{1,0:T(8,128)(2,1)S(1)} %shard_map.173.refs_0_, bf16[128,1024]{1,0:T(8,128)(2,1)S(1)} %collective-permute-done.refs_1_, ...), custom_call_target="tpu_custom_call" | custom-call | tf_op jit(solution)/shard_map/pallas_call | solution.py:220
  177.7 1.7 shard_map.177
  179.4 0.8 shard_map.179
  180.7 2.2 %collective-permute-done.19.refs_0_ = bf16[256,512]{1,0:T(8,128)(2,1)S(1)} collective-permute-done((bf16[256,512]{1,0:T(8,128)(2,1)S(1)}, bf16[256,512]{1,0:T(8,128)(2,1)S(1)}, u32[]{:S(2)}, u32[]{:S(2)}) %collective-permute-start.19) | collective-permute-done | bytes 262176 | tf_op jit(solution)/shard_map/ppermute | solution.py:287
  182.9 0.7 shard_map.180
  183.7 2.1 %collective-permute-done.2.refs_0_ = bf16[128,1024]{1,0:T(8,128)(2,1)S(1)} collective-permute-done((bf16[128,1024]{1,0:T(8,128)(2,1)S(1)}, bf16[128,1024]{1,0:T(8,128)(2,1)S(1)}, u32[]{:S(2)}, u32[]{:S(2)}) %collective-permute-start.2) | collective-permute-done | bytes 262176 | tf_op jit(solution)/shard_map/ppermute | solution.py:287
  185.8 1.3 shard_map.178
  (18 shorter events, 2.7 us)
Async XLA Ops:
  3.7 43.1 %collective-permute-start.3 = (bf16[1792,512]{1,0:T(8,128)(2,1)S(1)}, bf16[1792,512]{1,0:T(8,128)(2,1)S(1)}, u32[]{:S(2)}, u32[]{:S(2)}) collective-permute-start(bf16[1792,512]{1,0:T(8,128)(2,1)S(1)} %get-tuple-element.23.refs_3_), channel_id=1, source_target_pairs={{8,0},{0,8},{24,16},{16,24},{9,1},{1,9},{25,17},{17,25},{10,2},{2,... | collective-permute-start | bytes 5505032 | tf_op jit(solution)/shard_map/ppermute | solution.py:287
  6.8 40.8 %collective-permute-start.8 = (bf16[1792,512]{1,0:T(8,128)(2,1)S(1)}, bf16[1792,512]{1,0:T(8,128)(2,1)S(1)}, u32[]{:S(2)}, u32[]{:S(2)}) collective-permute-start(bf16[1792,512]{1,0:T(8,128)(2,1)S(1)} %get-tuple-element.23.refs_3_), channel_id=1, source_target_pairs={{16,8},{8,16},{17,9},{9,17},{18,10},{10,18},{19,11},{11,19},{20,12... | collective-permute-start | bytes 5505032 | tf_op jit(solution)/shard_map/ppermute | solution.py:287
  46.8 2.1 %collective-permute-start.4 = (bf16[1792,512]{1,0:T(8,128)(2,1)S(1)}, bf16[1792,512]{1,0:T(8,128)(2,1)S(1)}, u32[]{:S(2)}, u32[]{:S(2)}) collective-permute-start(bf16[1792,512]{1,0:T(8,128)(2,1)S(1)} %collective-permute-done.3.refs_4_), channel_id=1, source_target_pairs={{16,8},{8,16},{17,9},{9,17},{18,10},{10,18},{19,11},{11,19},{20,12... | collective-permute-start | bytes 5505032 | tf_op jit(solution)/shard_map/ppermute | solution.py:287
  47.6 130.0 %collective-permute-start.9 = (bf16[1792,512]{1,0:T(8,128)(2,1)S(1)}, bf16[1792,512]{1,0:T(8,128)(2,1)S(1)}, u32[]{:S(2)}, u32[]{:S(2)}) collective-permute-start(bf16[1792,512]{1,0:T(8,128)(2,1)S(1)} %collective-permute-done.8.refs_5_), channel_id=1, source_target_pairs={{8,0},{16,24},{9,1},{17,25},{10,2},{18,26},{11,3},{19,27},{12,4},{... | collective-permute-start | bytes 5505032 | tf_op jit(solution)/shard_map/ppermute | solution.py:287
  48.9 136.8 %collective-permute-start.5 = (bf16[1792,512]{1,0:T(8,128)(2,1)S(1)}, bf16[1792,512]{1,0:T(8,128)(2,1)S(1)}, u32[]{:S(2)}, u32[]{:S(2)}) collective-permute-start(bf16[1792,512]{1,0:T(8,128)(2,1)S(1)} %collective-permute-done.4.refs_3_), channel_id=1, source_target_pairs={{8,0},{16,24},{9,1},{17,25},{10,2},{18,26},{11,3},{19,27},{12,4},{... | collective-permute-start | bytes 5505032 | tf_op jit(solution)/shard_map/ppermute | solution.py:287
  53.7 47.4 %collective-permute-start.14 = (bf16[256,512]{1,0:T(8,128)(2,1)S(1)}, bf16[256,512]{1,0:T(8,128)(2,1)S(1)}, u32[]{:S(2)}, u32[]{:S(2)}) collective-permute-start(bf16[256,512]{1,0:T(8,128)(2,1)S(1)} %get-tuple-element.26.refs_9_), channel_id=1, source_target_pairs={{16,8},{8,16},{17,9},{9,17},{18,10},{10,18},{19,11},{11,19},{20,12... | collective-permute-start | bytes 786440 | tf_op jit(solution)/shard_map/ppermute | solution.py:287
  54.4 84.7 %collective-permute-start.16 = (bf16[256,512]{1,0:T(8,128)(2,1)S(1)}, bf16[256,512]{1,0:T(8,128)(2,1)S(1)}, u32[]{:S(2)}, u32[]{:S(2)}) collective-permute-start(bf16[256,512]{1,0:T(8,128)(2,1)S(1)} %get-tuple-element.26.refs_9_), channel_id=1, source_target_pairs={{8,0},{0,8},{24,16},{16,24},{9,1},{1,9},{25,17},{17,25},{10,2},{2,... | collective-permute-start | bytes 786440 | tf_op jit(solution)/shard_map/ppermute | solution.py:287
  101.0 41.8 %collective-permute-start = (bf16[128,1024]{1,0:T(8,128)(2,1)S(1)}, bf16[128,1024]{1,0:T(8,128)(2,1)S(1)}, u32[]{:S(2)}, u32[]{:S(2)}) collective-permute-start(bf16[128,1024]{1,0:T(8,128)(2,1)S(1)} %shard_map.173.refs_0_), channel_id=1, source_target_pairs={{8,0},{0,8},{24,16},{16,24},{9,1},{1,9},{25,17},{17,25},{10,2},{2,... | collective-permute-start | bytes 786440 | tf_op jit(solution)/shard_map/ppermute | solution.py:287
  101.1 41.7 %collective-permute-start.6 = (bf16[128,1024]{1,0:T(8,128)(2,1)S(1)}, bf16[128,1024]{1,0:T(8,128)(2,1)S(1)}, u32[]{:S(2)}, u32[]{:S(2)}) collective-permute-start(bf16[128,1024]{1,0:T(8,128)(2,1)S(1)} %shard_map.173.refs_0_), channel_id=1, source_target_pairs={{16,8},{8,16},{17,9},{9,17},{18,10},{10,18},{19,11},{11,19},{20,12... | collective-permute-start | bytes 786440 | tf_op jit(solution)/shard_map/ppermute | solution.py:287
  139.1 4.3 %collective-permute-start.10 = (bf16[1032,128]{1,0:T(8,128)(2,1)S(1)}, bf16[1032,128]{1,0:T(8,128)(2,1)S(1)}, u32[]{:S(2)}, u32[]{:S(2)}) collective-permute-start(bf16[1032,128]{1,0:T(8,128)(2,1)S(1)} %get-tuple-element.25.refs_6_), channel_id=1, source_target_pairs={{16,8},{8,16},{17,9},{9,17},{18,10},{10,18},{19,11},{11,19},{20,12... | collective-permute-start | bytes 792584 | tf_op jit(solution)/shard_map/ppermute | solution.py:287
  142.8 8.2 %collective-permute-start.12 = (bf16[1032,128]{1,0:T(8,128)(2,1)S(1)}, bf16[1032,128]{1,0:T(8,128)(2,1)S(1)}, u32[]{:S(2)}, u32[]{:S(2)}) collective-permute-start(bf16[1032,128]{1,0:T(8,128)(2,1)S(1)} %get-tuple-element.25.refs_6_), channel_id=1, source_target_pairs={{8,0},{0,8},{24,16},{16,24},{9,1},{1,9},{25,17},{17,25},{10,2},{2,... | collective-permute-start | bytes 792584 | tf_op jit(solution)/shard_map/ppermute | solution.py:287
  142.8 8.9 %collective-permute-start.17 = (bf16[256,512]{1,0:T(8,128)(2,1)S(1)}, bf16[256,512]{1,0:T(8,128)(2,1)S(1)}, u32[]{:S(2)}, u32[]{:S(2)}) collective-permute-start(bf16[256,512]{1,0:T(8,128)(2,1)S(1)} %collective-permute-done.16.refs_10_), channel_id=1, source_target_pairs={{16,8},{8,16},{17,9},{9,17},{18,10},{10,18},{19,11},{11,19},{20,12... | collective-permute-start | bytes 786440 | tf_op jit(solution)/shard_map/ppermute | solution.py:287
  143.5 11.3 %collective-permute-start.15 = (bf16[256,512]{1,0:T(8,128)(2,1)S(1)}, bf16[256,512]{1,0:T(8,128)(2,1)S(1)}, u32[]{:S(2)}, u32[]{:S(2)}) collective-permute-start(bf16[256,512]{1,0:T(8,128)(2,1)S(1)} %collective-permute-done.14.refs_11_), channel_id=1, source_target_pairs={{8,0},{16,24},{9,1},{17,25},{10,2},{18,26},{11,3},{19,27},{12,4},{... | collective-permute-start | bytes 786440 | tf_op jit(solution)/shard_map/ppermute | solution.py:287
  151.0 5.1 %collective-permute-start.1 = (bf16[128,1024]{1,0:T(8,128)(2,1)S(1)}, bf16[128,1024]{1,0:T(8,128)(2,1)S(1)}, u32[]{:S(2)}, u32[]{:S(2)}) collective-permute-start(bf16[128,1024]{1,0:T(8,128)(2,1)S(1)} %collective-permute-done.refs_1_), channel_id=1, source_target_pairs={{16,8},{8,16},{17,9},{9,17},{18,10},{10,18},{19,11},{11,19},{20,12... | collective-permute-start | bytes 786440 | tf_op jit(solution)/shard_map/ppermute | solution.py:287
  151.6 5.7 %collective-permute-start.13 = (bf16[1032,128]{1,0:T(8,128)(2,1)S(1)}, bf16[1032,128]{1,0:T(8,128)(2,1)S(1)}, u32[]{:S(2)}, u32[]{:S(2)}) collective-permute-start(bf16[1032,128]{1,0:T(8,128)(2,1)S(1)} %collective-permute-done.12.refs_7_), channel_id=1, source_target_pairs={{16,8},{8,16},{17,9},{9,17},{18,10},{10,18},{19,11},{11,19},{20,12... | collective-permute-start | bytes 792584 | tf_op jit(solution)/shard_map/ppermute | solution.py:287
  154.8 19.0 %collective-permute-start.11 = (bf16[1032,128]{1,0:T(8,128)(2,1)S(1)}, bf16[1032,128]{1,0:T(8,128)(2,1)S(1)}, u32[]{:S(2)}, u32[]{:S(2)}) collective-permute-start(bf16[1032,128]{1,0:T(8,128)(2,1)S(1)} %collective-permute-done.10.refs_8_), channel_id=1, source_target_pairs={{8,0},{16,24},{9,1},{17,25},{10,2},{18,26},{11,3},{19,27},{12,4},{... | collective-permute-start | bytes 792584 | tf_op jit(solution)/shard_map/ppermute | solution.py:287
  156.1 16.4 %collective-permute-start.7 = (bf16[128,1024]{1,0:T(8,128)(2,1)S(1)}, bf16[128,1024]{1,0:T(8,128)(2,1)S(1)}, u32[]{:S(2)}, u32[]{:S(2)}) collective-permute-start(bf16[128,1024]{1,0:T(8,128)(2,1)S(1)} %collective-permute-done.6.refs_2_), channel_id=1, source_target_pairs={{8,0},{16,24},{9,1},{17,25},{10,2},{18,26},{11,3},{19,27},{12,4},{... | collective-permute-start | bytes 786440 | tf_op jit(solution)/shard_map/ppermute | solution.py:287
  157.4 22.0 %collective-permute-start.18 = (bf16[1032,128]{1,0:T(8,128)(2,1)S(1)}, bf16[1032,128]{1,0:T(8,128)(2,1)S(1)}, u32[]{:S(2)}, u32[]{:S(2)}) collective-permute-start(bf16[1032,128]{1,0:T(8,128)(2,1)S(1)} %collective-permute-done.13.refs_5_), channel_id=1, source_target_pairs={{8,0},{16,24},{9,1},{17,25},{10,2},{18,26},{11,3},{19,27},{12,4},{... | collective-permute-start | bytes 792584 | tf_op jit(solution)/shard_map/ppermute | solution.py:287
  172.5 10.5 %collective-permute-start.19 = (bf16[256,512]{1,0:T(8,128)(2,1)S(1)}, bf16[256,512]{1,0:T(8,128)(2,1)S(1)}, u32[]{:S(2)}, u32[]{:S(2)}) collective-permute-start(bf16[256,512]{1,0:T(8,128)(2,1)S(1)} %collective-permute-done.17.refs_7_), channel_id=1, source_target_pairs={{8,0},{16,24},{9,1},{17,25},{10,2},{18,26},{11,3},{19,27},{12,4},{... | collective-permute-start | bytes 786440 | tf_op jit(solution)/shard_map/ppermute | solution.py:287
  173.7 12.0 %collective-permute-start.2 = (bf16[128,1024]{1,0:T(8,128)(2,1)S(1)}, bf16[128,1024]{1,0:T(8,128)(2,1)S(1)}, u32[]{:S(2)}, u32[]{:S(2)}) collective-permute-start(bf16[128,1024]{1,0:T(8,128)(2,1)S(1)} %collective-permute-done.1.refs_1_), channel_id=1, source_target_pairs={{8,0},{16,24},{9,1},{17,25},{10,2},{18,26},{11,3},{19,27},{12,4},{... | collective-permute-start | bytes 786440 | tf_op jit(solution)/shard_map/ppermute | solution.py:287

commit v8 on v7

--- a/solution.py
+++ b/solution.py
@@ -22,7 +22,18 @@
     return [(base, min(size, total - base)) for base in range(0, total, size)]
 
 
-def merge_into(out_ref, offset, total, first, w_ref, low_ref, high_ref, w_held, low_held, high_held, sems):
+def stacked(out_ref, offset, total):
+    width = out_ref.shape[1]
+
+    def store(base, result):
+        for h in range(result.shape[1] // width):
+            row = pl.ds(offset + h * total + base, result.shape[0])
+            out_ref[row, :] = result[:, h * width : (h + 1) * width]
+
+    return store
+
+
+def merge_into(store, total, first, w_ref, low_ref, high_ref, w_held, low_held, high_held, sems):
     copies = [
         pltpu.make_async_copy(low_ref, low_held, sems.at[0]),
         pltpu.make_async_copy(high_ref.at[:, pl.ds(first, total)], high_held, sems.at[1]),
@@ -36,7 +47,6 @@
     def finish():
         copies[0].wait()
         copies[1].wait()
-        width = out_ref.shape[1]
         for (base, size), copy in zip(blocks(total), copies[2:]):
             copy.wait()
             part = pl.ds(base, size)
@@ -47,10 +57,7 @@
                 preferred_element_type=jnp.float32,
             )
             kept = w_held[:, part].T.astype(jnp.float32)
-            result = (kept + mix_rate * delta).astype(jnp.bfloat16)
-            for h in range(w_held.shape[0] // width):
-                row = offset + h * total + base
-                out_ref[pl.ds(row, size), :] = result[:, h * width : (h + 1) * width]
+            store(base, (kept + mix_rate * delta).astype(jnp.bfloat16))
 
     return finish
 
@@ -110,17 +117,25 @@
 
 
 def merged_body(mixed, query, norms, head):
-    rest = mixed[0].shape[1] - head
-    width = query[0].shape[0]
+    rest, width, wide = mixed[0].shape[1] - head, query[0].shape[0], query[0].shape[1]
     below = rest * (mixed[0].shape[0] // width)
     used = norms[0].size // lanes
+    tall = tiles(used)
     held = 4
 
     def body(wm, lm, hm, wq, lq, hq, train, step, out_ref, row_ref, *scratch):
-        finish_mixed = merge_into(out_ref, 0, rest, head, wm, lm, hm, *scratch[:held])
-        finish_query = merge_into(
-            out_ref, below, wq.shape[1], 0, wq, lq, hq, *scratch[held : 2 * held]
-        )
+        keep = stacked(out_ref, below, wide)
+        share = stacked(row_ref, tall, shared)
+
+        def store(base, result):
+            last = base + result.shape[0] == wide
+            kept = result.shape[0] - (shared if last else 0)
+            keep(base, result[:kept])
+            if last:
+                share(0, result[kept:])
+
+        finish_mixed = merge_into(stacked(out_ref, 0, rest), rest, head, wm, lm, hm, *scratch[:held])
+        finish_query = merge_into(store, wide, 0, wq, lq, hq, *scratch[held : 2 * held])
         train_held, step_held, sems = scratch[2 * held :]
         copies = [
             pltpu.make_async_copy(train, train_held, sems.at[0]),
@@ -132,7 +147,7 @@
         finish_query()
         for copy in copies:
             copy.wait()
-        row_ref[...] = jnp.zeros_like(row_ref)
+        row_ref[:tall, :] = jnp.zeros((tall, lanes), jnp.bfloat16)
         row_ref[:used, :] = (train_held[...] + step_held[...]).astype(jnp.bfloat16)
 
     return pl.pallas_call(
@@ -140,12 +155,12 @@
         in_specs=[in_hbm] * 8,
         out_specs=[in_vmem] * 2,
         out_shape=[
-            jax.ShapeDtypeStruct((below + query[0].shape[1], width), jnp.bfloat16),
-            jax.ShapeDtypeStruct((tiles(used), lanes), jnp.bfloat16),
+            jax.ShapeDtypeStruct((below + wide - shared, width), jnp.bfloat16),
+            jax.ShapeDtypeStruct((tall + shared * (width // lanes), lanes), jnp.bfloat16),
         ],
         scratch_shapes=[
             *scratch_of(mixed[0], mixed[1], rest),
-            *scratch_of(query[0], query[1], query[0].shape[1]),
+            *scratch_of(query[0], query[1], wide),
             *[pltpu.VMEM((used, lanes), jnp.float32)] * 2,
             pltpu.SemaphoreType.DMA((2,)),
         ],
@@ -156,39 +171,58 @@
     )
 
 
-def merged_tail(key, value, rows_of_cores, cores, used):
-    under = key[0].shape[1] * (key[0].shape[0] // lanes)
-    packed = tiles(cores * used)
+def merged_tail(*weights):
     held = 4
 
-    def body(wk, lk, hk, wv, lv, hv, rows_ref, key_ref, value_ref, *scratch):
-        finish_key = merge_into(key_ref, 0, wk.shape[1], 0, wk, lk, hk, *scratch[:held])
-        finish_value = merge_into(value_ref, 0, wv.shape[1], 0, wv, lv, hv, *scratch[held : 2 * held])
-        packed_ref = scratch[2 * held]
-        packed_ref[...] = jnp.zeros_like(packed_ref)
-        rows = rows_ref[...].astype(jnp.float32)
-        tall = rows.shape[0] // cores
-        for core in range(cores):
-            packed_ref[core * used : (core + 1) * used, :] = rows[core * tall : core * tall + used]
-        key_ref[pl.ds(under, packed), :] = packed_ref[...].astype(jnp.bfloat16)
-        finish_key()
-        finish_value()
+    def body(*refs):
+        outs, scratch = refs[3 * len(weights) :][: len(weights)], refs[4 * len(weights) :]
+        finishes = [
+            merge_into(
+                stacked(outs[j], 0, outs[j].shape[0]),
+                outs[j].shape[0],
+                0,
+                *refs[3 * j : 3 * j + 3],
+                *scratch[held * j : held * (j + 1)],
+            )
+            for j in range(len(weights))
+        ]
+        for finish in finishes:
+            finish()
 
     return pl.pallas_call(
         body,
-        in_specs=[in_hbm] * 6 + [in_vmem],
-        out_specs=[in_vmem] * 2,
-        out_shape=[
-            jax.ShapeDtypeStruct((under + packed, lanes), jnp.bfloat16),
-            jax.ShapeDtypeStruct(value[0].shape[::-1], jnp.bfloat16),
-        ],
-        scratch_shapes=[
-            *scratch_of(key[0], key[1], key[0].shape[1]),
-            *scratch_of(value[0], value[1], value[0].shape[1]),
-            pltpu.VMEM((packed, lanes), jnp.float32),
-        ],
+        in_specs=[in_hbm] * (3 * len(weights)),
+        out_specs=[in_vmem] * len(weights),
+        out_shape=[jax.ShapeDtypeStruct(w.shape[::-1], jnp.bfloat16) for w, _, _ in weights],
+        scratch_shapes=[ref for w, low, _ in weights for ref in scratch_of(w, low, w.shape[1])],
         compiler_params=merge_params,
-    )(*hbm(key[0], key[1].T, key[2], value[0], value[1].T, value[2]), rows_of_cores)
+    )(*hbm(*(a for w, low, high in weights for a in (w, low.T, high))))
+
+
+def place_shared(query_out, gathered, count, cores, tall, extent):
+    stacks = extent // lanes
+    each = tall + shared * stacks
+    low = query_out.shape[0] - shared
+
+    def body(gathered_ref, _, out_ref, sems):
+        mine = lax.axis_index("width") * each + tall
+        for act in ("start", "wait"):
+            for owner in range(count):
+                for b in range(stacks):
+                    at = ((cores - 1) * count + owner) * cores * each + b * shared
+                    source = gathered_ref.at[pl.ds(pl.multiple_of(mine + at, sublanes), shared)]
+                    target = out_ref.at[pl.ds(low, shared), pl.ds(owner * extent + b * lanes, lanes)]
+                    getattr(pltpu.make_async_copy(source, target, sems.at[owner * stacks + b]), act)()
+
+    return pl.pallas_call(
+        body,
+        in_specs=[in_vmem, in_hbm],
+        out_specs=in_hbm,
+        out_shape=jax.ShapeDtypeStruct(query_out.shape, query_out.dtype),
+        scratch_shapes=[pltpu.SemaphoreType.DMA((count * stacks,))],
+        input_output_aliases={1: 0},
+        compiler_params=pltpu.CompilerParams(vmem_limit_bytes=4 << 20),
+    )(gathered, query_out)
 
 
 def place_body(count, moves, pieces_at, outs_at, *refs):
@@ -246,7 +280,8 @@
 
 
 head = lanes
-chunk_names = ("head", "body", "key", "value")
+shared = 2 * sublanes
+chunk_names = ("head", "body", "shared", "key", "value")
 
 
 def groups(count):
@@ -257,25 +292,26 @@
 def by_line(count, cores, query, key, value, mixed, norms):
     rows, columns = query[0].shape[0], mixed[0].shape[1]
     used = norms[0].size // lanes
-    packed = tiles(cores * used)
+    tall = tiles(used)
     pieces = {}
     pieces["head"] = merged_head(*mixed, head)
     pieces["body"], row = merged_body(mixed, query, norms, head)
-    rows_of_cores = lax.all_gather(row, "width", axis=0, tiled=True)
-    pieces["key"], pieces["value"] = merged_tail(key, value, rows_of_cores, cores, used)
+    pieces["shared"] = lax.all_gather(row, "width", axis=0, tiled=True)
+    pieces["key"], pieces["value"] = merged_tail(key, value)
     rest, halves = columns - head, mixed[0].shape[0] // rows
     wide = {name: weight[0].shape[1] for name, weight in (("query", query), ("key", key), ("value", value))}
+    both = pieces["shared"].shape[0]
     regions = {
         "head": [("mixed", 0, head, columns, 0, 0, 0)],
         "body": [("mixed", h * rest, rest, columns, head, 0, h * rows) for h in range(halves)]
-        + [("query", halves * rest, wide["query"], 0, 0, rows, 0)],
-        "key": [("key", b * wide["key"], wide["key"], 0, 0, rows, b * lanes) for b in range(rows // lanes)]
-        + [("norm", wide["key"] * (rows // lanes), packed, packed, 0, 0, 0)],
+        + [("query", halves * rest, wide["query"] - shared, 0, 0, rows, 0)],
+        "shared": [("shared", 0, both, both, 0, 0, 0)],
+        "key": [("key", 0, wide["key"], 0, 0, rows, 0)],
         "value": [("value", 0, wide["value"], 0, 0, rows, 0)],
     }
     shapes = {name: (size, count * rows) for name, size in wide.items()}
     shapes["mixed"] = (count * columns, mixed[0].shape[0])
-    shapes["norm"] = (count * packed, lanes)
+    shapes["shared"] = (count * both, lanes)
     plan = hops(count)
     outs = {}
     held = {name: {"a0": piece, "b0": piece} for name, piece in pieces.items()}
@@ -284,13 +320,20 @@
         for hop, source, pairs, offset in plan:
             if int(hop[1:]) == k:
                 for name in chunk_names:
-                    held[name][hop] = lax.ppermute(held[name][source], "shard", pairs)
+                    if name == "shared":
+                        last = [(i * cores + cores - 1, j * cores + cores - 1) for i, j in pairs]
+                        held[name][hop] = lax.ppermute(held[name][source], ("shard", "width"), last)
+                    else:
+                        held[name][hop] = lax.ppermute(held[name][source], "shard", pairs)
                     arrived[name].append((regions[name], offset, held[name][hop]))
         for part in parts:
             place(outs, shapes, [piece for name in part for piece in arrived[name]], count)
         arrived = {name: [] for name in chunk_names}
-    serve_norm = outs["norm"].reshape(count, packed, lanes)[:, : cores * used].reshape(-1)
-    return outs["query"], outs["key"], outs["value"], outs["mixed"], serve_norm
+    gathered = lax.all_gather(outs["shared"], "width", axis=0, tiled=True)
+    final_query = place_shared(outs["query"], gathered, count, cores, tall, rows)
+    sums = gathered[(cores - 1) * count * both :].reshape(count * cores, both // cores, lanes)
+    serve_norm = sums[:, :used].reshape(-1)
+    return final_query, outs["key"], outs["value"], outs["mixed"], serve_norm
 
 
 def by_gather(count, cores, query, key, value, mixed, norms):

time: 188 us -> 195 us (1.037)
  blocking collectives: 1.84 us -> 11.7 us
  waiting for transfers between devices: 106 us -> 96.3 us
  starting transfers between devices: 64.5 us -> 71.3 us
    ppermute x20, waiting for transfers between devices: 106 us -> 96.2 us  [by_line(): held[name][hop] = lax.ppermute(held[name][source], 'shard', pairs)]
    all_gather x1 -> x2, blocking collectives: 1.84 us -> 11.7 us  [the longest x1 9.9 us: by_line(): gathered = lax.all_gather(outs['shared'], 'width', axis=0, tiled=True)]
    ppermute x20, starting transfers between devices: 64.5 us -> 68 us  [by_line(): held[name][hop] = lax.ppermute(held[name][source], 'shard', pairs)]
    ppermute x0 -> x5, starting transfers between devices: none -> 3.31 us  [by_line(): held[name][hop] = lax.ppermute(held[name][source], ('shard', 'width'), last)]
  transfers between devices with their start and end apart: 20 -> 25, of which waited for: 8 -> 9; matrix products, arithmetic and copies ran while one was open for 0% -> 0% of each run, Pallas kernels for 5% -> 4%
where the time goes in v8:
time: 195 us
  waiting for transfers between devices  96.3 us (49%)
  starting transfers between devices  71.3 us (37%)
  Pallas kernels  13.7 us (7%)
  blocking collectives  11.7 us (6%)
    ppermute x20, waiting for transfers between devices, by_line(): held[name][hop] = lax.ppermute(held[name][source], 'shard', pairs)  96.2 us
    ppermute x20, starting transfers between devices, by_line(): held[name][hop] = lax.ppermute(held[name][source], 'shard', pairs)  68 us
    all_gather x1, blocking collectives, by_line(): gathered = lax.all_gather(outs['shared'], 'width', axis=0, tiled=True)  9.9 us
    pallas_call x5, Pallas kernels, place(): pl.pallas_call(functools.partial(place_body, count, moves, 0, len(arrays)...  6.93 us
  transfers between devices with their start and end apart: 25, of which 9 were waited for; matrix products, arithmetic and copies ran while one was open for 0% of the time, Pallas kernels for 4%

profile of v8, /device:TPU:0, one launch (start us, length us, event | category | flops | bytes accessed | tf_op | source)
XLA Modules:
  0.0 194.6 jit_solution(11927703810767974824)
XLA Ops:
  0.6 3.1 %shard_map.174 = (bf16[1776,512]{1,0:T(8,128)(2,1)S(1)}, bf16[72,128]{1,0:T(8,128)(2,1)S(1)}) custom-call(bf16[1024,512]{1,0:T(8,128)(2,1)} %wm.1, bf16[16,1024]{1,0:T(8,128)(2,1)} %bitcast.9, bf16[16,512]{1,0:T(8,128)(2,1)} %hm.1, bf16[512,1024]{1,0:T(8,128)(2,1)} %wq.1, bf16[16,512]{1,0:T(8,128)(2,1)} %bitcast.11, bf16[16,1024]{1,0:T(8,128)(2,1)} %hq.1, ...), custom_call_target="tpu_custom_call" | custom-call | tf_op jit(solution)/shard_map/pallas_call | solution.py:153
  3.7 3.1 %collective-permute-start.3 = (bf16[1776,512]{1,0:T(8,128)(2,1)S(1)}, bf16[1776,512]{1,0:T(8,128)(2,1)S(1)}, u32[]{:S(2)}, u32[]{:S(2)}) collective-permute-start(bf16[1776,512]{1,0:T(8,128)(2,1)S(1)} %get-tuple-element.22.refs_3_), channel_id=1, source_target_pairs={{8,0},{0,8},{24,16},{16,24},{9,1},{1,9},{25,17},{17,25},{10,2},{2,... | collective-permute-start | bytes 5455880 | tf_op jit(solution)/shard_map/ppermute | solution.py:327
  6.8 0.8 collective-permute-start.11
  7.6 38.9 %collective-permute-done.3.refs_4_ = bf16[1776,512]{1,0:T(8,128)(2,1)S(1)} collective-permute-done((bf16[1776,512]{1,0:T(8,128)(2,1)S(1)}, bf16[1776,512]{1,0:T(8,128)(2,1)S(1)}, u32[]{:S(2)}, u32[]{:S(2)}) %collective-permute-start.3) | collective-permute-done | bytes 1818656 | tf_op jit(solution)/shard_map/ppermute | solution.py:327
  46.5 0.8 collective-permute-start.4
  47.3 1.3 collective-permute-start.12
  48.6 1.3 collective-permute-start.5
  49.9 1.8 all_gather.6.refs_6_
  54.4 1.6 shard_map.175
  56.7 45.0 %collective-permute-start.17 = (bf16[256,512]{1,0:T(8,128)(2,1)S(1)}, bf16[256,512]{1,0:T(8,128)(2,1)S(1)}, u32[]{:S(2)}, u32[]{:S(2)}) collective-permute-start(bf16[256,512]{1,0:T(8,128)(2,1)S(1)} %get-tuple-element.24.refs_9_), channel_id=1, source_target_pairs={{8,0},{0,8},{24,16},{16,24},{9,1},{1,9},{25,17},{17,25},{10,2},{2,... | collective-permute-start | bytes 786440 | tf_op jit(solution)/shard_map/ppermute | solution.py:327
  102.4 4.0 %collective-permute-start.21 = (bf16[256,512]{1,0:T(8,128)(2,1)S(1)}, bf16[256,512]{1,0:T(8,128)(2,1)S(1)}, u32[]{:S(2)}, u32[]{:S(2)}) collective-permute-start(bf16[256,512]{1,0:T(8,128)(2,1)S(1)} %get-tuple-element.25.refs_12_), channel_id=1, source_target_pairs={{8,0},{0,8},{24,16},{16,24},{9,1},{1,9},{25,17},{17,25},{10,2},{2,... | collective-permute-start | bytes 786440 | tf_op jit(solution)/shard_map/ppermute | solution.py:327
  106.5 1.2 shard_map.173.refs_0_
  107.7 25.9 %collective-permute-done.17.refs_10_ = bf16[256,512]{1,0:T(8,128)(2,1)S(1)} collective-permute-done((bf16[256,512]{1,0:T(8,128)(2,1)S(1)}, bf16[256,512]{1,0:T(8,128)(2,1)S(1)}, u32[]{:S(2)}, u32[]{:S(2)}) %collective-permute-start.17) | collective-permute-done | bytes 262176 | tf_op jit(solution)/shard_map/ppermute | solution.py:327
  134.4 2.5 %collective-permute-done.21.refs_13_ = bf16[256,512]{1,0:T(8,128)(2,1)S(1)} collective-permute-done((bf16[256,512]{1,0:T(8,128)(2,1)S(1)}, bf16[256,512]{1,0:T(8,128)(2,1)S(1)}, u32[]{:S(2)}, u32[]{:S(2)}) %collective-permute-start.21) | collective-permute-done | bytes 262176 | tf_op jit(solution)/shard_map/ppermute | solution.py:327
  137.6 3.7 %collective-permute-done.refs_1_ = bf16[128,1024]{1,0:T(8,128)(2,1)S(1)} collective-permute-done((bf16[128,1024]{1,0:T(8,128)(2,1)S(1)}, bf16[128,1024]{1,0:T(8,128)(2,1)S(1)}, u32[]{:S(2)}, u32[]{:S(2)}) %collective-permute-start) | collective-permute-done | bytes 262176 | tf_op jit(solution)/shard_map/ppermute | solution.py:327
  142.6 1.3 collective-permute-start.16
  143.9 1.3 collective-permute-start.20
  145.2 1.3 collective-permute-start.10
  146.5 10.2 %collective-permute-done.16.refs_6_ = bf16[256,512]{1,0:T(8,128)(2,1)S(1)} collective-permute-done((bf16[256,512]{1,0:T(8,128)(2,1)S(1)}, bf16[256,512]{1,0:T(8,128)(2,1)S(1)}, u32[]{:S(2)}, u32[]{:S(2)}) %collective-permute-start.16) | collective-permute-done | bytes 262176 | tf_op jit(solution)/shard_map/ppermute | solution.py:327
  156.7 1.3 collective-permute-start.23
  158.0 1.5 collective-permute-done.20.refs_8_
  159.5 1.3 collective-permute-start.24
  160.8 4.3 %collective-permute-done.10.refs_0_ = bf16[128,1024]{1,0:T(8,128)(2,1)S(1)} collective-permute-done((bf16[128,1024]{1,0:T(8,128)(2,1)S(1)}, bf16[128,1024]{1,0:T(8,128)(2,1)S(1)}, u32[]{:S(2)}, u32[]{:S(2)}) %collective-permute-start.10) | collective-permute-done | bytes 262176 | tf_op jit(solution)/shard_map/ppermute | solution.py:327
  165.0 1.3 collective-permute-start.2
  167.0 2.5 %shard_map.176 = (bf16[2048,1024]{1,0:T(8,128)(2,1)}, bf16[1024,2048]{1,0:T(8,128)(2,1)}, bf16[576,128]{1,0:T(8,128)(2,1)S(1)}, bf16[256,2048]{1,0:T(8,128)(2,1)}, bf16[256,2048]{1,0:T(8,128)(2,1)}) custom-call(bf16[128,1024]{1,0:T(8,128)(2,1)S(1)} %shard_map.173.refs_0_, bf16[128,1024]{1,0:T(8,128)(2,1)S(1)} %collective-permute-done.refs_1_, ...), custom_call_target="tpu_custom_call" | custom-call | tf_op jit(solution)/shard_map/pallas_call | solution.py:254
  169.5 1.6 shard_map.177
  171.2 0.7 shard_map.180
  171.9 4.4 %collective-permute-done.24.refs_0_ = bf16[256,512]{1,0:T(8,128)(2,1)S(1)} collective-permute-done((bf16[256,512]{1,0:T(8,128)(2,1)S(1)}, bf16[256,512]{1,0:T(8,128)(2,1)S(1)}, u32[]{:S(2)}, u32[]{:S(2)}) %collective-permute-start.24) | collective-permute-done | bytes 262176 | tf_op jit(solution)/shard_map/ppermute | solution.py:327
  177.0 4.9 %collective-permute-done.2.refs_0_ = bf16[128,1024]{1,0:T(8,128)(2,1)S(1)} collective-permute-done((bf16[128,1024]{1,0:T(8,128)(2,1)S(1)}, bf16[128,1024]{1,0:T(8,128)(2,1)S(1)}, u32[]{:S(2)}, u32[]{:S(2)}) %collective-permute-start.2) | collective-permute-done | bytes 262176 | tf_op jit(solution)/shard_map/ppermute | solution.py:327
  181.9 1.4 shard_map.178
  183.3 9.9 %all_gather.7.gathered_ref = bf16[1152,128]{1,0:T(8,128)(2,1)S(1)} all-gather(bf16[576,128]{1,0:T(8,128)(2,1)S(1)} %get-tuple-element.34), channel_id=1, replica_groups=mesh['shard'=4,'width'=2,'shift'=4] {'width'}, dimensions={0}, use_global_device_ids=true | all-gather | bytes 442368 | tf_op jit(solution)/shard_map/all_gather | solution.py:332
  193.2 0.8 shard_map.179
  (31 shorter events, 8.7 us)
Async XLA Ops:
  3.7 42.8 %collective-permute-start.3 = (bf16[1776,512]{1,0:T(8,128)(2,1)S(1)}, bf16[1776,512]{1,0:T(8,128)(2,1)S(1)}, u32[]{:S(2)}, u32[]{:S(2)}) collective-permute-start(bf16[1776,512]{1,0:T(8,128)(2,1)S(1)} %get-tuple-element.22.refs_3_), channel_id=1, source_target_pairs={{8,0},{0,8},{24,16},{16,24},{9,1},{1,9},{25,17},{17,25},{10,2},{2,... | collective-permute-start | bytes 5455880 | tf_op jit(solution)/shard_map/ppermute | solution.py:327
  6.8 40.4 %collective-permute-start.11 = (bf16[1776,512]{1,0:T(8,128)(2,1)S(1)}, bf16[1776,512]{1,0:T(8,128)(2,1)S(1)}, u32[]{:S(2)}, u32[]{:S(2)}) collective-permute-start(bf16[1776,512]{1,0:T(8,128)(2,1)S(1)} %get-tuple-element.22.refs_3_), channel_id=1, source_target_pairs={{16,8},{8,16},{17,9},{9,17},{18,10},{10,18},{19,11},{11,19},{20,12... | collective-permute-start | bytes 5455880 | tf_op jit(solution)/shard_map/ppermute | solution.py:327
  46.5 2.1 %collective-permute-start.4 = (bf16[1776,512]{1,0:T(8,128)(2,1)S(1)}, bf16[1776,512]{1,0:T(8,128)(2,1)S(1)}, u32[]{:S(2)}, u32[]{:S(2)}) collective-permute-start(bf16[1776,512]{1,0:T(8,128)(2,1)S(1)} %collective-permute-done.3.refs_4_), channel_id=1, source_target_pairs={{16,8},{8,16},{17,9},{9,17},{18,10},{10,18},{19,11},{11,19},{20,12... | collective-permute-start | bytes 5455880 | tf_op jit(solution)/shard_map/ppermute | solution.py:327
  47.3 119.1 %collective-permute-start.12 = (bf16[1776,512]{1,0:T(8,128)(2,1)S(1)}, bf16[1776,512]{1,0:T(8,128)(2,1)S(1)}, u32[]{:S(2)}, u32[]{:S(2)}) collective-permute-start(bf16[1776,512]{1,0:T(8,128)(2,1)S(1)} %collective-permute-done.11.refs_5_), channel_id=1, source_target_pairs={{8,0},{16,24},{9,1},{17,25},{10,2},{18,26},{11,3},{19,27},{12,4},{... | collective-permute-start | bytes 5455880 | tf_op jit(solution)/shard_map/ppermute | solution.py:327
  48.6 133.3 %collective-permute-start.5 = (bf16[1776,512]{1,0:T(8,128)(2,1)S(1)}, bf16[1776,512]{1,0:T(8,128)(2,1)S(1)}, u32[]{:S(2)}, u32[]{:S(2)}) collective-permute-start(bf16[1776,512]{1,0:T(8,128)(2,1)S(1)} %collective-permute-done.4.refs_3_), channel_id=1, source_target_pairs={{8,0},{16,24},{9,1},{17,25},{10,2},{18,26},{11,3},{19,27},{12,4},{... | collective-permute-start | bytes 5455880 | tf_op jit(solution)/shard_map/ppermute | solution.py:327
  51.7 1.3 collective-permute-start.6
  52.4 1.4 collective-permute-start.13
  53.1 3.7 %collective-permute-start.7 = (bf16[144,128]{1,0:T(8,128)(2,1)S(1)}, bf16[144,128]{1,0:T(8,128)(2,1)S(1)}, u32[]{:S(2)}, u32[]{:S(2)}) collective-permute-start(bf16[144,128]{1,0:T(8,128)(2,1)S(1)} %collective-permute-done.6.refs_7_), channel_id=1, source_target_pairs={{20,12},{12,20},{21,13},{13,21},{22,14},{14,22},{23,15},{15,23}} | collective-permute-start | bytes 110600 | tf_op jit(solution)/shard_map/ppermute | solution.py:325
  53.7 48.0 %collective-permute-start.14 = (bf16[144,128]{1,0:T(8,128)(2,1)S(1)}, bf16[144,128]{1,0:T(8,128)(2,1)S(1)}, u32[]{:S(2)}, u32[]{:S(2)}) collective-permute-start(bf16[144,128]{1,0:T(8,128)(2,1)S(1)} %collective-permute-done.13.refs_8_), channel_id=1, source_target_pairs={{12,4},{20,28},{13,5},{21,29},{14,6},{22,30},{15,7},{23,31}} | collective-permute-start | bytes 110600 | tf_op jit(solution)/shard_map/ppermute | solution.py:325
  56.0 46.4 %collective-permute-start.15 = (bf16[256,512]{1,0:T(8,128)(2,1)S(1)}, bf16[256,512]{1,0:T(8,128)(2,1)S(1)}, u32[]{:S(2)}, u32[]{:S(2)}) collective-permute-start(bf16[256,512]{1,0:T(8,128)(2,1)S(1)} %get-tuple-element.24.refs_9_), channel_id=1, source_target_pairs={{16,8},{8,16},{17,9},{9,17},{18,10},{10,18},{19,11},{11,19},{20,12... | collective-permute-start | bytes 786440 | tf_op jit(solution)/shard_map/ppermute | solution.py:327
  56.7 77.0 %collective-permute-start.17 = (bf16[256,512]{1,0:T(8,128)(2,1)S(1)}, bf16[256,512]{1,0:T(8,128)(2,1)S(1)}, u32[]{:S(2)}, u32[]{:S(2)}) collective-permute-start(bf16[256,512]{1,0:T(8,128)(2,1)S(1)} %get-tuple-element.24.refs_9_), channel_id=1, source_target_pairs={{8,0},{0,8},{24,16},{16,24},{9,1},{1,9},{25,17},{17,25},{10,2},{2,... | collective-permute-start | bytes 786440 | tf_op jit(solution)/shard_map/ppermute | solution.py:327
  101.8 31.9 %collective-permute-start.19 = (bf16[256,512]{1,0:T(8,128)(2,1)S(1)}, bf16[256,512]{1,0:T(8,128)(2,1)S(1)}, u32[]{:S(2)}, u32[]{:S(2)}) collective-permute-start(bf16[256,512]{1,0:T(8,128)(2,1)S(1)} %get-tuple-element.25.refs_12_), channel_id=1, source_target_pairs={{16,8},{8,16},{17,9},{9,17},{18,10},{10,18},{19,11},{11,19},{20,12... | collective-permute-start | bytes 786440 | tf_op jit(solution)/shard_map/ppermute | solution.py:327
  102.4 34.4 %collective-permute-start.21 = (bf16[256,512]{1,0:T(8,128)(2,1)S(1)}, bf16[256,512]{1,0:T(8,128)(2,1)S(1)}, u32[]{:S(2)}, u32[]{:S(2)}) collective-permute-start(bf16[256,512]{1,0:T(8,128)(2,1)S(1)} %get-tuple-element.25.refs_12_), channel_id=1, source_target_pairs={{8,0},{0,8},{24,16},{16,24},{9,1},{1,9},{25,17},{17,25},{10,2},{2,... | collective-permute-start | bytes 786440 | tf_op jit(solution)/shard_map/ppermute | solution.py:327
  133.7 7.5 %collective-permute-start = (bf16[128,1024]{1,0:T(8,128)(2,1)S(1)}, bf16[128,1024]{1,0:T(8,128)(2,1)S(1)}, u32[]{:S(2)}, u32[]{:S(2)}) collective-permute-start(bf16[128,1024]{1,0:T(8,128)(2,1)S(1)} %shard_map.173.refs_0_), channel_id=1, source_target_pairs={{8,0},{0,8},{24,16},{16,24},{9,1},{1,9},{25,17},{17,25},{10,2},{2,... | collective-permute-start | bytes 786440 | tf_op jit(solution)/shard_map/ppermute | solution.py:327
  133.7 8.2 %collective-permute-start.9 = (bf16[128,1024]{1,0:T(8,128)(2,1)S(1)}, bf16[128,1024]{1,0:T(8,128)(2,1)S(1)}, u32[]{:S(2)}, u32[]{:S(2)}) collective-permute-start(bf16[128,1024]{1,0:T(8,128)(2,1)S(1)} %shard_map.173.refs_0_), channel_id=1, source_target_pairs={{16,8},{8,16},{17,9},{9,17},{18,10},{10,18},{19,11},{11,19},{20,12... | collective-permute-start | bytes 786440 | tf_op jit(solution)/shard_map/ppermute | solution.py:327
  136.9 5.7 %collective-permute-start.18 = (bf16[256,512]{1,0:T(8,128)(2,1)S(1)}, bf16[256,512]{1,0:T(8,128)(2,1)S(1)}, u32[]{:S(2)}, u32[]{:S(2)}) collective-permute-start(bf16[256,512]{1,0:T(8,128)(2,1)S(1)} %collective-permute-done.17.refs_10_), channel_id=1, source_target_pairs={{16,8},{8,16},{17,9},{9,17},{18,10},{10,18},{19,11},{11,19},{20,12... | collective-permute-start | bytes 786440 | tf_op jit(solution)/shard_map/ppermute | solution.py:327
  141.2 2.7 %collective-permute-start.22 = (bf16[256,512]{1,0:T(8,128)(2,1)S(1)}, bf16[256,512]{1,0:T(8,128)(2,1)S(1)}, u32[]{:S(2)}, u32[]{:S(2)}) collective-permute-start(bf16[256,512]{1,0:T(8,128)(2,1)S(1)} %collective-permute-done.21.refs_13_), channel_id=1, source_target_pairs={{16,8},{8,16},{17,9},{9,17},{18,10},{10,18},{19,11},{11,19},{20,12... | collective-permute-start | bytes 786440 | tf_op jit(solution)/shard_map/ppermute | solution.py:327
  141.9 3.3 %collective-permute-start.1 = (bf16[128,1024]{1,0:T(8,128)(2,1)S(1)}, bf16[128,1024]{1,0:T(8,128)(2,1)S(1)}, u32[]{:S(2)}, u32[]{:S(2)}) collective-permute-start(bf16[128,1024]{1,0:T(8,128)(2,1)S(1)} %collective-permute-done.refs_1_), channel_id=1, source_target_pairs={{16,8},{8,16},{17,9},{9,17},{18,10},{10,18},{19,11},{11,19},{20,12... | collective-permute-start | bytes 786440 | tf_op jit(solution)/shard_map/ppermute | solution.py:327
  142.6 14.1 %collective-permute-start.16 = (bf16[256,512]{1,0:T(8,128)(2,1)S(1)}, bf16[256,512]{1,0:T(8,128)(2,1)S(1)}, u32[]{:S(2)}, u32[]{:S(2)}) collective-permute-start(bf16[256,512]{1,0:T(8,128)(2,1)S(1)} %collective-permute-done.15.refs_11_), channel_id=1, source_target_pairs={{8,0},{16,24},{9,1},{17,25},{10,2},{18,26},{11,3},{19,27},{12,4},{... | collective-permute-start | bytes 786440 | tf_op jit(solution)/shard_map/ppermute | solution.py:327
  143.9 15.6 %collective-permute-start.20 = (bf16[256,512]{1,0:T(8,128)(2,1)S(1)}, bf16[256,512]{1,0:T(8,128)(2,1)S(1)}, u32[]{:S(2)}, u32[]{:S(2)}) collective-permute-start(bf16[256,512]{1,0:T(8,128)(2,1)S(1)} %collective-permute-done.19.refs_14_), channel_id=1, source_target_pairs={{8,0},{16,24},{9,1},{17,25},{10,2},{18,26},{11,3},{19,27},{12,4},{... | collective-permute-start | bytes 786440 | tf_op jit(solution)/shard_map/ppermute | solution.py:327
  145.2 19.8 %collective-permute-start.10 = (bf16[128,1024]{1,0:T(8,128)(2,1)S(1)}, bf16[128,1024]{1,0:T(8,128)(2,1)S(1)}, u32[]{:S(2)}, u32[]{:S(2)}) collective-permute-start(bf16[128,1024]{1,0:T(8,128)(2,1)S(1)} %collective-permute-done.9.refs_2_), channel_id=1, source_target_pairs={{8,0},{16,24},{9,1},{17,25},{10,2},{18,26},{11,3},{19,27},{12,4},{... | collective-permute-start | bytes 786440 | tf_op jit(solution)/shard_map/ppermute | solution.py:327
  156.7 14.5 %collective-permute-start.23 = (bf16[256,512]{1,0:T(8,128)(2,1)S(1)}, bf16[256,512]{1,0:T(8,128)(2,1)S(1)}, u32[]{:S(2)}, u32[]{:S(2)}) collective-permute-start(bf16[256,512]{1,0:T(8,128)(2,1)S(1)} %collective-permute-done.18.refs_7_), channel_id=1, source_target_pairs={{8,0},{16,24},{9,1},{17,25},{10,2},{18,26},{11,3},{19,27},{12,4},{... | collective-permute-start | bytes 786440 | tf_op jit(solution)/shard_map/ppermute | solution.py:327
  159.5 16.8 %collective-permute-start.24 = (bf16[256,512]{1,0:T(8,128)(2,1)S(1)}, bf16[256,512]{1,0:T(8,128)(2,1)S(1)}, u32[]{:S(2)}, u32[]{:S(2)}) collective-permute-start(bf16[256,512]{1,0:T(8,128)(2,1)S(1)} %collective-permute-done.22.refs_9_), channel_id=1, source_target_pairs={{8,0},{16,24},{9,1},{17,25},{10,2},{18,26},{11,3},{19,27},{12,4},{... | collective-permute-start | bytes 786440 | tf_op jit(solution)/shard_map/ppermute | solution.py:327
  165.0 16.9 %collective-permute-start.2 = (bf16[128,1024]{1,0:T(8,128)(2,1)S(1)}, bf16[128,1024]{1,0:T(8,128)(2,1)S(1)}, u32[]{:S(2)}, u32[]{:S(2)}) collective-permute-start(bf16[128,1024]{1,0:T(8,128)(2,1)S(1)} %collective-permute-done.1.refs_1_), channel_id=1, source_target_pairs={{8,0},{16,24},{9,1},{17,25},{10,2},{18,26},{11,3},{19,27},{12,4},{... | collective-permute-start | bytes 786440 | tf_op jit(solution)/shard_map/ppermute | solution.py:327
  166.3 10.7 %collective-permute-start.8 = (bf16[144,128]{1,0:T(8,128)(2,1)S(1)}, bf16[144,128]{1,0:T(8,128)(2,1)S(1)}, u32[]{:S(2)}, u32[]{:S(2)}) collective-permute-start(bf16[144,128]{1,0:T(8,128)(2,1)S(1)} %collective-permute-done.7.refs_5_), channel_id=1, source_target_pairs={{12,4},{20,28},{13,5},{21,29},{14,6},{22,30},{15,7},{23,31}} | collective-permute-start | bytes 110600 | tf_op jit(solution)/shard_map/ppermute | solution.py:325

commit v9 on v5

--- a/solution.py
+++ b/solution.py
@@ -76,100 +76,128 @@
 merge_params = pltpu.CompilerParams(vmem_limit_bytes=12 << 20)
 
 
-def merged_head(w, low, high, head):
-    def body(w_ref, low_ref, high_ref, out_ref, *scratch):
-        merge_into(out_ref, 0, head, 0, w_ref, low_ref, high_ref, *scratch)()
+def merged(weights, extra=()):
+    held, count = 4, len(weights)
+    shapes = [
+        jax.ShapeDtypeStruct((w.shape[1] * (w.shape[0] // width), width), jnp.bfloat16)
+        for w, _, _, width in weights
+    ]
+    scratch_shapes = [ref for w, low, _, _ in weights for ref in scratch_of(w, low, w.shape[1])]
+    operands = hbm(*(a for w, low, high, _ in weights for a in (w, low.T, high)))
+    if extra:
+        part, rank, used = extra[3], extra[0].shape[1], extra[1].size // lanes
+        blocks_of_low = part // lanes
+        operands += hbm(extra[0].T, *(a.reshape(used, lanes) for a in extra[1:3]))
+        side = rank * blocks_of_low
+        shapes.append(jax.ShapeDtypeStruct((side + tiles(used), lanes), jnp.bfloat16))
+        scratch_shapes += [pltpu.VMEM((rank, part), jnp.bfloat16)]
+        scratch_shapes += [pltpu.VMEM((used, lanes), jnp.float32)] * 2
+        scratch_shapes += [pltpu.SemaphoreType.DMA((3,))]
+
+    def body(*refs):
+        inputs, outs = refs[: len(operands)], refs[len(operands) :][: len(shapes)]
+        scratch = refs[len(operands) + len(shapes) :]
+        finishes = [
+            merge_into(
+                outs[j], 0, inputs[3 * j].shape[1], 0, *inputs[3 * j : 3 * j + 3], *scratch[held * j : held * j + held]
+            )
+            for j in range(count)
+        ]
+        if extra:
+            targets, sems = scratch[held * count : -1], scratch[-1]
+            low_ref, train, step = inputs[3 * count :]
+            mine = pl.ds(pl.multiple_of(lax.axis_index("width") * part, lanes), part)
+            copies = [
+                pltpu.make_async_copy(source, target, sems.at[j])
+                for j, (source, target) in enumerate(zip((low_ref.at[:, mine], train, step), targets))
+            ]
+            for copy in copies:
+                copy.start()
+        for finish in finishes:
+            finish()
+        if extra:
+            for copy in copies:
+                copy.wait()
+            low_held, train_held, step_held = targets
+            for j in range(blocks_of_low):
+                outs[-1][pl.ds(j * rank, rank), :] = low_held[:, pl.ds(j * lanes, lanes)]
+            outs[-1][pl.ds(side, tiles(used)), :] = jnp.zeros((tiles(used), lanes), jnp.bfloat16)
+            outs[-1][pl.ds(side, used), :] = (train_held[...] + step_held[...]).astype(jnp.bfloat16)
 
     return pl.pallas_call(
         body,
-        in_specs=[in_hbm] * 3,
-        out_specs=in_vmem,
-        out_shape=jax.ShapeDtypeStruct((head, w.shape[0]), jnp.bfloat16),
-        scratch_shapes=scratch_of(w, low, head),
+        in_specs=[in_hbm] * len(operands),
+        out_specs=[in_vmem] * len(shapes),
+        out_shape=shapes,
+        scratch_shapes=scratch_shapes,
         compiler_params=merge_params,
-    )(*hbm(w, low.T, high))
-
-
-def merged_body(mixed, query, norms, head):
-    rest = mixed[0].shape[1] - head
-    width = query[0].shape[0]
-    below = rest * (mixed[0].shape[0] // width)
-    used = norms[0].size // lanes
-    held = 4
-
-    def body(wm, lm, hm, wq, lq, hq, train, step, out_ref, row_ref, *scratch):
-        finish_mixed = merge_into(out_ref, 0, rest, head, wm, lm, hm, *scratch[:held])
-        finish_query = merge_into(
-            out_ref, below, wq.shape[1], 0, wq, lq, hq, *scratch[held : 2 * held]
-        )
-        train_held, step_held, sems = scratch[2 * held :]
-        copies = [
-            pltpu.make_async_copy(train, train_held, sems.at[0]),
-            pltpu.make_async_copy(step, step_held, sems.at[1]),
-        ]
-        for copy in copies:
-            copy.start()
-        finish_mixed()
-        finish_query()
-        for copy in copies:
-            copy.wait()
-        row_ref[...] = jnp.zeros_like(row_ref)
-        row_ref[:used, :] = (train_held[...] + step_held[...]).astype(jnp.bfloat16)
+    )(*operands)
+
+
+def merged_pieces(pieces, sides, high, count, cores, each):
+    rows, wide = pieces[0][1].shape
+    rank = high.shape[0]
+    stacks = rows // lanes // cores
+    offsets = [offset for offset, _ in pieces]
+    total = len(pieces)
+
+    def body(*refs):
+        raws, sides_ref, high_ref, out_ref = refs[:total], refs[total], refs[total + 1], refs[total + 2]
+        low_held, result, low_sems, out_sems = refs[total + 3 :]
+        me = lax.axis_index("shard")
+        sign = 1 - 2 * lax.rem(me, 2)
+        for act in ("work", "wait"):
+            for j, offset in enumerate(offsets):
+                owner = me + sign * offset
+
+                @pl.when(jnp.logical_and(owner >= 0, owner < count))
+                def _():
+                    column = pl.multiple_of(owner * rows, lanes)
+                    move = pltpu.make_async_copy(
+                        result.at[j], out_ref.at[:, pl.ds(column, rows)], out_sems.at[j]
+                    )
+                    if act == "wait":
+                        move.wait()
+                        return
+                    copies = []
+                    for core in range(cores):
+                        for b in range(stacks):
+                            at = pl.multiple_of((core * count + owner) * each + b * rank, sublanes)
+                            n = core * stacks + b
+                            copies.append(
+                                pltpu.make_async_copy(
+                                    sides_ref.at[pl.ds(at, rank)],
+                                    low_held.at[j, :, pl.ds(n * lanes, lanes)],
+                                    low_sems.at[n],
+                                )
+                            )
+                    for copy in copies:
+                        copy.start()
+                    for copy in copies:
+                        copy.wait()
+                    delta = lax.dot_general(
+                        high_ref[...],
+                        low_held[j],
+                        (((0,), (0,)), ((), ())),
+                        preferred_element_type=jnp.float32,
+                    )
+                    kept = raws[j][...].T.astype(jnp.float32)
+                    result[j] = (kept + mix_rate * delta).astype(jnp.bfloat16)
+                    move.start()
 
     return pl.pallas_call(
         body,
-        in_specs=[in_hbm] * 8,
-        out_specs=[in_vmem] * 2,
-        out_shape=[
-            jax.ShapeDtypeStruct((below + query[0].shape[1], width), jnp.bfloat16),
-            jax.ShapeDtypeStruct((tiles(used), lanes), jnp.bfloat16),
-        ],
+        in_specs=[in_vmem] * (total + 2),
+        out_specs=in_hbm,
+        out_shape=jax.ShapeDtypeStruct((wide, count * rows), jnp.bfloat16),
         scratch_shapes=[
-            *scratch_of(mixed[0], mixed[1], rest),
-            *scratch_of(query[0], query[1], query[0].shape[1]),
-            *[pltpu.VMEM((used, lanes), jnp.float32)] * 2,
-            pltpu.SemaphoreType.DMA((2,)),
+            pltpu.VMEM((total, rank, rows), jnp.bfloat16),
+            pltpu.VMEM((total, wide, rows), jnp.bfloat16),
+            pltpu.SemaphoreType.DMA((cores * stacks,)),
+            pltpu.SemaphoreType.DMA((total,)),
         ],
         compiler_params=merge_params,
-    )(
-        *hbm(mixed[0], mixed[1].T, mixed[2], query[0], query[1].T, query[2]),
-        *hbm(*(a.reshape(used, lanes) for a in norms)),
-    )
-
-
-def merged_tail(key, value, rows_of_cores, cores, used):
-    under = key[0].shape[1] * (key[0].shape[0] // lanes)
-    packed = tiles(cores * used)
-    held = 4
-
-    def body(wk, lk, hk, wv, lv, hv, rows_ref, key_ref, value_ref, *scratch):
-        finish_key = merge_into(key_ref, 0, wk.shape[1], 0, wk, lk, hk, *scratch[:held])
-        finish_value = merge_into(value_ref, 0, wv.shape[1], 0, wv, lv, hv, *scratch[held : 2 * held])
-        packed_ref = scratch[2 * held]
-        packed_ref[...] = jnp.zeros_like(packed_ref)
-        rows = rows_ref[...].astype(jnp.float32)
-        tall = rows.shape[0] // cores
-        for core in range(cores):
-            packed_ref[core * used : (core + 1) * used, :] = rows[core * tall : core * tall + used]
-        key_ref[pl.ds(under, packed), :] = packed_ref[...].astype(jnp.bfloat16)
-        finish_key()
-        finish_value()
-
-    return pl.pallas_call(
-        body,
-        in_specs=[in_hbm] * 6 + [in_vmem],
-        out_specs=[in_vmem] * 2,
-        out_shape=[
-            jax.ShapeDtypeStruct((under + packed, lanes), jnp.bfloat16),
-            jax.ShapeDtypeStruct(value[0].shape[::-1], jnp.bfloat16),
-        ],
-        scratch_shapes=[
-            *scratch_of(key[0], key[1], key[0].shape[1]),
-            *scratch_of(value[0], value[1], value[0].shape[1]),
-            pltpu.VMEM((packed, lanes), jnp.float32),
-        ],
-        compiler_params=merge_params,
-    )(*hbm(key[0], key[1].T, key[2], value[0], value[1].T, value[2]), rows_of_cores)
+    )(*(w for _, w in pieces), sides, high)
 
 
 def place_body(count, moves, pieces_at, outs_at, *refs):
@@ -226,52 +254,56 @@
     return plan
 
 
-head = lanes
-chunk_names = ("head", "body", "key", "value")
+chunk_names = ("key", "mixed", "side", "query", "value")
+late = ("mixed", "side", "query", "value")
 
 
 def groups(count):
-    whole = (chunk_names,)
-    return [whole] * (count - 2) + [(chunk_names[:-2], chunk_names[-2:-1], chunk_names[-1:])]
+    return [(late,)] * (count - 2) + [(late[:2], late[2:3], late[3:])]
 
 
 def by_line(count, cores, query, key, value, mixed, norms):
     rows, columns = query[0].shape[0], mixed[0].shape[1]
     used = norms[0].size // lanes
-    packed = tiles(cores * used)
-    pieces = {}
-    pieces["head"] = merged_head(*mixed, head)
-    pieces["body"], row = merged_body(mixed, query, norms, head)
-    rows_of_cores = lax.all_gather(row, "width", axis=0, tiled=True)
-    pieces["key"], pieces["value"] = merged_tail(key, value, rows_of_cores, cores, used)
-    rest, halves = columns - head, mixed[0].shape[0] // rows
-    wide = {name: weight[0].shape[1] for name, weight in (("query", query), ("key", key), ("value", value))}
+    part = rows // cores
+    pieces = {"key": key[0]}
+    pieces["mixed"], pieces["side"] = merged([(*mixed, rows)], (key[1], *norms, part))
+    pieces["query"], pieces["value"] = merged([(*query, rows), (*value, rows)])
+    each = pieces["side"].shape[0]
+    wide = {name: weight[0].shape[1] for name, weight in (("query", query), ("value", value))}
     regions = {
-        "head": [("mixed", 0, head, columns, 0, 0, 0)],
-        "body": [("mixed", h * rest, rest, columns, head, 0, h * rows) for h in range(halves)]
-        + [("query", halves * rest, wide["query"], 0, 0, rows, 0)],
-        "key": [("key", b * wide["key"], wide["key"], 0, 0, rows, b * lanes) for b in range(rows // lanes)]
-        + [("norm", wide["key"] * (rows // lanes), packed, packed, 0, 0, 0)],
+        "mixed": [
+            ("mixed", h * columns, columns, columns, 0, 0, h * rows)
+            for h in range(mixed[0].shape[0] // rows)
+        ],
+        "side": [("side", 0, each, each, 0, 0, 0)],
+        "query": [("query", 0, wide["query"], 0, 0, rows, 0)],
         "value": [("value", 0, wide["value"], 0, 0, rows, 0)],
     }
     shapes = {name: (size, count * rows) for name, size in wide.items()}
     shapes["mixed"] = (count * columns, mixed[0].shape[0])
-    shapes["norm"] = (count * packed, lanes)
+    shapes["side"] = (count * each, lanes)
     plan = hops(count)
     outs = {}
     held = {name: {"a0": piece, "b0": piece} for name, piece in pieces.items()}
-    arrived = {name: [(regions[name], 0, piece)] for name, piece in pieces.items()}
+    raw = [(0, key[0])]
+    arrived = {name: [(regions[name], 0, pieces[name])] for name in late}
     for k, parts in enumerate(groups(count), start=1):
         for hop, source, pairs, offset in plan:
             if int(hop[1:]) == k:
                 for name in chunk_names:
                     held[name][hop] = lax.ppermute(held[name][source], "shard", pairs)
-                    arrived[name].append((regions[name], offset, held[name][hop]))
+                    if name in late:
+                        arrived[name].append((regions[name], offset, held[name][hop]))
+                raw.append((offset, held["key"][hop]))
         for part in parts:
             place(outs, shapes, [piece for name in part for piece in arrived[name]], count)
-        arrived = {name: [] for name in chunk_names}
-    serve_norm = outs["norm"].reshape(count, packed, lanes)[:, : cores * used].reshape(-1)
-    return outs["query"], outs["key"], outs["value"], outs["mixed"], serve_norm
+        arrived = {name: [] for name in late}
+    sides = lax.all_gather(outs["side"], "width", axis=0, tiled=True)
+    final_key = merged_pieces(raw, sides, key[2], count, cores, each)
+    sums = sides.reshape(cores, count, each, lanes)[:, :, each - tiles(used) :][:, :, :used]
+    serve_norm = sums.transpose(1, 0, 2, 3).reshape(-1)
+    return outs["query"], final_key, outs["value"], outs["mixed"], serve_norm
 
 
 def by_gather(count, cores, query, key, value, mixed, norms):
@@ -305,7 +337,7 @@
         gains = args[12].shape[0] // (mesh.shape["shift"] * count * cores)
         aligned = all(size % (2 * lanes) == 0 for size in (rows, columns, *narrow, gains))
         tall = args[9].shape[0] // (mesh.shape["shift"] * cores)
-        line = count > 2 and aligned and tall % rows == 0
+        line = count > 2 and aligned and tall % rows == 0 and rows % (cores * lanes) == 0
         program = jax.shard_map(
             functools.partial(on_device, by_line if line else by_gather, count, cores),
             mesh=mesh,

time: 188 us -> 258 us (1.37)
  waiting for transfers between devices: 106 us -> 179 us
  starting transfers between devices: 64.5 us -> 61.4 us
    ppermute x20 -> x25, waiting for transfers between devices: 106 us -> 179 us  [by_line(): held[name][hop] = lax.ppermute(held[name][source], 'shard', pairs)]
    ppermute x20 -> x25, starting transfers between devices: 64.5 us -> 61.4 us  [by_line(): held[name][hop] = lax.ppermute(held[name][source], 'shard', pairs)]
  transfers between devices with their start and end apart: 20 -> 25, of which waited for: 8 -> 7; matrix products, arithmetic and copies ran while one was open for 0% -> 0% of each run, Pallas kernels for 5% -> 3%
where the time goes in v9:
time: 258 us; the launch traced here: 257 us
  waiting for transfers between devices  179 us (69%)
  starting transfers between devices  61.4 us (24%)
  Pallas kernels  12.7 us (5%)
    ppermute x25, waiting for transfers between devices, by_line(): held[name][hop] = lax.ppermute(held[name][source], 'shard', pairs)  179 us
    ppermute x25, starting transfers between devices, by_line(): held[name][hop] = lax.ppermute(held[name][source], 'shard', pairs)  61.4 us
    pallas_call x5, Pallas kernels, place(): pl.pallas_call(functools.partial(place_body, count, moves, 0, len(arrays)...  6.51 us
  transfers between devices with their start and end apart: 25, of which 7 were waited for; matrix products, arithmetic and copies ran while one was open for 0% of the time, Pallas kernels for 3%

profile of v9, /device:TPU:0, one launch (start us, length us, event | category | flops | bytes accessed | tf_op | source)
XLA Modules:
  0.0 257.0 jit_solution(5584901736965011966)
XLA Ops:
  0.6 1.8 shard_map.174
  2.5 3.1 %collective-permute-start.5 = (bf16[1024,512]{1,0:T(8,128)(2,1)S(1)}, bf16[1024,512]{1,0:T(8,128)(2,1)S(1)}, u32[]{:S(2)}, u32[]{:S(2)}) collective-permute-start(bf16[1024,512]{1,0:T(8,128)(2,1)S(1)} %get-tuple-element.20.refs_0_), channel_id=1, source_target_pairs={{8,0},{0,8},{24,16},{16,24},{9,1},{1,9},{25,17},{17,25},{10,2},{2,... | collective-permute-start | bytes 3145736 | tf_op jit(solution)/shard_map/ppermute | solution.py:295
  5.6 2.4 shard_map.173
  8.8 0.7 collective-permute-start.11
  10.2 32.0 %collective-permute-start.9 = (bf16[40,128]{1,0:T(8,128)(2,1)S(1)}, bf16[40,128]{1,0:T(8,128)(2,1)S(1)}, u32[]{:S(2)}, u32[]{:S(2)}) collective-permute-start(bf16[40,128]{1,0:T(8,128)(2,1)S(1)} %get-tuple-element.21.refs_3_), channel_id=1, source_target_pairs={{8,0},{0,8},{24,16},{16,24},{9,1},{1,9},{25,17},{17,25},{10,2},{2,... | collective-permute-start | bytes 30728 | tf_op jit(solution)/shard_map/ppermute | solution.py:295
  42.1 9.3 %collective-permute-done.9.refs_4_ = bf16[40,128]{1,0:T(8,128)(2,1)S(1)} collective-permute-done((bf16[40,128]{1,0:T(8,128)(2,1)S(1)}, bf16[40,128]{1,0:T(8,128)(2,1)S(1)}, u32[]{:S(2)}, u32[]{:S(2)}) %collective-permute-start.9) | collective-permute-done | bytes 10272 | tf_op jit(solution)/shard_map/ppermute | solution.py:295
  52.1 1.3 collective-permute-start.8
  53.4 8.2 %collective-permute-done.8.refs_2_ = bf16[40,128]{1,0:T(8,128)(2,1)S(1)} collective-permute-done((bf16[40,128]{1,0:T(8,128)(2,1)S(1)}, bf16[40,128]{1,0:T(8,128)(2,1)S(1)}, u32[]{:S(2)}, u32[]{:S(2)}) %collective-permute-start.8) | collective-permute-done | bytes 10272 | tf_op jit(solution)/shard_map/ppermute | solution.py:295
  62.4 0.7 collective-permute-start.6
  63.1 4.2 %collective-permute-start.15 = (bf16[256,512]{1,0:T(8,128)(2,1)S(1)}, bf16[256,512]{1,0:T(8,128)(2,1)S(1)}, u32[]{:S(2)}, u32[]{:S(2)}) collective-permute-start(bf16[256,512]{1,0:T(8,128)(2,1)S(1)} %get-tuple-element.22.refs_9_), channel_id=1, source_target_pairs={{8,0},{0,8},{24,16},{16,24},{9,1},{1,9},{25,17},{17,25},{10,2},{2,... | collective-permute-start | bytes 786440 | tf_op jit(solution)/shard_map/ppermute | solution.py:295
  68.1 4.7 %collective-permute-done.15.refs_10_ = bf16[256,512]{1,0:T(8,128)(2,1)S(1)} collective-permute-done((bf16[256,512]{1,0:T(8,128)(2,1)S(1)}, bf16[256,512]{1,0:T(8,128)(2,1)S(1)}, u32[]{:S(2)}, u32[]{:S(2)}) %collective-permute-start.15) | collective-permute-done | bytes 262176 | tf_op jit(solution)/shard_map/ppermute | solution.py:295
  72.7 2.3 collective-permute-start.17
  75.0 4.6 %collective-permute-done.17.refs_1_ = bf16[512,256]{1,0:T(8,128)(2,1)S(1)} collective-permute-done((bf16[512,256]{1,0:T(8,128)(2,1)}, bf16[512,256]{1,0:T(8,128)(2,1)S(1)}, u32[]{:S(2)}, u32[]{:S(2)}) %collective-permute-start.17) | collective-permute-done | bytes 262176 | tf_op jit(solution)/shard_map/ppermute | solution.py:295
  81.0 1.3 collective-permute-start.12
  82.3 1.3 collective-permute-start.4
  83.6 1.3 collective-permute-start.22
  84.9 1.3 collective-permute-start.14
  86.2 1.3 collective-permute-start.2
  87.5 128.0 %collective-permute-done.14.refs_6_ = bf16[256,512]{1,0:T(8,128)(2,1)S(1)} collective-permute-done((bf16[256,512]{1,0:T(8,128)(2,1)S(1)}, bf16[256,512]{1,0:T(8,128)(2,1)S(1)}, u32[]{:S(2)}, u32[]{:S(2)}) %collective-permute-start.14) | collective-permute-done | bytes 262176 | tf_op jit(solution)/shard_map/ppermute | solution.py:295
  216.2 1.3 collective-permute-start.24
  217.5 21.5 %collective-permute-done.24.refs_0_ = bf16[256,512]{1,0:T(8,128)(2,1)S(1)} collective-permute-done((bf16[256,512]{1,0:T(8,128)(2,1)S(1)}, bf16[256,512]{1,0:T(8,128)(2,1)S(1)}, u32[]{:S(2)}, u32[]{:S(2)}) %collective-permute-start.24) | collective-permute-done | bytes 262176 | tf_op jit(solution)/shard_map/ppermute | solution.py:295
  239.0 1.3 collective-permute-start.19
  240.3 1.3 collective-permute-start.21
  241.6 1.3 collective-permute-start.23
  242.9 2.3 shard_map.175
  245.2 1.5 shard_map.176
  246.7 0.7 shard_map.180
  247.5 3.0 %collective-permute-done.23.refs_1_ = bf16[40,128]{1,0:T(8,128)(2,1)S(1)} collective-permute-done((bf16[40,128]{1,0:T(8,128)(2,1)S(1)}, bf16[40,128]{1,0:T(8,128)(2,1)S(1)}, u32[]{:S(2)}, u32[]{:S(2)}) %collective-permute-start.23) | collective-permute-done | bytes 10272 | tf_op jit(solution)/shard_map/ppermute | solution.py:295
  250.5 1.0 shard_map.178
  251.5 1.9 all_gather.3.refs_6_
  254.0 1.0 shard_map.177
  255.0 1.9 shard_map.179
  (33 shorter events, 6.3 us)
Async XLA Ops:
  2.5 59.9 %collective-permute-start.5 = (bf16[1024,512]{1,0:T(8,128)(2,1)S(1)}, bf16[1024,512]{1,0:T(8,128)(2,1)S(1)}, u32[]{:S(2)}, u32[]{:S(2)}) collective-permute-start(bf16[1024,512]{1,0:T(8,128)(2,1)S(1)} %get-tuple-element.20.refs_0_), channel_id=1, source_target_pairs={{8,0},{0,8},{24,16},{16,24},{9,1},{1,9},{25,17},{17,25},{10,2},{2,... | collective-permute-start | bytes 3145736 | tf_op jit(solution)/shard_map/ppermute | solution.py:295
  8.0 59.3 %collective-permute-start = (bf16[1024,512]{1,0:T(8,128)(2,1)S(1)}, bf16[1024,512]{1,0:T(8,128)(2,1)S(1)}, u32[]{:S(2)}, u32[]{:S(2)}) collective-permute-start(bf16[1024,512]{1,0:T(8,128)(2,1)S(1)} %get-tuple-element.19.refs_6_), channel_id=1, source_target_pairs={{8,0},{0,8},{24,16},{16,24},{9,1},{1,9},{25,17},{17,25},{10,2},{2,... | collective-permute-start | bytes 3145736 | tf_op jit(solution)/shard_map/ppermute | solution.py:295
  8.1 55.0 %collective-permute-start.13 = (bf16[256,512]{1,0:T(8,128)(2,1)S(1)}, bf16[256,512]{1,0:T(8,128)(2,1)S(1)}, u32[]{:S(2)}, u32[]{:S(2)}) collective-permute-start(bf16[256,512]{1,0:T(8,128)(2,1)S(1)} %get-tuple-element.22.refs_9_), channel_id=1, source_target_pairs={{16,8},{8,16},{17,9},{9,17},{18,10},{10,18},{19,11},{11,19},{20,12... | collective-permute-start | bytes 786440 | tf_op jit(solution)/shard_map/ppermute | solution.py:295
  8.8 72.2 %collective-permute-start.11 = (bf16[1024,512]{1,0:T(8,128)(2,1)S(1)}, bf16[1024,512]{1,0:T(8,128)(2,1)S(1)}, u32[]{:S(2)}, u32[]{:S(2)}) collective-permute-start(bf16[1024,512]{1,0:T(8,128)(2,1)S(1)} %get-tuple-element.19.refs_6_), channel_id=1, source_target_pairs={{16,8},{8,16},{17,9},{9,17},{18,10},{10,18},{19,11},{11,19},{20,12... | collective-permute-start | bytes 3145736 | tf_op jit(solution)/shard_map/ppermute | solution.py:295
  9.5 0.7 collective-permute-start.7
  10.2 41.3 %collective-permute-start.9 = (bf16[40,128]{1,0:T(8,128)(2,1)S(1)}, bf16[40,128]{1,0:T(8,128)(2,1)S(1)}, u32[]{:S(2)}, u32[]{:S(2)}) collective-permute-start(bf16[40,128]{1,0:T(8,128)(2,1)S(1)} %get-tuple-element.21.refs_3_), channel_id=1, source_target_pairs={{8,0},{0,8},{24,16},{16,24},{9,1},{1,9},{25,17},{17,25},{10,2},{2,... | collective-permute-start | bytes 30728 | tf_op jit(solution)/shard_map/ppermute | solution.py:295
  51.4 0.7 collective-permute-start.10
  52.1 9.5 %collective-permute-start.8 = (bf16[40,128]{1,0:T(8,128)(2,1)S(1)}, bf16[40,128]{1,0:T(8,128)(2,1)S(1)}, u32[]{:S(2)}, u32[]{:S(2)}) collective-permute-start(bf16[40,128]{1,0:T(8,128)(2,1)S(1)} %collective-permute-done.7.refs_5_), channel_id=1, source_target_pairs={{8,0},{16,24},{9,1},{17,25},{10,2},{18,26},{11,3},{19,27},{12,4},{... | collective-permute-start | bytes 30728 | tf_op jit(solution)/shard_map/ppermute | solution.py:295
  61.7 20.6 %collective-permute-start.3 = (bf16[1024,512]{1,0:T(8,128)(2,1)S(1)}, bf16[1024,512]{1,0:T(8,128)(2,1)S(1)}, u32[]{:S(2)}, u32[]{:S(2)}) collective-permute-start(bf16[1024,512]{1,0:T(8,128)(2,1)S(1)} %get-tuple-element.20.refs_0_), channel_id=1, source_target_pairs={{16,8},{8,16},{17,9},{9,17},{18,10},{10,18},{19,11},{11,19},{20,12... | collective-permute-start | bytes 3145736 | tf_op jit(solution)/shard_map/ppermute | solution.py:295
  62.4 21.2 %collective-permute-start.6 = (bf16[1024,512]{1,0:T(8,128)(2,1)S(1)}, bf16[1024,512]{1,0:T(8,128)(2,1)S(1)}, u32[]{:S(2)}, u32[]{:S(2)}) collective-permute-start(bf16[1024,512]{1,0:T(8,128)(2,1)S(1)} %collective-permute-done.5.refs_1_), channel_id=1, source_target_pairs={{16,8},{8,16},{17,9},{9,17},{18,10},{10,18},{19,11},{11,19},{20,12... | collective-permute-start | bytes 3145736 | tf_op jit(solution)/shard_map/ppermute | solution.py:295
  63.1 9.6 %collective-permute-start.15 = (bf16[256,512]{1,0:T(8,128)(2,1)S(1)}, bf16[256,512]{1,0:T(8,128)(2,1)S(1)}, u32[]{:S(2)}, u32[]{:S(2)}) collective-permute-start(bf16[256,512]{1,0:T(8,128)(2,1)S(1)} %get-tuple-element.22.refs_9_), channel_id=1, source_target_pairs={{8,0},{0,8},{24,16},{16,24},{9,1},{1,9},{25,17},{17,25},{10,2},{2,... | collective-permute-start | bytes 786440 | tf_op jit(solution)/shard_map/ppermute | solution.py:295
  67.3 18.9 %collective-permute-start.1 = (bf16[1024,512]{1,0:T(8,128)(2,1)S(1)}, bf16[1024,512]{1,0:T(8,128)(2,1)S(1)}, u32[]{:S(2)}, u32[]{:S(2)}) collective-permute-start(bf16[1024,512]{1,0:T(8,128)(2,1)S(1)} %collective-permute-done.refs_7_), channel_id=1, source_target_pairs={{16,8},{8,16},{17,9},{9,17},{18,10},{10,18},{19,11},{11,19},{20,12... | collective-permute-start | bytes 3145736 | tf_op jit(solution)/shard_map/ppermute | solution.py:295
  72.7 6.9 %collective-permute-start.17 = (bf16[512,256]{1,0:T(8,128)(2,1)}, bf16[512,256]{1,0:T(8,128)(2,1)S(1)}, u32[]{:S(2)}, u32[]{:S(2)}) collective-permute-start(bf16[512,256]{1,0:T(8,128)(2,1)} %refs_0_.5), channel_id=1, source_target_pairs={{8,0},{0,8},{24,16},{16,24},{9,1},{1,9},{25,17},{17,25},{10,2},{2,... | collective-permute-start | bytes 786440 | tf_op jit(solution)/shard_map/ppermute | solution.py:295
  79.6 0.7 collective-permute-start.18
  80.3 4.6 %collective-permute-start.16 = (bf16[256,512]{1,0:T(8,128)(2,1)S(1)}, bf16[256,512]{1,0:T(8,128)(2,1)S(1)}, u32[]{:S(2)}, u32[]{:S(2)}) collective-permute-start(bf16[256,512]{1,0:T(8,128)(2,1)S(1)} %collective-permute-done.15.refs_10_), channel_id=1, source_target_pairs={{16,8},{8,16},{17,9},{9,17},{18,10},{10,18},{19,11},{11,19},{20,12... | collective-permute-start | bytes 786440 | tf_op jit(solution)/shard_map/ppermute | solution.py:295
  81.0 159.3 %collective-permute-start.12 = (bf16[1024,512]{1,0:T(8,128)(2,1)S(1)}, bf16[1024,512]{1,0:T(8,128)(2,1)S(1)}, u32[]{:S(2)}, u32[]{:S(2)}) collective-permute-start(bf16[1024,512]{1,0:T(8,128)(2,1)S(1)} %collective-permute-done.11.refs_8_), channel_id=1, source_target_pairs={{8,0},{16,24},{9,1},{17,25},{10,2},{18,26},{11,3},{19,27},{12,4},{... | collective-permute-start | bytes 3145736 | tf_op jit(solution)/shard_map/ppermute | solution.py:295
  82.3 159.3 %collective-permute-start.4 = (bf16[1024,512]{1,0:T(8,128)(2,1)S(1)}, bf16[1024,512]{1,0:T(8,128)(2,1)S(1)}, u32[]{:S(2)}, u32[]{:S(2)}) collective-permute-start(bf16[1024,512]{1,0:T(8,128)(2,1)S(1)} %collective-permute-done.3.refs_2_), channel_id=1, source_target_pairs={{8,0},{16,24},{9,1},{17,25},{10,2},{18,26},{11,3},{19,27},{12,4},{... | collective-permute-start | bytes 3145736 | tf_op jit(solution)/shard_map/ppermute | solution.py:295
  83.6 166.9 %collective-permute-start.22 = (bf16[1024,512]{1,0:T(8,128)(2,1)S(1)}, bf16[1024,512]{1,0:T(8,128)(2,1)S(1)}, u32[]{:S(2)}, u32[]{:S(2)}) collective-permute-start(bf16[1024,512]{1,0:T(8,128)(2,1)S(1)} %collective-permute-done.6.refs_1_), channel_id=1, source_target_pairs={{8,0},{16,24},{9,1},{17,25},{10,2},{18,26},{11,3},{19,27},{12,4},{... | collective-permute-start | bytes 3145736 | tf_op jit(solution)/shard_map/ppermute | solution.py:295
  84.9 130.6 %collective-permute-start.14 = (bf16[256,512]{1,0:T(8,128)(2,1)S(1)}, bf16[256,512]{1,0:T(8,128)(2,1)S(1)}, u32[]{:S(2)}, u32[]{:S(2)}) collective-permute-start(bf16[256,512]{1,0:T(8,128)(2,1)S(1)} %collective-permute-done.13.refs_11_), channel_id=1, source_target_pairs={{8,0},{16,24},{9,1},{17,25},{10,2},{18,26},{11,3},{19,27},{12,4},{... | collective-permute-start | bytes 786440 | tf_op jit(solution)/shard_map/ppermute | solution.py:295
  86.2 167.7 %collective-permute-start.2 = (bf16[1024,512]{1,0:T(8,128)(2,1)S(1)}, bf16[1024,512]{1,0:T(8,128)(2,1)S(1)}, u32[]{:S(2)}, u32[]{:S(2)}) collective-permute-start(bf16[1024,512]{1,0:T(8,128)(2,1)S(1)} %collective-permute-done.1.refs_5_), channel_id=1, source_target_pairs={{8,0},{16,24},{9,1},{17,25},{10,2},{18,26},{11,3},{19,27},{12,4},{... | collective-permute-start | bytes 3145736 | tf_op jit(solution)/shard_map/ppermute | solution.py:295
  215.5 0.7 collective-permute-start.20
  216.2 22.8 %collective-permute-start.24 = (bf16[256,512]{1,0:T(8,128)(2,1)S(1)}, bf16[256,512]{1,0:T(8,128)(2,1)S(1)}, u32[]{:S(2)}, u32[]{:S(2)}) collective-permute-start(bf16[256,512]{1,0:T(8,128)(2,1)S(1)} %collective-permute-done.16.refs_7_), channel_id=1, source_target_pairs={{8,0},{16,24},{9,1},{17,25},{10,2},{18,26},{11,3},{19,27},{12,4},{... | collective-permute-start | bytes 786440 | tf_op jit(solution)/shard_map/ppermute | solution.py:295
  239.0 15.9 %collective-permute-start.19 = (bf16[512,256]{1,0:T(8,128)(2,1)S(1)}, bf16[512,256]{1,0:T(8,128)(2,1)S(1)}, u32[]{:S(2)}, u32[]{:S(2)}) collective-permute-start(bf16[512,256]{1,0:T(8,128)(2,1)S(1)} %collective-permute-done.18.refs_2_), channel_id=1, source_target_pairs={{8,0},{16,24},{9,1},{17,25},{10,2},{18,26},{11,3},{19,27},{12,4},{... | collective-permute-start | bytes 786440 | tf_op jit(solution)/shard_map/ppermute | solution.py:295
  240.3 14.7 %collective-permute-start.21 = (bf16[512,256]{1,0:T(8,128)(2,1)S(1)}, bf16[512,256]{1,0:T(8,128)(2,1)S(1)}, u32[]{:S(2)}, u32[]{:S(2)}) collective-permute-start(bf16[512,256]{1,0:T(8,128)(2,1)S(1)} %collective-permute-done.20.refs_4_), channel_id=1, source_target_pairs={{8,0},{16,24},{9,1},{17,25},{10,2},{18,26},{11,3},{19,27},{12,4},{... | collective-permute-start | bytes 786440 | tf_op jit(solution)/shard_map/ppermute | solution.py:295
  241.6 8.9 %collective-permute-start.23 = (bf16[40,128]{1,0:T(8,128)(2,1)S(1)}, bf16[40,128]{1,0:T(8,128)(2,1)S(1)}, u32[]{:S(2)}, u32[]{:S(2)}) collective-permute-start(bf16[40,128]{1,0:T(8,128)(2,1)S(1)} %collective-permute-done.10.refs_3_), channel_id=1, source_target_pairs={{8,0},{16,24},{9,1},{17,25},{10,2},{18,26},{11,3},{19,27},{12,4},{... | collective-permute-start | bytes 30728 | tf_op jit(solution)/shard_map/ppermute | solution.py:295
  253.9 1.1 copy-start
  253.9 1.1 copy-start.1

commit v10 on v9

--- a/solution.py
+++ b/solution.py
@@ -88,8 +88,9 @@
         part, rank, used = extra[3], extra[0].shape[1], extra[1].size // lanes
         blocks_of_low = part // lanes
         operands += hbm(extra[0].T, *(a.reshape(used, lanes) for a in extra[1:3]))
-        side = rank * blocks_of_low
-        shapes.append(jax.ShapeDtypeStruct((side + tiles(used), lanes), jnp.bfloat16))
+        under = shapes[0].shape[0]
+        side = under + rank * blocks_of_low
+        shapes[0] = jax.ShapeDtypeStruct((side + tiles(used), lanes), jnp.bfloat16)
         scratch_shapes += [pltpu.VMEM((rank, part), jnp.bfloat16)]
         scratch_shapes += [pltpu.VMEM((used, lanes), jnp.float32)] * 2
         scratch_shapes += [pltpu.SemaphoreType.DMA((3,))]
@@ -120,9 +121,9 @@
                 copy.wait()
             low_held, train_held, step_held = targets
             for j in range(blocks_of_low):
-                outs[-1][pl.ds(j * rank, rank), :] = low_held[:, pl.ds(j * lanes, lanes)]
-            outs[-1][pl.ds(side, tiles(used)), :] = jnp.zeros((tiles(used), lanes), jnp.bfloat16)
-            outs[-1][pl.ds(side, used), :] = (train_held[...] + step_held[...]).astype(jnp.bfloat16)
+                outs[0][pl.ds(under + j * rank, rank), :] = low_held[:, pl.ds(j * lanes, lanes)]
+            outs[0][pl.ds(side, tiles(used)), :] = jnp.zeros((tiles(used), lanes), jnp.bfloat16)
+            outs[0][pl.ds(side, used), :] = (train_held[...] + step_held[...]).astype(jnp.bfloat16)
 
     return pl.pallas_call(
         body,
@@ -254,12 +255,12 @@
     return plan
 
 
-chunk_names = ("key", "mixed", "side", "query", "value")
-late = ("mixed", "side", "query", "value")
+chunk_names = ("key", "mixed", "query", "value")
+late = chunk_names[1:]
 
 
 def groups(count):
-    return [(late,)] * (count - 2) + [(late[:2], late[2:3], late[3:])]
+    return [(late,)] * (count - 2) + [(late[:1], late[1:2], late[2:])]
 
 
 def by_line(count, cores, query, key, value, mixed, norms):
@@ -267,16 +268,16 @@
     used = norms[0].size // lanes
     part = rows // cores
     pieces = {"key": key[0]}
-    pieces["mixed"], pieces["side"] = merged([(*mixed, rows)], (key[1], *norms, part))
+    (pieces["mixed"],) = merged([(*mixed, lanes)], (key[1], *norms, part))
     pieces["query"], pieces["value"] = merged([(*query, rows), (*value, rows)])
-    each = pieces["side"].shape[0]
+    stacks = mixed[0].shape[0] // lanes
+    each = pieces["mixed"].shape[0] - stacks * columns
     wide = {name: weight[0].shape[1] for name, weight in (("query", query), ("value", value))}
     regions = {
         "mixed": [
-            ("mixed", h * columns, columns, columns, 0, 0, h * rows)
-            for h in range(mixed[0].shape[0] // rows)
+            *(("mixed", h * columns, columns, columns, 0, 0, h * lanes) for h in range(stacks)),
+            ("side", stacks * columns, each, each, 0, 0, 0),
         ],
-        "side": [("side", 0, each, each, 0, 0, 0)],
         "query": [("query", 0, wide["query"], 0, 0, rows, 0)],
         "value": [("value", 0, wide["value"], 0, 0, rows, 0)],
     }

time: 258 us -> 240 us (0.930)
  waiting for transfers between devices: 179 us -> 147 us
  starting transfers between devices: 61.4 us -> 76 us
    ppermute x25 -> x20, waiting for transfers between devices: 179 us -> 147 us  [by_line(): held[name][hop] = lax.ppermute(held[name][source], 'shard', pairs)]
    ppermute x25 -> x20, starting transfers between devices: 61.4 us -> 76 us  [by_line(): held[name][hop] = lax.ppermute(held[name][source], 'shard', pairs)]
  transfers between devices with their start and end apart: 25 -> 20, of which waited for: 7 -> 7; matrix products, arithmetic and copies ran while one was open for 0% -> 0% of each run, Pallas kernels for 3% -> 4%
where the time goes in v10:
time: 240 us
  waiting for transfers between devices  147 us (61%)
  starting transfers between devices  76 us (32%)
  Pallas kernels  13 us (5%)
    ppermute x20, waiting for transfers between devices, by_line(): held[name][hop] = lax.ppermute(held[name][source], 'shard', pairs)  147 us
    ppermute x20, starting transfers between devices, by_line(): held[name][hop] = lax.ppermute(held[name][source], 'shard', pairs)  76 us
    pallas_call x5, Pallas kernels, place(): pl.pallas_call(functools.partial(place_body, count, moves, 0, len(arrays)...  6.84 us
  transfers between devices with their start and end apart: 20, of which 7 were waited for; matrix products, arithmetic and copies ran while one was open for 0% of the time, Pallas kernels for 4%

profile of v10, /device:TPU:0, one launch (start us, length us, event | category | flops | bytes accessed | tf_op | source)
XLA Modules:
  0.0 239.6 jit_solution(1603641023015790219)
XLA Ops:
  0.6 1.8 shard_map.174.refs_0_
  2.5 3.1 %collective-permute-start.5 = (bf16[4136,128]{1,0:T(8,128)(2,1)S(1)}, bf16[4136,128]{1,0:T(8,128)(2,1)S(1)}, u32[]{:S(2)}, u32[]{:S(2)}) collective-permute-start(bf16[4136,128]{1,0:T(8,128)(2,1)S(1)} %shard_map.174.refs_0_), channel_id=1, source_target_pairs={{8,0},{0,8},{24,16},{16,24},{9,1},{1,9},{25,17},{17,25},{10,2},{2,... | collective-permute-start | bytes 3176456 | tf_op jit(solution)/shard_map/ppermute | solution.py:296
  5.6 2.4 %shard_map.173 = (bf16[1024,512]{1,0:T(8,128)(2,1)S(1)}, bf16[256,512]{1,0:T(8,128)(2,1)S(1)}) custom-call(bf16[512,1024]{1,0:T(8,128)(2,1)} %refs_0_.3, bf16[16,512]{1,0:T(8,128)(2,1)} %bitcast.13, bf16[16,1024]{1,0:T(8,128)(2,1)} %refs_2_.2, bf16[512,256]{1,0:T(8,128)(2,1)} %refs_3_.1, bf16[16,512]{1,0:T(8,128)(2,1)} %bitcast.14, bf16[16,256]{1,0:T(8,128)(2,1)} %refs_5_.1), custom_call_target="tpu_custom_call" | custom-call | tf_op jit(solution)/shard_map/pallas_call | solution.py:128
  8.1 0.7 collective-permute-start.3
  8.8 0.7 collective-permute-start.7
  9.5 20.3 %collective-permute-done.5.refs_1_ = bf16[4136,128]{1,0:T(8,128)(2,1)S(1)} collective-permute-done((bf16[4136,128]{1,0:T(8,128)(2,1)S(1)}, bf16[4136,128]{1,0:T(8,128)(2,1)S(1)}, u32[]{:S(2)}, u32[]{:S(2)}) %collective-permute-start.5) | collective-permute-done | bytes 1058848 | tf_op jit(solution)/shard_map/ppermute | solution.py:296
  29.8 0.7 collective-permute-start.6
  30.5 4.9 %collective-permute-start.11 = (bf16[256,512]{1,0:T(8,128)(2,1)S(1)}, bf16[256,512]{1,0:T(8,128)(2,1)S(1)}, u32[]{:S(2)}, u32[]{:S(2)}) collective-permute-start(bf16[256,512]{1,0:T(8,128)(2,1)S(1)} %get-tuple-element.18.refs_6_), channel_id=1, source_target_pairs={{8,0},{0,8},{24,16},{16,24},{9,1},{1,9},{25,17},{17,25},{10,2},{2,... | collective-permute-start | bytes 786440 | tf_op jit(solution)/shard_map/ppermute | solution.py:296
  35.4 16.9 %collective-permute-done.refs_4_ = bf16[1024,512]{1,0:T(8,128)(2,1)S(1)} collective-permute-done((bf16[1024,512]{1,0:T(8,128)(2,1)S(1)}, bf16[1024,512]{1,0:T(8,128)(2,1)S(1)}, u32[]{:S(2)}, u32[]{:S(2)}) %collective-permute-start) | collective-permute-done | bytes 1048608 | tf_op jit(solution)/shard_map/ppermute | solution.py:296
  52.3 0.7 collective-permute-start.1
  53.0 4.0 %collective-permute-done.11.refs_7_ = bf16[256,512]{1,0:T(8,128)(2,1)S(1)} collective-permute-done((bf16[256,512]{1,0:T(8,128)(2,1)S(1)}, bf16[256,512]{1,0:T(8,128)(2,1)S(1)}, u32[]{:S(2)}, u32[]{:S(2)}) %collective-permute-start.11) | collective-permute-done | bytes 262176 | tf_op jit(solution)/shard_map/ppermute | solution.py:296
  57.7 52.0 %collective-permute-start.13 = (bf16[512,256]{1,0:T(8,128)(2,1)}, bf16[512,256]{1,0:T(8,128)(2,1)S(1)}, u32[]{:S(2)}, u32[]{:S(2)}) collective-permute-start(bf16[512,256]{1,0:T(8,128)(2,1)} %refs_0_.5), channel_id=1, source_target_pairs={{8,0},{0,8},{24,16},{16,24},{9,1},{1,9},{25,17},{17,25},{10,2},{2,... | collective-permute-start | bytes 786440 | tf_op jit(solution)/shard_map/ppermute | solution.py:296
  109.8 5.1 %collective-permute-done.13.refs_1_ = bf16[512,256]{1,0:T(8,128)(2,1)S(1)} collective-permute-done((bf16[512,256]{1,0:T(8,128)(2,1)}, bf16[512,256]{1,0:T(8,128)(2,1)S(1)}, u32[]{:S(2)}, u32[]{:S(2)}) %collective-permute-start.13) | collective-permute-done | bytes 262176 | tf_op jit(solution)/shard_map/ppermute | solution.py:296
  115.6 1.3 collective-permute-start.4
  116.9 1.3 collective-permute-start.8
  118.2 1.3 collective-permute-start.18
  119.5 0.7 collective-permute-start.12
  120.2 1.3 collective-permute-start.2
  121.5 1.3 collective-permute-start.10
  122.8 92.6 %collective-permute-done.10.refs_4_ = bf16[256,512]{1,0:T(8,128)(2,1)S(1)} collective-permute-done((bf16[256,512]{1,0:T(8,128)(2,1)S(1)}, bf16[256,512]{1,0:T(8,128)(2,1)S(1)}, u32[]{:S(2)}, u32[]{:S(2)}) %collective-permute-start.10) | collective-permute-done | bytes 262176 | tf_op jit(solution)/shard_map/ppermute | solution.py:296
  216.1 1.3 collective-permute-start.19
  217.4 1.3 collective-permute-start.15
  218.7 1.3 collective-permute-start.17
  220.0 2.5 %shard_map.175 = (bf16[2048,1024]{1,0:T(8,128)(2,1)}, bf16[160,128]{1,0:T(8,128)(2,1)S(1)}, bf16[1024,2048]{1,0:T(8,128)(2,1)}, bf16[256,2048]{1,0:T(8,128)(2,1)}) custom-call(bf16[4136,128]{1,0:T(8,128)(2,1)S(1)} %shard_map.174.refs_0_, bf16[4136,128]{1,0:T(8,128)(2,1)S(1)} %collective-permute-done.5.refs_1_, ...), custom_call_target="tpu_custom_call" | custom-call | tf_op jit(solution)/shard_map/pallas_call | solution.py:230
  222.5 1.6 shard_map.176
  224.1 7.5 %collective-permute-done.19.refs_0_ = bf16[256,512]{1,0:T(8,128)(2,1)S(1)} collective-permute-done((bf16[256,512]{1,0:T(8,128)(2,1)S(1)}, bf16[256,512]{1,0:T(8,128)(2,1)S(1)}, u32[]{:S(2)}, u32[]{:S(2)}) %collective-permute-start.19) | collective-permute-done | bytes 262176 | tf_op jit(solution)/shard_map/ppermute | solution.py:296
  231.6 0.7 shard_map.180
  232.4 1.0 shard_map.177
  233.4 1.1 shard_map.178
  234.5 1.9 all_gather.3.refs_6_
  237.0 0.8 collective-permute-done.17.refs_5_
  237.7 1.9 shard_map.179
  (23 shorter events, 2.7 us)
Async XLA Ops:
  2.5 27.3 %collective-permute-start.5 = (bf16[4136,128]{1,0:T(8,128)(2,1)S(1)}, bf16[4136,128]{1,0:T(8,128)(2,1)S(1)}, u32[]{:S(2)}, u32[]{:S(2)}) collective-permute-start(bf16[4136,128]{1,0:T(8,128)(2,1)S(1)} %shard_map.174.refs_0_), channel_id=1, source_target_pairs={{8,0},{0,8},{24,16},{16,24},{9,1},{1,9},{25,17},{17,25},{10,2},{2,... | collective-permute-start | bytes 3176456 | tf_op jit(solution)/shard_map/ppermute | solution.py:296
  8.0 44.3 %collective-permute-start = (bf16[1024,512]{1,0:T(8,128)(2,1)S(1)}, bf16[1024,512]{1,0:T(8,128)(2,1)S(1)}, u32[]{:S(2)}, u32[]{:S(2)}) collective-permute-start(bf16[1024,512]{1,0:T(8,128)(2,1)S(1)} %get-tuple-element.17.refs_3_), channel_id=1, source_target_pairs={{8,0},{0,8},{24,16},{16,24},{9,1},{1,9},{25,17},{17,25},{10,2},{2,... | collective-permute-start | bytes 3145736 | tf_op jit(solution)/shard_map/ppermute | solution.py:296
  8.1 107.5 %collective-permute-start.3 = (bf16[4136,128]{1,0:T(8,128)(2,1)S(1)}, bf16[4136,128]{1,0:T(8,128)(2,1)S(1)}, u32[]{:S(2)}, u32[]{:S(2)}) collective-permute-start(bf16[4136,128]{1,0:T(8,128)(2,1)S(1)} %shard_map.174.refs_0_), channel_id=1, source_target_pairs={{16,8},{8,16},{17,9},{9,17},{18,10},{10,18},{19,11},{11,19},{20,12... | collective-permute-start | bytes 3176456 | tf_op jit(solution)/shard_map/ppermute | solution.py:296
  8.8 108.1 %collective-permute-start.7 = (bf16[1024,512]{1,0:T(8,128)(2,1)S(1)}, bf16[1024,512]{1,0:T(8,128)(2,1)S(1)}, u32[]{:S(2)}, u32[]{:S(2)}) collective-permute-start(bf16[1024,512]{1,0:T(8,128)(2,1)S(1)} %get-tuple-element.17.refs_3_), channel_id=1, source_target_pairs={{16,8},{8,16},{17,9},{9,17},{18,10},{10,18},{19,11},{11,19},{20,12... | collective-permute-start | bytes 3145736 | tf_op jit(solution)/shard_map/ppermute | solution.py:296
  29.8 88.4 %collective-permute-start.6 = (bf16[4136,128]{1,0:T(8,128)(2,1)S(1)}, bf16[4136,128]{1,0:T(8,128)(2,1)S(1)}, u32[]{:S(2)}, u32[]{:S(2)}) collective-permute-start(bf16[4136,128]{1,0:T(8,128)(2,1)S(1)} %collective-permute-done.5.refs_1_), channel_id=1, source_target_pairs={{16,8},{8,16},{17,9},{9,17},{18,10},{10,18},{19,11},{11,19},{20,12... | collective-permute-start | bytes 3176456 | tf_op jit(solution)/shard_map/ppermute | solution.py:296
  30.5 26.5 %collective-permute-start.11 = (bf16[256,512]{1,0:T(8,128)(2,1)S(1)}, bf16[256,512]{1,0:T(8,128)(2,1)S(1)}, u32[]{:S(2)}, u32[]{:S(2)}) collective-permute-start(bf16[256,512]{1,0:T(8,128)(2,1)S(1)} %get-tuple-element.18.refs_6_), channel_id=1, source_target_pairs={{8,0},{0,8},{24,16},{16,24},{9,1},{1,9},{25,17},{17,25},{10,2},{2,... | collective-permute-start | bytes 786440 | tf_op jit(solution)/shard_map/ppermute | solution.py:296
  52.3 67.9 %collective-permute-start.1 = (bf16[1024,512]{1,0:T(8,128)(2,1)S(1)}, bf16[1024,512]{1,0:T(8,128)(2,1)S(1)}, u32[]{:S(2)}, u32[]{:S(2)}) collective-permute-start(bf16[1024,512]{1,0:T(8,128)(2,1)S(1)} %collective-permute-done.refs_4_), channel_id=1, source_target_pairs={{16,8},{8,16},{17,9},{9,17},{18,10},{10,18},{19,11},{11,19},{20,12... | collective-permute-start | bytes 3145736 | tf_op jit(solution)/shard_map/ppermute | solution.py:296
  57.1 0.7 collective-permute-start.9
  57.7 57.1 %collective-permute-start.13 = (bf16[512,256]{1,0:T(8,128)(2,1)}, bf16[512,256]{1,0:T(8,128)(2,1)S(1)}, u32[]{:S(2)}, u32[]{:S(2)}) collective-permute-start(bf16[512,256]{1,0:T(8,128)(2,1)} %refs_0_.5), channel_id=1, source_target_pairs={{8,0},{0,8},{24,16},{16,24},{9,1},{1,9},{25,17},{17,25},{10,2},{2,... | collective-permute-start | bytes 786440 | tf_op jit(solution)/shard_map/ppermute | solution.py:296
  114.9 4.6 %collective-permute-start.14 = (bf16[512,256]{1,0:T(8,128)(2,1)}, bf16[512,256]{1,0:T(8,128)(2,1)S(1)}, u32[]{:S(2)}, u32[]{:S(2)}) collective-permute-start(bf16[512,256]{1,0:T(8,128)(2,1)} %refs_0_.5), channel_id=1, source_target_pairs={{16,8},{8,16},{17,9},{9,17},{18,10},{10,18},{19,11},{11,19},{20,12... | collective-permute-start | bytes 786440 | tf_op jit(solution)/shard_map/ppermute | solution.py:296
  115.6 103.2 %collective-permute-start.4 = (bf16[4136,128]{1,0:T(8,128)(2,1)S(1)}, bf16[4136,128]{1,0:T(8,128)(2,1)S(1)}, u32[]{:S(2)}, u32[]{:S(2)}) collective-permute-start(bf16[4136,128]{1,0:T(8,128)(2,1)S(1)} %collective-permute-done.3.refs_2_), channel_id=1, source_target_pairs={{8,0},{16,24},{9,1},{17,25},{10,2},{18,26},{11,3},{19,27},{12,4},{... | collective-permute-start | bytes 3176456 | tf_op jit(solution)/shard_map/ppermute | solution.py:296
  116.9 100.5 %collective-permute-start.8 = (bf16[1024,512]{1,0:T(8,128)(2,1)S(1)}, bf16[1024,512]{1,0:T(8,128)(2,1)S(1)}, u32[]{:S(2)}, u32[]{:S(2)}) collective-permute-start(bf16[1024,512]{1,0:T(8,128)(2,1)S(1)} %collective-permute-done.7.refs_5_), channel_id=1, source_target_pairs={{8,0},{16,24},{9,1},{17,25},{10,2},{18,26},{11,3},{19,27},{12,4},{... | collective-permute-start | bytes 3145736 | tf_op jit(solution)/shard_map/ppermute | solution.py:296
  118.2 115.2 %collective-permute-start.18 = (bf16[4136,128]{1,0:T(8,128)(2,1)S(1)}, bf16[4136,128]{1,0:T(8,128)(2,1)S(1)}, u32[]{:S(2)}, u32[]{:S(2)}) collective-permute-start(bf16[4136,128]{1,0:T(8,128)(2,1)S(1)} %collective-permute-done.6.refs_1_), channel_id=1, source_target_pairs={{8,0},{16,24},{9,1},{17,25},{10,2},{18,26},{11,3},{19,27},{12,4},{... | collective-permute-start | bytes 3176456 | tf_op jit(solution)/shard_map/ppermute | solution.py:296
  119.5 2.0 collective-permute-start.12
  120.2 112.2 %collective-permute-start.2 = (bf16[1024,512]{1,0:T(8,128)(2,1)S(1)}, bf16[1024,512]{1,0:T(8,128)(2,1)S(1)}, u32[]{:S(2)}, u32[]{:S(2)}) collective-permute-start(bf16[1024,512]{1,0:T(8,128)(2,1)S(1)} %collective-permute-done.1.refs_3_), channel_id=1, source_target_pairs={{8,0},{16,24},{9,1},{17,25},{10,2},{18,26},{11,3},{19,27},{12,4},{... | collective-permute-start | bytes 3145736 | tf_op jit(solution)/shard_map/ppermute | solution.py:296
  121.5 93.9 %collective-permute-start.10 = (bf16[256,512]{1,0:T(8,128)(2,1)S(1)}, bf16[256,512]{1,0:T(8,128)(2,1)S(1)}, u32[]{:S(2)}, u32[]{:S(2)}) collective-permute-start(bf16[256,512]{1,0:T(8,128)(2,1)S(1)} %collective-permute-done.9.refs_8_), channel_id=1, source_target_pairs={{8,0},{16,24},{9,1},{17,25},{10,2},{18,26},{11,3},{19,27},{12,4},{... | collective-permute-start | bytes 786440 | tf_op jit(solution)/shard_map/ppermute | solution.py:296
  215.4 0.7 collective-permute-start.16
  216.1 15.5 %collective-permute-start.19 = (bf16[256,512]{1,0:T(8,128)(2,1)S(1)}, bf16[256,512]{1,0:T(8,128)(2,1)S(1)}, u32[]{:S(2)}, u32[]{:S(2)}) collective-permute-start(bf16[256,512]{1,0:T(8,128)(2,1)S(1)} %collective-permute-done.12.refs_5_), channel_id=1, source_target_pairs={{8,0},{16,24},{9,1},{17,25},{10,2},{18,26},{11,3},{19,27},{12,4},{... | collective-permute-start | bytes 786440 | tf_op jit(solution)/shard_map/ppermute | solution.py:296
  217.4 19.5 %collective-permute-start.15 = (bf16[512,256]{1,0:T(8,128)(2,1)S(1)}, bf16[512,256]{1,0:T(8,128)(2,1)S(1)}, u32[]{:S(2)}, u32[]{:S(2)}) collective-permute-start(bf16[512,256]{1,0:T(8,128)(2,1)S(1)} %collective-permute-done.14.refs_2_), channel_id=1, source_target_pairs={{8,0},{16,24},{9,1},{17,25},{10,2},{18,26},{11,3},{19,27},{12,4},{... | collective-permute-start | bytes 786440 | tf_op jit(solution)/shard_map/ppermute | solution.py:296
  218.7 19.0 %collective-permute-start.17 = (bf16[512,256]{1,0:T(8,128)(2,1)S(1)}, bf16[512,256]{1,0:T(8,128)(2,1)S(1)}, u32[]{:S(2)}, u32[]{:S(2)}) collective-permute-start(bf16[512,256]{1,0:T(8,128)(2,1)S(1)} %collective-permute-done.16.refs_4_), channel_id=1, source_target_pairs={{8,0},{16,24},{9,1},{17,25},{10,2},{18,26},{11,3},{19,27},{12,4},{... | collective-permute-start | bytes 786440 | tf_op jit(solution)/shard_map/ppermute | solution.py:296
  233.4 4.4 %copy-start = (bf16[512,256]{1,0:T(8,128)(2,1)S(1)}, bf16[512,256]{1,0:T(8,128)(2,1)}, u32[]{:S(2)}) copy-start(bf16[512,256]{1,0:T(8,128)(2,1)} %refs_0_.5) | copy-start | bytes 786436
  233.4 4.3 %copy-start.1 = (bf16[16,256]{1,0:T(8,128)(2,1)S(1)}, bf16[16,256]{1,0:T(8,128)(2,1)}, u32[]{:S(2)}) copy-start(bf16[16,256]{1,0:T(8,128)(2,1)} %refs_7_.1) | copy-start | bytes 24580

commit v11 on v9

--- a/solution.py
+++ b/solution.py
@@ -162,7 +162,8 @@
                     copies = []
                     for core in range(cores):
                         for b in range(stacks):
-                            at = pl.multiple_of((core * count + owner) * each + b * rank, sublanes)
+                            row = (((cores - 1) * count + owner) * cores + core) * each + b * rank
+                            at = pl.multiple_of(row, sublanes)
                             n = core * stacks + b
                             copies.append(
                                 pltpu.make_async_copy(
@@ -267,22 +268,23 @@
     used = norms[0].size // lanes
     part = rows // cores
     pieces = {"key": key[0]}
-    pieces["mixed"], pieces["side"] = merged([(*mixed, rows)], (key[1], *norms, part))
+    pieces["mixed"], side = merged([(*mixed, rows)], (key[1], *norms, part))
+    pieces["side"] = lax.all_gather(side, "width", axis=0, tiled=True)
     pieces["query"], pieces["value"] = merged([(*query, rows), (*value, rows)])
-    each = pieces["side"].shape[0]
+    each, both = side.shape[0], pieces["side"].shape[0]
     wide = {name: weight[0].shape[1] for name, weight in (("query", query), ("value", value))}
     regions = {
         "mixed": [
             ("mixed", h * columns, columns, columns, 0, 0, h * rows)
             for h in range(mixed[0].shape[0] // rows)
         ],
-        "side": [("side", 0, each, each, 0, 0, 0)],
+        "side": [("side", 0, both, both, 0, 0, 0)],
         "query": [("query", 0, wide["query"], 0, 0, rows, 0)],
         "value": [("value", 0, wide["value"], 0, 0, rows, 0)],
     }
     shapes = {name: (size, count * rows) for name, size in wide.items()}
     shapes["mixed"] = (count * columns, mixed[0].shape[0])
-    shapes["side"] = (count * each, lanes)
+    shapes["side"] = (count * both, lanes)
     plan = hops(count)
     outs = {}
     held = {name: {"a0": piece, "b0": piece} for name, piece in pieces.items()}
@@ -292,7 +294,11 @@
         for hop, source, pairs, offset in plan:
             if int(hop[1:]) == k:
                 for name in chunk_names:
-                    held[name][hop] = lax.ppermute(held[name][source], "shard", pairs)
+                    if name == "side":
+                        last = [(i * cores + cores - 1, j * cores + cores - 1) for i, j in pairs]
+                        held[name][hop] = lax.ppermute(held[name][source], ("shard", "width"), last)
+                    else:
+                        held[name][hop] = lax.ppermute(held[name][source], "shard", pairs)
                     if name in late:
                         arrived[name].append((regions[name], offset, held[name][hop]))
                 raw.append((offset, held["key"][hop]))
@@ -301,8 +307,8 @@
         arrived = {name: [] for name in late}
     sides = lax.all_gather(outs["side"], "width", axis=0, tiled=True)
     final_key = merged_pieces(raw, sides, key[2], count, cores, each)
-    sums = sides.reshape(cores, count, each, lanes)[:, :, each - tiles(used) :][:, :, :used]
-    serve_norm = sums.transpose(1, 0, 2, 3).reshape(-1)
+    sums = sides[(cores - 1) * count * both :].reshape(count * cores, each, lanes)
+    serve_norm = sums[:, each - tiles(used) :][:, :used].reshape(-1)
     return outs["query"], final_key, outs["value"], outs["mixed"], serve_norm
 
 

time: 258 us -> 223 us (0.86)
  waiting for transfers between devices: 179 us -> 144 us
  blocking collectives: 1.87 us -> 34.5 us
  starting transfers between devices: 61.4 us -> 29.7 us
    ppermute x25 -> x20, waiting for transfers between devices: 179 us -> 144 us  [by_line(): held[name][hop] = lax.ppermute(held[name][source], 'shard', pairs)]
    ppermute x25 -> x20, starting transfers between devices: 61.4 us -> 26.4 us  [by_line(): held[name][hop] = lax.ppermute(held[name][source], 'shard', pairs)]
    all_gather x1, blocking collectives: 1.87 us -> 32.6 us  [by_line(): sides = lax.all_gather(outs['side'], 'width', axis=0, tiled=True)]
    ppermute x0 -> x5, starting transfers between devices: none -> 3.3 us  [by_line(): held[name][hop] = lax.ppermute(held[name][source], ('shard', 'width'), last)]
  transfers between devices with their start and end apart: 25 -> 25, of which waited for: 7 -> 6; matrix products, arithmetic and copies ran while one was open for 0% -> 0% of each run, Pallas kernels for 3% -> 4%
where the time goes in v11:
time: 223 us
  waiting for transfers between devices  144 us (65%)
  blocking collectives  34.5 us (15%)
  starting transfers between devices  29.7 us (13%)
  Pallas kernels  12.7 us (6%)
    ppermute x20, waiting for transfers between devices, by_line(): held[name][hop] = lax.ppermute(held[name][source], 'shard', pairs)  144 us
    all_gather x1, blocking collectives, by_line(): sides = lax.all_gather(outs['side'], 'width', axis=0, tiled=True)  32.6 us
    ppermute x20, starting transfers between devices, by_line(): held[name][hop] = lax.ppermute(held[name][source], 'shard', pairs)  26.4 us
    pallas_call x5, Pallas kernels, place(): pl.pallas_call(functools.partial(place_body, count, moves, 0, len(arrays)...  6.53 us
  transfers between devices with their start and end apart: 25, of which 6 were waited for; matrix products, arithmetic and copies ran while one was open for 0% of the time, Pallas kernels for 4%

profile of v11, /device:TPU:0, one launch (start us, length us, event | category | flops | bytes accessed | tf_op | source)
XLA Modules:
  0.0 222.9 jit_solution(15691639805262443797)
XLA Ops:
  0.6 1.8 shard_map.174
  2.5 3.1 %collective-permute-start.5 = (bf16[1024,512]{1,0:T(8,128)(2,1)S(1)}, bf16[1024,512]{1,0:T(8,128)(2,1)S(1)}, u32[]{:S(2)}, u32[]{:S(2)}) collective-permute-start(bf16[1024,512]{1,0:T(8,128)(2,1)S(1)} %get-tuple-element.20.refs_0_), channel_id=1, source_target_pairs={{8,0},{0,8},{24,16},{16,24},{9,1},{1,9},{25,17},{17,25},{10,2},{2,... | collective-permute-start | bytes 3145736 | tf_op jit(solution)/shard_map/ppermute | solution.py:301
  5.6 2.4 %shard_map.173 = (bf16[1024,512]{1,0:T(8,128)(2,1)S(1)}, bf16[256,512]{1,0:T(8,128)(2,1)S(1)}) custom-call(bf16[512,1024]{1,0:T(8,128)(2,1)} %refs_0_.3, bf16[16,512]{1,0:T(8,128)(2,1)} %bitcast.11, bf16[16,1024]{1,0:T(8,128)(2,1)} %refs_2_.2, bf16[512,256]{1,0:T(8,128)(2,1)} %refs_3_.1, bf16[16,512]{1,0:T(8,128)(2,1)} %bitcast.12, bf16[16,256]{1,0:T(8,128)(2,1)} %refs_5_.1), custom_call_target="tpu_custom_call" | custom-call | tf_op jit(solution)/shard_map/pallas_call | solution.py:127
  8.8 0.7 collective-permute-start.11
  9.5 1.8 all_gather.6.refs_3_
  14.0 0.7 collective-permute-start.3
  14.8 14.8 %collective-permute-done.5.refs_1_ = bf16[1024,512]{1,0:T(8,128)(2,1)S(1)} collective-permute-done((bf16[1024,512]{1,0:T(8,128)(2,1)S(1)}, bf16[1024,512]{1,0:T(8,128)(2,1)S(1)}, u32[]{:S(2)}, u32[]{:S(2)}) %collective-permute-start.5) | collective-permute-done | bytes 1048608 | tf_op jit(solution)/shard_map/ppermute | solution.py:301
  29.6 0.7 collective-permute-start.6
  30.3 4.8 %collective-permute-start.15 = (bf16[256,512]{1,0:T(8,128)(2,1)S(1)}, bf16[256,512]{1,0:T(8,128)(2,1)S(1)}, u32[]{:S(2)}, u32[]{:S(2)}) collective-permute-start(bf16[256,512]{1,0:T(8,128)(2,1)S(1)} %get-tuple-element.22.refs_9_), channel_id=1, source_target_pairs={{8,0},{0,8},{24,16},{16,24},{9,1},{1,9},{25,17},{17,25},{10,2},{2,... | collective-permute-start | bytes 786440 | tf_op jit(solution)/shard_map/ppermute | solution.py:301
  35.2 16.3 %collective-permute-done.refs_7_ = bf16[1024,512]{1,0:T(8,128)(2,1)S(1)} collective-permute-done((bf16[1024,512]{1,0:T(8,128)(2,1)S(1)}, bf16[1024,512]{1,0:T(8,128)(2,1)S(1)}, u32[]{:S(2)}, u32[]{:S(2)}) %collective-permute-start) | collective-permute-done | bytes 1048608 | tf_op jit(solution)/shard_map/ppermute | solution.py:301
  51.4 0.7 collective-permute-start.1
  52.2 2.1 collective-permute-done.15.refs_10_
  54.2 2.5 %collective-permute-start.17 = (bf16[512,256]{1,0:T(8,128)(2,1)}, bf16[512,256]{1,0:T(8,128)(2,1)S(1)}, u32[]{:S(2)}, u32[]{:S(2)}) collective-permute-start(bf16[512,256]{1,0:T(8,128)(2,1)} %refs_0_.5), channel_id=1, source_target_pairs={{8,0},{0,8},{24,16},{16,24},{9,1},{1,9},{25,17},{17,25},{10,2},{2,... | collective-permute-start | bytes 786440 | tf_op jit(solution)/shard_map/ppermute | solution.py:301
  56.7 4.8 %collective-permute-done.17.refs_1_ = bf16[512,256]{1,0:T(8,128)(2,1)S(1)} collective-permute-done((bf16[512,256]{1,0:T(8,128)(2,1)}, bf16[512,256]{1,0:T(8,128)(2,1)S(1)}, u32[]{:S(2)}, u32[]{:S(2)}) %collective-permute-start.17) | collective-permute-done | bytes 262176 | tf_op jit(solution)/shard_map/ppermute | solution.py:301
  62.2 0.7 collective-permute-start.16
  62.9 1.3 collective-permute-start.12
  64.2 1.3 collective-permute-start.4
  65.5 1.3 collective-permute-start.22
  66.8 1.3 collective-permute-start.14
  68.1 1.3 collective-permute-start.2
  69.4 80.2 %collective-permute-done.14.refs_6_ = bf16[256,512]{1,0:T(8,128)(2,1)S(1)} collective-permute-done((bf16[256,512]{1,0:T(8,128)(2,1)S(1)}, bf16[256,512]{1,0:T(8,128)(2,1)S(1)}, u32[]{:S(2)}, u32[]{:S(2)}) %collective-permute-start.14) | collective-permute-done | bytes 262176 | tf_op jit(solution)/shard_map/ppermute | solution.py:301
  150.3 1.3 collective-permute-start.24
  151.6 26.1 %collective-permute-done.24.refs_0_ = bf16[256,512]{1,0:T(8,128)(2,1)S(1)} collective-permute-done((bf16[256,512]{1,0:T(8,128)(2,1)S(1)}, bf16[256,512]{1,0:T(8,128)(2,1)S(1)}, u32[]{:S(2)}, u32[]{:S(2)}) %collective-permute-start.24) | collective-permute-done | bytes 262176 | tf_op jit(solution)/shard_map/ppermute | solution.py:301
  177.7 1.3 collective-permute-start.19
  179.0 1.3 collective-permute-start.21
  181.0 2.3 %shard_map.175 = (bf16[2048,1024]{1,0:T(8,128)(2,1)}, bf16[320,128]{1,0:T(8,128)(2,1)S(1)}, bf16[1024,2048]{1,0:T(8,128)(2,1)}, bf16[256,2048]{1,0:T(8,128)(2,1)}) custom-call(bf16[1024,512]{1,0:T(8,128)(2,1)S(1)} %get-tuple-element.20.refs_0_, bf16[1024,512]{1,0:T(8,128)(2,1)S(1)} %collective-permute-done.5.refs_1_, ...), custom_call_target="tpu_custom_call" | custom-call | tf_op jit(solution)/shard_map/pallas_call | solution.py:230
  183.3 1.5 shard_map.176
  184.8 0.7 shard_map.180
  185.6 1.0 shard_map.178
  186.6 32.6 %all_gather.7.refs_6_ = bf16[640,128]{1,0:T(8,128)(2,1)S(1)} all-gather(bf16[320,128]{1,0:T(8,128)(2,1)S(1)} %get-tuple-element.30), channel_id=1, replica_groups=mesh['shard'=4,'width'=2,'shift'=4] {'width'}, dimensions={0}, use_global_device_ids=true | all-gather | bytes 245760 | tf_op jit(solution)/shard_map/all_gather | solution.py:308
  219.9 1.0 shard_map.177
  220.9 1.9 shard_map.179
  (34 shorter events, 6.1 us)
Async XLA Ops:
  2.5 27.1 %collective-permute-start.5 = (bf16[1024,512]{1,0:T(8,128)(2,1)S(1)}, bf16[1024,512]{1,0:T(8,128)(2,1)S(1)}, u32[]{:S(2)}, u32[]{:S(2)}) collective-permute-start(bf16[1024,512]{1,0:T(8,128)(2,1)S(1)} %get-tuple-element.20.refs_0_), channel_id=1, source_target_pairs={{8,0},{0,8},{24,16},{16,24},{9,1},{1,9},{25,17},{17,25},{10,2},{2,... | collective-permute-start | bytes 3145736 | tf_op jit(solution)/shard_map/ppermute | solution.py:301
  8.0 43.5 %collective-permute-start = (bf16[1024,512]{1,0:T(8,128)(2,1)S(1)}, bf16[1024,512]{1,0:T(8,128)(2,1)S(1)}, u32[]{:S(2)}, u32[]{:S(2)}) collective-permute-start(bf16[1024,512]{1,0:T(8,128)(2,1)S(1)} %get-tuple-element.19.refs_6_), channel_id=1, source_target_pairs={{8,0},{0,8},{24,16},{16,24},{9,1},{1,9},{25,17},{17,25},{10,2},{2,... | collective-permute-start | bytes 3145736 | tf_op jit(solution)/shard_map/ppermute | solution.py:301
  8.1 22.2 %collective-permute-start.13 = (bf16[256,512]{1,0:T(8,128)(2,1)S(1)}, bf16[256,512]{1,0:T(8,128)(2,1)S(1)}, u32[]{:S(2)}, u32[]{:S(2)}) collective-permute-start(bf16[256,512]{1,0:T(8,128)(2,1)S(1)} %get-tuple-element.22.refs_9_), channel_id=1, source_target_pairs={{16,8},{8,16},{17,9},{9,17},{18,10},{10,18},{19,11},{11,19},{20,12... | collective-permute-start | bytes 786440 | tf_op jit(solution)/shard_map/ppermute | solution.py:301
  8.8 54.1 %collective-permute-start.11 = (bf16[1024,512]{1,0:T(8,128)(2,1)S(1)}, bf16[1024,512]{1,0:T(8,128)(2,1)S(1)}, u32[]{:S(2)}, u32[]{:S(2)}) collective-permute-start(bf16[1024,512]{1,0:T(8,128)(2,1)S(1)} %get-tuple-element.19.refs_6_), channel_id=1, source_target_pairs={{16,8},{8,16},{17,9},{9,17},{18,10},{10,18},{19,11},{11,19},{20,12... | collective-permute-start | bytes 3145736 | tf_op jit(solution)/shard_map/ppermute | solution.py:301
  11.3 0.7 collective-permute-start.7
  12.0 0.7 collective-permute-start.9
  12.7 0.7 collective-permute-start.10
  13.3 0.7 collective-permute-start.8
  14.0 50.2 %collective-permute-start.3 = (bf16[1024,512]{1,0:T(8,128)(2,1)S(1)}, bf16[1024,512]{1,0:T(8,128)(2,1)S(1)}, u32[]{:S(2)}, u32[]{:S(2)}) collective-permute-start(bf16[1024,512]{1,0:T(8,128)(2,1)S(1)} %get-tuple-element.20.refs_0_), channel_id=1, source_target_pairs={{16,8},{8,16},{17,9},{9,17},{18,10},{10,18},{19,11},{11,19},{20,12... | collective-permute-start | bytes 3145736 | tf_op jit(solution)/shard_map/ppermute | solution.py:301
  29.6 35.9 %collective-permute-start.6 = (bf16[1024,512]{1,0:T(8,128)(2,1)S(1)}, bf16[1024,512]{1,0:T(8,128)(2,1)S(1)}, u32[]{:S(2)}, u32[]{:S(2)}) collective-permute-start(bf16[1024,512]{1,0:T(8,128)(2,1)S(1)} %collective-permute-done.5.refs_1_), channel_id=1, source_target_pairs={{16,8},{8,16},{17,9},{9,17},{18,10},{10,18},{19,11},{11,19},{20,12... | collective-permute-start | bytes 3145736 | tf_op jit(solution)/shard_map/ppermute | solution.py:301
  30.3 23.9 %collective-permute-start.15 = (bf16[256,512]{1,0:T(8,128)(2,1)S(1)}, bf16[256,512]{1,0:T(8,128)(2,1)S(1)}, u32[]{:S(2)}, u32[]{:S(2)}) collective-permute-start(bf16[256,512]{1,0:T(8,128)(2,1)S(1)} %get-tuple-element.22.refs_9_), channel_id=1, source_target_pairs={{8,0},{0,8},{24,16},{16,24},{9,1},{1,9},{25,17},{17,25},{10,2},{2,... | collective-permute-start | bytes 786440 | tf_op jit(solution)/shard_map/ppermute | solution.py:301
  51.4 16.7 %collective-permute-start.1 = (bf16[1024,512]{1,0:T(8,128)(2,1)S(1)}, bf16[1024,512]{1,0:T(8,128)(2,1)S(1)}, u32[]{:S(2)}, u32[]{:S(2)}) collective-permute-start(bf16[1024,512]{1,0:T(8,128)(2,1)S(1)} %collective-permute-done.refs_7_), channel_id=1, source_target_pairs={{16,8},{8,16},{17,9},{9,17},{18,10},{10,18},{19,11},{11,19},{20,12... | collective-permute-start | bytes 3145736 | tf_op jit(solution)/shard_map/ppermute | solution.py:301
  54.2 7.3 %collective-permute-start.17 = (bf16[512,256]{1,0:T(8,128)(2,1)}, bf16[512,256]{1,0:T(8,128)(2,1)S(1)}, u32[]{:S(2)}, u32[]{:S(2)}) collective-permute-start(bf16[512,256]{1,0:T(8,128)(2,1)} %refs_0_.5), channel_id=1, source_target_pairs={{8,0},{0,8},{24,16},{16,24},{9,1},{1,9},{25,17},{17,25},{10,2},{2,... | collective-permute-start | bytes 786440 | tf_op jit(solution)/shard_map/ppermute | solution.py:301
  61.5 0.7 collective-permute-start.18
  62.2 4.6 %collective-permute-start.16 = (bf16[256,512]{1,0:T(8,128)(2,1)S(1)}, bf16[256,512]{1,0:T(8,128)(2,1)S(1)}, u32[]{:S(2)}, u32[]{:S(2)}) collective-permute-start(bf16[256,512]{1,0:T(8,128)(2,1)S(1)} %collective-permute-done.15.refs_10_), channel_id=1, source_target_pairs={{16,8},{8,16},{17,9},{9,17},{18,10},{10,18},{19,11},{11,19},{20,12... | collective-permute-start | bytes 786440 | tf_op jit(solution)/shard_map/ppermute | solution.py:301
  62.9 116.1 %collective-permute-start.12 = (bf16[1024,512]{1,0:T(8,128)(2,1)S(1)}, bf16[1024,512]{1,0:T(8,128)(2,1)S(1)}, u32[]{:S(2)}, u32[]{:S(2)}) collective-permute-start(bf16[1024,512]{1,0:T(8,128)(2,1)S(1)} %collective-permute-done.11.refs_8_), channel_id=1, source_target_pairs={{8,0},{16,24},{9,1},{17,25},{10,2},{18,26},{11,3},{19,27},{12,4},{... | collective-permute-start | bytes 3145736 | tf_op jit(solution)/shard_map/ppermute | solution.py:301
  64.2 116.1 %collective-permute-start.4 = (bf16[1024,512]{1,0:T(8,128)(2,1)S(1)}, bf16[1024,512]{1,0:T(8,128)(2,1)S(1)}, u32[]{:S(2)}, u32[]{:S(2)}) collective-permute-start(bf16[1024,512]{1,0:T(8,128)(2,1)S(1)} %collective-permute-done.3.refs_2_), channel_id=1, source_target_pairs={{8,0},{16,24},{9,1},{17,25},{10,2},{18,26},{11,3},{19,27},{12,4},{... | collective-permute-start | bytes 3145736 | tf_op jit(solution)/shard_map/ppermute | solution.py:301
  65.5 120.1 %collective-permute-start.22 = (bf16[1024,512]{1,0:T(8,128)(2,1)S(1)}, bf16[1024,512]{1,0:T(8,128)(2,1)S(1)}, u32[]{:S(2)}, u32[]{:S(2)}) collective-permute-start(bf16[1024,512]{1,0:T(8,128)(2,1)S(1)} %collective-permute-done.6.refs_1_), channel_id=1, source_target_pairs={{8,0},{16,24},{9,1},{17,25},{10,2},{18,26},{11,3},{19,27},{12,4},{... | collective-permute-start | bytes 3145736 | tf_op jit(solution)/shard_map/ppermute | solution.py:301
  66.8 82.8 %collective-permute-start.14 = (bf16[256,512]{1,0:T(8,128)(2,1)S(1)}, bf16[256,512]{1,0:T(8,128)(2,1)S(1)}, u32[]{:S(2)}, u32[]{:S(2)}) collective-permute-start(bf16[256,512]{1,0:T(8,128)(2,1)S(1)} %collective-permute-done.13.refs_11_), channel_id=1, source_target_pairs={{8,0},{16,24},{9,1},{17,25},{10,2},{18,26},{11,3},{19,27},{12,4},{... | collective-permute-start | bytes 786440 | tf_op jit(solution)/shard_map/ppermute | solution.py:301
  68.1 151.7 %collective-permute-start.2 = (bf16[1024,512]{1,0:T(8,128)(2,1)S(1)}, bf16[1024,512]{1,0:T(8,128)(2,1)S(1)}, u32[]{:S(2)}, u32[]{:S(2)}) collective-permute-start(bf16[1024,512]{1,0:T(8,128)(2,1)S(1)} %collective-permute-done.1.refs_5_), channel_id=1, source_target_pairs={{8,0},{16,24},{9,1},{17,25},{10,2},{18,26},{11,3},{19,27},{12,4},{... | collective-permute-start | bytes 3145736 | tf_op jit(solution)/shard_map/ppermute | solution.py:301
  149.6 0.7 collective-permute-start.20
  150.3 27.4 %collective-permute-start.24 = (bf16[256,512]{1,0:T(8,128)(2,1)S(1)}, bf16[256,512]{1,0:T(8,128)(2,1)S(1)}, u32[]{:S(2)}, u32[]{:S(2)}) collective-permute-start(bf16[256,512]{1,0:T(8,128)(2,1)S(1)} %collective-permute-done.16.refs_7_), channel_id=1, source_target_pairs={{8,0},{16,24},{9,1},{17,25},{10,2},{18,26},{11,3},{19,27},{12,4},{... | collective-permute-start | bytes 786440 | tf_op jit(solution)/shard_map/ppermute | solution.py:301
  177.7 43.1 %collective-permute-start.19 = (bf16[512,256]{1,0:T(8,128)(2,1)S(1)}, bf16[512,256]{1,0:T(8,128)(2,1)S(1)}, u32[]{:S(2)}, u32[]{:S(2)}) collective-permute-start(bf16[512,256]{1,0:T(8,128)(2,1)S(1)} %collective-permute-done.18.refs_2_), channel_id=1, source_target_pairs={{8,0},{16,24},{9,1},{17,25},{10,2},{18,26},{11,3},{19,27},{12,4},{... | collective-permute-start | bytes 786440 | tf_op jit(solution)/shard_map/ppermute | solution.py:301
  179.0 41.8 %collective-permute-start.21 = (bf16[512,256]{1,0:T(8,128)(2,1)S(1)}, bf16[512,256]{1,0:T(8,128)(2,1)S(1)}, u32[]{:S(2)}, u32[]{:S(2)}) collective-permute-start(bf16[512,256]{1,0:T(8,128)(2,1)S(1)} %collective-permute-done.20.refs_4_), channel_id=1, source_target_pairs={{8,0},{16,24},{9,1},{17,25},{10,2},{18,26},{11,3},{19,27},{12,4},{... | collective-permute-start | bytes 786440 | tf_op jit(solution)/shard_map/ppermute | solution.py:301
  180.3 5.2 %collective-permute-start.23 = (bf16[80,128]{1,0:T(8,128)(2,1)S(1)}, bf16[80,128]{1,0:T(8,128)(2,1)S(1)}, u32[]{:S(2)}, u32[]{:S(2)}) collective-permute-start(bf16[80,128]{1,0:T(8,128)(2,1)S(1)} %collective-permute-done.10.refs_3_), channel_id=1, source_target_pairs={{12,4},{20,28},{13,5},{21,29},{14,6},{22,30},{15,7},{23,31}} | collective-permute-start | bytes 61448 | tf_op jit(solution)/shard_map/ppermute | solution.py:299
  219.8 1.1 copy-start
  219.9 1.1 copy-start.1
